TPU v7x, 512 devices: a 4x2x32 block of a 4x8x32 slice. The times are simulated.
512 devices in a mesh: groups: 2 (over y), seq: 32 (over z), tp: 8 (over x, core).
Axes of the slice: x: 4, y: 2, z: 32, core: 2. Of those that a mesh axis runs over, the one named last changes fastest.
The devices are a block of a 4x8x32 slice.
Arguments:
- q_prefill: bfloat16 [16384, 4096], P(('groups', 'seq'), 'tp'), parts along dimension 0, may hold values from -8 to 8
- k_prefill: bfloat16 [16384, 1024], P(('groups', 'seq'), 'tp'), parts along dimension 0, may hold values from -8 to 8
- v_prefill: bfloat16 [16384, 1024], P(('groups', 'seq'), 'tp'), parts along dimension 0, may hold values from -6 to 6
- pair_lengths: int32 [16], P('groups'), parts along dimension 0, may hold values from 1 to 5120, 8192 in all
- q_decode: bfloat16 [8, 4096], P('groups', 'tp'), parts along dimension 0, may hold values from -8 to 8
- cache_k: bfloat16 [8, 2048, 1024], P('groups', 'seq', 'tp'), parts along dimension 0, may hold values from -8 to 8
- cache_v: bfloat16 [8, 2048, 1024], P('groups', 'seq', 'tp'), parts along dimension 0, may hold values from -6 to 6
- cache_lengths: int32 [8], P('groups'), parts along dimension 0, may hold values from 256 to 2048
- stream: bfloat16 [24, 8192], P('groups', 'seq'), parts along dimension 0, may hold values from -40 to 40
- out_weight: bfloat16 [4096, 8192], P('tp', 'seq'), may hold values from -0.09375 to 0.09375
- norm_gain: bfloat16 [8192], P('seq'), may hold values from 0.099609375 to 1.8984375
- vocab_table: bfloat16 [64128, 8192], P('tp', 'seq'), may hold values from -0.0625 to 0.0625
- verdict_ids: int32 [24, 2], P('groups'), parts along dimension 0, may hold values from 0 to 64127
Outputs:
- attended: bfloat16 [16384, 4096], P(('groups', 'seq'), 'tp'), parts along dimension 0
- verdict_hidden: bfloat16 [24, 8192], P('groups', 'seq'), parts along dimension 0
- win: float32 [24], P('groups'), parts along dimension 0
There are 2 independent parts, one for each index of `groups`. A program takes and returns all parts, laid end to end along the dimension named above; an argument that names none is the same for every part. Nothing has to cross between parts.
Inputs may be any that keep to these rules, and one draw needn't show every extreme that they name: `pair_lengths`: the segments lie end to end from position 0 and each is at most 5120 long.
All inputs are finite; a program needn't handle non-finite values.
Results may differ from a plain program's by a relative error of at most 0.008.
Values may be sent and summed in bfloat16 or wider, within the bound.
No kernel may reach another device: no remote copies, remote signals or barrier semaphores. Data moves between devices by JAX's collectives and lax.ppermute only.
A program may use at most 64 MiB of HBM per device.

v0:
```python
import jax
import jax.numpy as jnp
from jax import lax
from jax.sharding import Mesh
from jax.sharding import PartitionSpec as P

D = 8192
H = 32
KVH = 8
HD = 128
PROMPTS = 4
TP = ("tp_0", "tp_1")
SEQ_TP = ("seq", "tp_0", "tp_1")


masked_score = -1e30
norm_eps = 1e-05


def sent_together(arrays, axis, dim, along):
    both = jnp.concatenate(arrays, axis=along)
    result, at, gathered = (lax.all_gather(both, axis, axis=dim, tiled=True), 0, [])
    for a in arrays:
        gathered.append(lax.slice_in_dim(result, at, at + a.shape[along], axis=along))
        at += a.shape[along]
    return tuple(gathered)


def total_of_pieces(shard, axis):
    pieces = lax.all_gather(shard, axis).astype(jnp.float32)
    return pieces.sum(axis=0)


def copy_for_each(shard, axis):
    length = lax.axis_size(axis)
    return lax.all_to_all(
        jnp.broadcast_to(shard[None], (length, *shard.shape)), axis, 0, 0, tiled=True
    )


def all_in_one(shard, axis):
    leaves = jax.tree.leaves(shard)
    order = sorted(range(len(leaves)), key=lambda k: -leaves[k].size)
    width = (1, *leaves[order[0]].shape)[-1]
    lines = [
        jnp.pad(leaves[k].reshape(-1), (0, -leaves[k].size % width)).reshape(-1, width)
        for k in order
    ]
    both, at, found = (copy_for_each(jnp.concatenate(lines), axis), 0, {})
    for k, line in zip(order, lines):
        section = both[:, at : at + len(line)].reshape(len(both), -1)
        found[k] = section[:, : leaves[k].size].reshape(-1, *leaves[k].shape)
        at += len(line)
    numbers = iter(range(len(leaves)))
    return jax.tree.map(lambda _: found[next(numbers)], shard)


def folded_in_pairs(pieces, combine):
    while len(jax.tree.leaves(pieces)[0]) > 1:
        pieces = jax.vmap(combine)(
            *(jax.tree.map(lambda part: part[side::2], pieces) for side in (0, 1))
        )
    return jax.tree.map(lambda part: part[0], pieces)


def joined_all(shard, axis, combine):
    pieces = all_in_one(shard, axis)
    return folded_in_pairs(pieces, combine)


def taken_together(shard, axis):
    everything = copy_for_each(shard, axis)
    return jnp.sum(everything, axis=0)


def over_axes(shard, axes):
    for axis in axes:
        shard = lax.psum(shard, axis)
    return shard


def segment_of(positions, pair_ends):
    return jnp.sum((pair_ends[None, :] <= positions[:, None]).astype(jnp.int32), axis=1)


def block_rows(row_count, tokens):
    for factor in (4, 3, 2):
        return tokens * factor
    return row_count


def merge_partials(first, second):
    max_first, total_first, sum_first = first
    max_second, total_second, sum_second = second
    new_max = jnp.maximum(max_first, max_second)
    scale_first = jnp.exp(max_first - new_max)
    scale_second = jnp.exp(max_second - new_max)
    new_total = total_first * scale_first + total_second * scale_second
    new_sum = sum_first * scale_first[..., None] + sum_second * scale_second[..., None]
    return (new_max, new_total, new_sum)


def shards(
    q_prefill,
    k_prefill,
    v_prefill,
    pair_lengths,
    q_decode,
    cache_k,
    cache_v,
    cache_lengths,
    stream,
    out_weight,
    norm_gain,
    vocab_table,
    verdict_ids,
):
    tokens = q_prefill.shape[0]
    seq_index = lax.axis_index("seq")
    kv_local = k_prefill.shape[1] // HD
    group_size = H // KVH
    score_scale = 1.0 / HD**0.5
    pair_ends = jnp.cumsum(pair_lengths)
    query_first = seq_index * tokens
    query_pos = query_first + jnp.arange(tokens, dtype=jnp.int32)
    query_seg = segment_of(query_pos, pair_ends)
    queries = q_prefill.reshape(tokens, kv_local, group_size, HD)

    def attend(state_now, key_block, value_block, first_row):
        key_count = key_block.shape[0]
        key_pos = first_row + jnp.arange(key_count, dtype=jnp.int32)
        key_seg = segment_of(key_pos, pair_ends)
        visible = (
            (query_seg[:, None] == key_seg[None, :])
            & (key_pos[None, :] <= query_pos[:, None])
            & (key_pos[None, :] >= 0)
        )

        def compute(state_in):
            row_max, row_total, weighted = state_in
            scores = (
                jnp.einsum(
                    "qkgd,nkd->kgqn",
                    queries,
                    key_block.reshape(key_count, kv_local, HD),
                    preferred_element_type=jnp.float32,
                )
                * score_scale
            )
            scores = jnp.where(visible, scores, masked_score)
            new_max = jnp.maximum(row_max, jnp.max(scores, axis=-1))
            exp_terms = jnp.where(visible, jnp.exp(scores - new_max[..., None]), 0.0)
            rescale = jnp.exp(row_max - new_max)
            new_total = row_total * rescale + jnp.sum(exp_terms, axis=-1)
            new_weighted = weighted * rescale[..., None] + jnp.einsum(
                "kgqn,nkd->kgqd",
                exp_terms.astype(jnp.bfloat16),
                value_block.reshape(key_count, kv_local, HD),
                preferred_element_type=jnp.float32,
            )
            return (new_max, new_total, new_weighted)

        return lax.cond(jnp.any(visible), compute, lambda state_in: state_in, state_now)

    initial = (
        jnp.full((kv_local, group_size, tokens), masked_score, jnp.float32),
        jnp.zeros((kv_local, group_size, tokens), jnp.float32),
        jnp.zeros((kv_local, group_size, tokens, HD), jnp.float32),
    )
    pieces = sent_together((k_prefill, v_prefill), "seq", 0, 1)
    key_rows = pieces[0]
    value_rows = pieces[1]
    row_count = key_rows.shape[0]
    block_len = block_rows(row_count, tokens)
    block_count = row_count // block_len
    stacked = (
        key_rows.reshape(block_count, block_len, key_rows.shape[1]),
        value_rows.reshape(block_count, block_len, value_rows.shape[1]),
        block_len * jnp.arange(block_count, dtype=jnp.int32),
    )

    def scan_step(state_in, pieces):
        return (attend(state_in, pieces[0], pieces[1], pieces[2]), None)

    state_out, unused = lax.scan(scan_step, initial, stacked)
    state_now = state_out
    final_max, final_total, final_weighted = state_now
    attended_f = final_weighted / final_total[..., None]
    attended = (
        jnp.transpose(attended_f, (2, 0, 1, 3))
        .reshape(tokens, kv_local * group_size * HD)
        .astype(jnp.bfloat16)
    )
    local_ends = pair_ends - 1 - query_first
    selector = (local_ends[:, None] == jnp.arange(tokens, dtype=jnp.int32)[None, :]).astype(
        jnp.bfloat16
    )
    picked = jnp.dot(selector, attended, preferred_element_type=jnp.float32)
    pair_rows = (
        total_of_pieces(picked.astype(jnp.bfloat16), "seq").astype(jnp.float32).astype(jnp.bfloat16)
    )
    cache_count = cache_k.shape[1]
    cache_pos = seq_index * cache_count + jnp.arange(cache_count, dtype=jnp.int32)
    valid = (cache_pos[None, :] < cache_lengths[:, None])[:, None, None, :]
    dec_queries = q_decode.reshape(PROMPTS, kv_local, group_size, HD)
    dec_scores = (
        jnp.einsum(
            "pkgd,pckd->pkgc",
            dec_queries,
            cache_k.reshape(PROMPTS, cache_count, kv_local, HD),
            preferred_element_type=jnp.float32,
        )
        * score_scale
    )
    dec_scores = jnp.where(valid, dec_scores, masked_score)
    dec_max = jnp.max(dec_scores, axis=-1)
    dec_exp = jnp.where(valid, jnp.exp(dec_scores - dec_max[..., None]), 0.0)
    dec_total = jnp.sum(dec_exp, axis=-1)
    dec_sum = jnp.einsum(
        "pkgc,pckd->pkgd",
        dec_exp.astype(jnp.bfloat16),
        cache_v.reshape(PROMPTS, cache_count, kv_local, HD),
        preferred_element_type=jnp.float32,
    )
    dec_max, dec_total, dec_sum = joined_all((dec_max, dec_total, dec_sum), "seq", merge_partials)
    decode_out = (
        (dec_sum / dec_total[..., None])
        .reshape(PROMPTS, kv_local * group_size * HD)
        .astype(jnp.bfloat16)
    )
    verdict_in = jnp.concatenate([pair_rows, decode_out], axis=0)
    partial_value = jnp.dot(verdict_in, out_weight, preferred_element_type=jnp.float32)
    residual = stream.astype(jnp.float32) + taken_together(partial_value, TP)
    squares = jnp.sum(residual * residual, axis=1)
    gained = residual * norm_gain.astype(jnp.float32)[None, :]
    vocab_rows = vocab_table.shape[0]
    local_ids = verdict_ids - lax.axis_index(TP) * vocab_rows
    inside = ((local_ids >= 0) & (local_ids < vocab_rows)).astype(jnp.float32)
    table_rows = vocab_table[jnp.clip(local_ids, 0, vocab_rows - 1)].astype(jnp.float32)
    raw_logits = jnp.sum(gained[:, None, :] * table_rows, axis=2) * inside
    own_squares = squares * (lax.axis_index(TP) == 0).astype(jnp.float32)
    total_squares, raw_total = (over_axes(own_squares, SEQ_TP), over_axes(raw_logits, SEQ_TP))
    inv_rms = 1.0 / jnp.sqrt(total_squares / D + norm_eps)
    verdict_logits = raw_total * inv_rms[:, None]
    verdict_hidden = (gained * inv_rms[:, None]).astype(jnp.bfloat16)
    win = 1.0 / (1.0 + jnp.exp(verdict_logits[:, 1] - verdict_logits[:, 0]))
    return (attended, verdict_hidden, win)


def solution(mesh):
    torus = Mesh(
        mesh.devices.reshape(mesh.shape["groups"], mesh.shape["seq"], 4, 2),
        ("groups", "seq", "tp_0", "tp_1"),
    )
    return jax.shard_map(
        shards,
        mesh=torus,
        in_specs=(
            P(("groups", "seq"), TP),
            P(("groups", "seq"), TP),
            P(("groups", "seq"), TP),
            P("groups"),
            P("groups", TP),
            P("groups", "seq", TP),
            P("groups", "seq", TP),
            P("groups"),
            P("groups", "seq"),
            P(TP, "seq"),
            P("seq"),
            P(TP, "seq"),
            P("groups", None),
        ),
        out_specs=(P(("groups", "seq"), TP), P("groups", "seq"), P("groups")),
        check_vma=False,
    )
```

profile of v0, /device:TPU:40, one launch (start us, length us, event | category | flops | bytes accessed | tf_op | source)
XLA Modules:
  0.0 406.4 jit_solution(13978736276279904751)
XLA Ops:
  7.3 1.5 pad_maximum_fusion
  9.6 0.7 broadcast_compare_fusion.1
  10.3 1.0 fusion.64
  11.7 1.0 fusion.47
  12.8 0.8 broadcast_in_dim.63
  13.6 45.8 %all-to-all-start = ((f32[32,18,128]{2,1,0:T(8,128)}), f32[32,18,128]{2,1,0:T(8,128)S(1)}, u32[]{:S(2)}, u32[]{:S(2)}) async-start(f32[32,18,128]{2,1,0:T(8,128)} %broadcast_in_dim.63), calls=%async_computation | async-start | bytes 786432 | tf_op jit(solution)/shard_map/all_to_all | solution.py:36
  59.3 0.8 reduce-window.7
  60.2 1.1 copy.107
  62.1 0.8 copy.123
  63.1 53.9 %all-to-all-done = f32[32,18,128]{2,1,0:T(8,128)S(1)} async-done(((f32[32,18,128]{2,1,0:T(8,128)}), f32[32,18,128]{2,1,0:T(8,128)S(1)}, u32[]{:S(2)}, u32[]{:S(2)}) %all-to-all-start) | async-done | bytes 294944 | tf_op jit(solution)/shard_map/all_to_all | solution.py:36
  125.4 75.6 %all-gather.3.cloned.1.call-done = bf16[8192,256]{1,0:T(8,128)(2,1)} async-done(((bf16[256,256]{1,0:T(8,128)(2,1)}), bf16[8192,256]{1,0:T(8,128)(2,1)}) %all-gather.3.cloned.1.call-update) | async-done | bytes 4194320 | tf_op jit(solution)/shard_map/all_gather | solution.py:22
  201.0 3.8 fusion.62
  204.8 39.9 %while.15 = (s32[]{:T(128)}, f32[1,4,256]{2,1,0:T(4,128)S(1)}, f32[1,4,256]{2,1,0:T(4,128)S(1)}, f32[1,4,256,128]{3,2,1,0:T(8,128)S(1)}, s32[256]{0:T(256)S(1)},...) while((s32[]{:T(128)}, f32[1,4,256]{2,1,0:T(4,128)S(1)}, ...), condition=%wide.region_9.10_spmd.clone, body=%wide.region_2.9_spmd.clone.sunk | while | flops 552105216 | bytes 15558455 | solution.py:185
  207.0 1.5 fusion.71
  209.3 4.3 %conditional.3 = ((f32[1,4,256]{2,1,0:T(4,128)S(1)}, f32[1,4,256]{2,1,0:T(4,128)S(1)}, f32[1,4,256,128]{3,2,1,0:T(8,128)S(1)})) conditional(s32[]{:T(128)} %convert_element_type.96, (f32[1,4,256]{2,1,0:T(4,128)S(1)}, f32[1,4,256]{2,1,0:T(4,128)S(1)}, f32[1,4,256,128]{3,2,1,0:T(8,128)S(1)}) %tuple.68, (pred[256,1024]{0,1:T(8,128)(4,1)S(1)}, ...), branch_computations={%region_5.5_spmd, %region_6.8_spmd} | conditional | flops 550767616 | bytes 15270436 | solution.py:163
  209.3 0.8 fusion.2
  210.1 1.0 fusion.4
  211.2 2.4 fusion.12
  215.8 1.5 fusion.71
  220.2 1.5 fusion.71
  224.7 1.5 fusion.71
  229.1 1.5 fusion.71
  233.6 1.5 fusion.71
  238.0 1.5 fusion.71
  242.4 1.5 fusion.71
  245.4 73.7 %all-gather = bf16[256,512]{1,0:T(8,128)(2,1)S(1)} all-gather(bf16[8,512]{1,0:T(8,128)(2,1)S(1)} %convolution_convert_fusion), channel_id=2, replica_groups=mesh['groups'=2,'seq'=32,'tp_0'=4,'tp_1'=2] {'seq'}, dimensions={0}, use_global_device_ids=true | all-gather | bytes 270336 | tf_op jit(solution)/shard_map/all_gather | solution.py:30
  320.0 4.7 %all-to-all-start.1 = ((f32[8,12,256]{2,1,0:T(8,128)}), f32[8,12,256]{2,1,0:T(8,128)S(1)}, u32[]{:S(2)}, u32[]{:S(2)}) async-start(f32[8,12,256]{2,1,0:T(8,128)} %broadcast_in_dim.64), calls=%async_computation.1 | async-start | bytes 262144 | tf_op jit(solution)/shard_map/all_to_all | solution.py:36
  324.7 3.3 gather_fusion
  328.0 2.8 all-to-all-done.1
  331.1 55.2 %all-reduce.2 = (f32[12]{0:T(128)S(1)}, f32[12,2]{1,0:T(8,128)S(1)}) all-reduce(f32[12]{0:T(128)S(1)} %broadcast_multiply_fusion.1, f32[12,2]{1,0:T(8,128)S(1)} %and_select_fusion), channel_id=1, replica_groups=mesh['groups'=2,'seq'=32,'tp_0'=4,'tp_1'=2] {'seq'}, use_global_device_ids=true, to_apply=%region_15.16 | all-reduce | flops 36 | bytes 288 | tf_op jit(solution)/shard_map/psum | solution.py:78
  386.3 9.2 %all-reduce.3 = (f32[12]{0:T(128)S(1)}, f32[12,2]{1,0:T(8,128)S(1)}) all-reduce(f32[12]{0:T(128)S(1)} %get-tuple-element.258, f32[12,2]{1,0:T(8,128)S(1)} %get-tuple-element.259), channel_id=1, replica_groups=mesh['groups'=2,'seq'=32,'tp_0'=4,'tp_1'=2] {'tp_0'}, use_global_device_ids=true, to_apply=%region_16.17 | all-reduce | flops 36 | bytes 288 | tf_op jit(solution)/shard_map/psum | solution.py:78
  395.5 2.6 all-reduce.4
  (138 shorter events, 31.0 us)
Async XLA Ops:
  7.2 312.0 %copy-start = (bf16[512,256]{1,0:T(8,128)(2,1)S(1)}, bf16[512,256]{1,0:T(8,128)(2,1)}, u32[]{:S(2)}) copy-start(bf16[512,256]{1,0:T(8,128)(2,1)} %param.26) | copy-start | bytes 786436
  7.2 193.8 %all-gather.3.cloned.1.call-start = ((), (), s32[]{:S(2)}) async-start(), calls=%async_computation.2 | async-start | bytes 4325376 | tf_op jit(solution)/shard_map/all_gather | solution.py:22
  13.6 103.4 %all-to-all-start = ((f32[32,18,128]{2,1,0:T(8,128)}), f32[32,18,128]{2,1,0:T(8,128)S(1)}, u32[]{:S(2)}, u32[]{:S(2)}) async-start(f32[32,18,128]{2,1,0:T(8,128)} %broadcast_in_dim.63), calls=%async_computation | async-start | bytes 786432 | tf_op jit(solution)/shard_map/all_to_all | solution.py:36
  204.8 126.0 %copy-start.2 = (bf16[12,256]{1,0:T(8,128)(2,1)S(1)}, bf16[12,256]{1,0:T(8,128)(2,1)}, u32[]{:S(2)}) copy-start(bf16[12,256]{1,0:T(8,128)(2,1)} %param.25) | copy-start | bytes 18436
  245.2 154.3 %copy-start.1 = (bf16[32,8,4,128]{3,1,2,0:T(8,128)(2,1)}, bf16[32,8,4,128]{3,1,2,0:T(8,128)(2,1)S(1)}, u32[]{:S(2)}) copy-start(bf16[32,8,4,128]{3,1,2,0:T(8,128)(2,1)S(1)} %copy.138) | copy-start | bytes 786436
  320.0 10.8 %all-to-all-start.1 = ((f32[8,12,256]{2,1,0:T(8,128)}), f32[8,12,256]{2,1,0:T(8,128)S(1)}, u32[]{:S(2)}, u32[]{:S(2)}) async-start(f32[8,12,256]{2,1,0:T(8,128)} %broadcast_in_dim.64), calls=%async_computation.1 | async-start | bytes 262144 | tf_op jit(solution)/shard_map/all_to_all | solution.py:36
Sparse Core Ops, SparseCore 0:
  10.7 190.2 all-gather.2
where the time goes:
time: 407 us; the launch traced here: 406 us
  blocking collectives  141 us (35%)
  waiting for transfers between devices  132 us (32%)
  starting transfers between devices  50.5 us (12%)
  other arithmetic  32.1 us (8%)
  local copies, waits for them, and re-layouts  24.6 us (6%)
  between operations  14.4 us (4%)
  loops' own time  6.09 us (1%)
  matrix products  5.65 us (1%)
    all_gather x1, waiting for transfers between devices, sent_together(): lax.all_gather(both, axis, axis=dim, tiled=True)  75.6 us
    all_gather x1, blocking collectives, total_of_pieces(): pieces = lax.all_gather(shard, axis).astype(jnp.float32)  73.7 us
    psum x3, blocking collectives, over_axes(): shard = lax.psum(shard, axis)  67 us
    all_to_all x2, waiting for transfers between devices, copy_for_each(): lax.all_to_all(jnp.broadcast_to(shard[None], (length, *shard.shape)), axi...  56.7 us
    all_to_all x2, starting transfers between devices, copy_for_each(): lax.all_to_all(jnp.broadcast_to(shard[None], (length, *shard.shape)), axi...  50.5 us
    reduce_or x8, other arithmetic, attend(): jnp.any(visible)  12.4 us
  transfers between devices with their start and end apart: 3, of which 3 were waited for; matrix products, arithmetic and copies ran while one was open for 5% of the time, Pallas kernels for 0%

commit v1 on v0

v1 whole, which is shorter than its diff:
```python
import functools

import jax
import jax.numpy as jnp
from jax import lax
from jax.experimental import pallas as pl
from jax.experimental.pallas import tpu as pltpu
from jax.sharding import Mesh
from jax.sharding import PartitionSpec as P

D = 8192
H = 32
KVH = 8
HD = 128
PROMPTS = 4
PAIRS = 8
ROWS = 12
GROUP = H // KVH
LO = 8
SLOT = 16
KEY_BLOCK = 512
TP = ("tp_0", "tp_1")
SEQ = ("seq_hi", "seq_lo")

masked_score = -1e30
norm_eps = 1e-05
score_scale = 1.0 / HD**0.5
exp2_scale = score_scale * 1.4426950408889634

NT = (((1,), (1,)), ((), ()))
VM = pl.BlockSpec(memory_space=pltpu.VMEM)
SM = pl.BlockSpec(memory_space=pltpu.SMEM)


def exchanged(copies, axis):
    return lax.all_to_all(copies, axis, 0, 0, tiled=True)


def ends_of(lengths_ref):
    ends, total = [], 0
    for p in range(PAIRS):
        total = total + lengths_ref[p]
        ends.append(total)
    return ends


def last_rows_kernel(lengths_ref, seq_ref, q_ref, out_ref):
    tokens = q_ref.shape[0]
    ends = ends_of(lengths_ref)
    row = lax.broadcasted_iota(jnp.int32, (SLOT, tokens), 0)
    col = lax.broadcasted_iota(jnp.int32, (SLOT, tokens), 1) + seq_ref[0] * tokens
    last = jnp.full((SLOT, tokens), -1, jnp.int32)
    for p in range(PAIRS):
        last = jnp.where(row == p, ends[p] - 1, last)
    selector = jnp.where(col == last, 1.0, 0.0).astype(jnp.bfloat16)
    picked = jnp.dot(selector, q_ref[...], preferred_element_type=jnp.float32)
    for c in range(out_ref.shape[0]):
        out_ref[c] = picked[:PAIRS].astype(out_ref.dtype)


def partials_kernel(
    lengths_ref, cache_lengths_ref, seq_ref, rows_ref, qd_ref, k_ref, v_ref, ck_ref, cv_ref,
    out_ref, q_scratch,
):
    tokens = k_ref.shape[0]
    cache_count = ck_ref.shape[1]
    ends = ends_of(lengths_ref)
    q_scratch[...] = jnp.zeros_like(q_scratch)
    for g in range(GROUP):
        q_scratch[g * SLOT : g * SLOT + PAIRS, :] = rows_ref[:, g * HD : (g + 1) * HD]
        q_scratch[g * SLOT + PAIRS : g * SLOT + ROWS, :] = qd_ref[
            :, g * HD : (g + 1) * HD
        ].astype(jnp.float32)
    queries = q_scratch[...].astype(jnp.bfloat16)
    keys = jnp.concatenate([k_ref[...], ck_ref[...].reshape(PROMPTS * cache_count, HD)], axis=0)
    values = jnp.concatenate([v_ref[...], cv_ref[...].reshape(PROMPTS * cache_count, HD)], axis=0)
    count = tokens + PROMPTS * cache_count
    scores = lax.dot_general(queries, keys, NT, preferred_element_type=jnp.float32) * score_scale
    lane = lax.broadcasted_iota(jnp.int32, (1, count), 1)
    key_pos = lane + seq_ref[0] * tokens
    key_seg = jnp.zeros((1, count), jnp.int32)
    for p in range(PAIRS):
        key_seg = key_seg + jnp.where(key_pos >= ends[p], 1, 0)
    owner = key_seg
    for p in range(PROMPTS):
        first = tokens + p * cache_count
        mine = (lane >= first) & (lane < first + cache_count)
        cache_pos = lane - first + seq_ref[0] * cache_count
        label = jnp.where(cache_pos < cache_lengths_ref[p], PAIRS + p, -1)
        owner = jnp.where(mine, label, owner)
    item = lax.broadcasted_iota(jnp.int32, (GROUP * SLOT, count), 0) % SLOT
    visible = item == owner
    scores = jnp.where(visible, scores, masked_score)
    top = jnp.max(scores, axis=1, keepdims=True)
    terms = jnp.where(visible, jnp.exp(scores - top), 0.0)
    total = jnp.sum(terms, axis=1, keepdims=True)
    sums = jnp.dot(terms.astype(jnp.bfloat16), values, preferred_element_type=jnp.float32)
    put_partials(out_ref, sums, top, total)


def put_partials(out_ref, sums, top, total):
    across = (GROUP * SLOT, HD)
    top_lanes = jnp.transpose(jnp.broadcast_to(top, across))[:1]
    total_lanes = jnp.transpose(jnp.broadcast_to(total, across))[:1]
    for c in range(out_ref.shape[0]):
        out_ref[c] = sums
        out_ref[c, ROWS : ROWS + 1, : GROUP * SLOT] = top_lanes
        out_ref[c, ROWS + 1 : ROWS + 2, : GROUP * SLOT] = total_lanes


def merged(pieces_ref):
    count = pieces_ref.shape[0]
    tops, totals = [], []
    for c in range(count):
        both = pieces_ref[c, ROWS - 4 : ROWS + 4, :]
        columns = jnp.transpose(both)[: GROUP * SLOT]
        tops.append(columns[:, 4:5])
        totals.append(columns[:, 5:6])
    top = functools.reduce(jnp.maximum, tops)
    total = jnp.zeros_like(top)
    sums = jnp.zeros((GROUP * SLOT, HD), jnp.float32)
    for c in range(count):
        scale = jnp.exp(tops[c] - top)
        total = total + totals[c] * scale
        sums = sums + pieces_ref[c] * scale
    return sums, top, total


def merge_kernel(pieces_ref, out_ref):
    put_partials(out_ref, *merged(pieces_ref))


def project_kernel(pieces_ref, w_ref, table_ref, out_ref):
    sums, _, total = merged(pieces_ref)
    rows = sums / total
    partial = jnp.zeros((SLOT, w_ref.shape[1]), jnp.float32)
    for g in range(GROUP):
        partial = partial + jnp.dot(
            rows[g * SLOT : (g + 1) * SLOT].astype(jnp.bfloat16),
            w_ref[g * HD : (g + 1) * HD, :],
            preferred_element_type=jnp.float32,
        )
    keep = lax.broadcasted_iota(jnp.int32, partial.shape, 0) < ROWS
    partial = jnp.where(keep, partial, 0.0)
    for c in range(out_ref.shape[0]):
        out_ref[c, :SLOT] = partial
        out_ref[c, SLOT:] = table_ref[...]


def residual_kernel(pieces_ref, stream_ref, gain_ref, gained_ref, sums_ref):
    total = pieces_ref[0]
    for c in range(1, pieces_ref.shape[0]):
        total = total + pieces_ref[c]
    residual = total[:ROWS] + stream_ref[...].astype(jnp.float32)
    gained = residual * gain_ref[...].astype(jnp.float32)
    gained_ref[...] = gained
    squares = jnp.sum(residual * residual, axis=1, keepdims=True)
    first = jnp.sum(gained * total[SLOT : SLOT + ROWS], axis=1, keepdims=True)
    second = jnp.sum(gained * total[2 * SLOT : 2 * SLOT + ROWS], axis=1, keepdims=True)
    lane = lax.broadcasted_iota(jnp.int32, (ROWS, HD), 1)
    packed = jnp.where(lane == 0, squares, jnp.where(lane == 1, first, second))
    for c in range(sums_ref.shape[0]):
        sums_ref[c] = packed


def verdict_kernel(sums_ref, gained_ref, hidden_ref, win_ref):
    inv_rms = 1.0 / jnp.sqrt(sums_ref[:, 0:1] / D + norm_eps)
    hidden_ref[...] = (gained_ref[...] * inv_rms).astype(hidden_ref.dtype)
    logits = sums_ref[...] * inv_rms
    win = 1.0 / (1.0 + jnp.exp(logits[:, 2:3] - logits[:, 1:2]))
    win_ref[...] = jnp.broadcast_to(win, win_ref.shape)


def attention_kernel(
    lengths_ref, seq_ref, q_ref, kv_ref, out_ref, kv_buf, top_ref, total_ref, sum_ref, sems
):
    tokens = q_ref.shape[0]
    first = seq_ref[0] * tokens
    ends = ends_of(lengths_ref)
    start_first = jnp.int32(0)
    start_last = jnp.int32(0)
    for p in range(PAIRS):
        start_first = jnp.where(ends[p] <= first, ends[p], start_first)
        start_last = jnp.where(ends[p] <= first + tokens - 1, ends[p], start_last)
    low = start_first // KEY_BLOCK
    high = (first + tokens + KEY_BLOCK - 1) // KEY_BLOCK

    def fetch(b):
        rows = pl.ds(pl.multiple_of(b * KEY_BLOCK, KEY_BLOCK), KEY_BLOCK)
        return pltpu.make_async_copy(kv_ref.at[rows], kv_buf.at[rows], sems.at[b])

    def begin(b, carry):
        fetch(b).start()
        return carry

    lax.fori_loop(low, high, begin, 0)
    top_ref[...] = jnp.full_like(top_ref, masked_score)
    total_ref[...] = jnp.zeros_like(total_ref)
    sum_ref[...] = jnp.zeros_like(sum_ref)
    query_pos = lax.broadcasted_iota(jnp.int32, (tokens, 1), 0) + first
    query_start = jnp.zeros((tokens, 1), jnp.int32)
    for p in range(PAIRS):
        query_start = jnp.where(query_pos >= ends[p], ends[p], query_start)

    def attend(b, masked):
        key_first = b * KEY_BLOCK
        rows = pl.ds(pl.multiple_of(key_first, KEY_BLOCK), KEY_BLOCK)
        keys = kv_buf[rows, :HD]
        values = kv_buf[rows, HD:]
        if masked:
            key_pos = lax.broadcasted_iota(jnp.int32, (tokens, KEY_BLOCK), 1) + key_first
            visible = (key_pos >= query_start) & (key_pos <= query_pos)
        for g in range(GROUP):
            columns = slice(g * HD, (g + 1) * HD)
            scores = lax.dot_general(
                q_ref[:, columns], keys, NT, preferred_element_type=jnp.float32
            )
            if masked:
                scores = jnp.where(visible, scores, masked_score)
            old_top = top_ref[g]
            new_top = jnp.maximum(old_top, jnp.max(scores, axis=1, keepdims=True))
            rescale = jnp.exp2((old_top - new_top) * exp2_scale)
            terms = jnp.exp2((scores - new_top) * exp2_scale)
            lanes = terms[:, :HD]
            for j in range(1, KEY_BLOCK // HD):
                lanes = lanes + terms[:, j * HD : (j + 1) * HD]
            total_ref[g] = total_ref[g] * rescale + lanes
            sum_ref[g] = sum_ref[g] * rescale + jnp.dot(
                terms.astype(jnp.bfloat16), values, preferred_element_type=jnp.float32
            )
            top_ref[g] = new_top

    def step(b, carry):
        fetch(b).wait()
        key_first = b * KEY_BLOCK
        masked = (key_first < start_last) | (key_first + KEY_BLOCK > first + 1)

        @pl.when(masked)
        def _():
            attend(b, True)

        @pl.when(jnp.logical_not(masked))
        def _():
            attend(b, False)

        return carry

    lax.fori_loop(low, high, step, 0)
    for g in range(GROUP):
        total = jnp.sum(total_ref[g], axis=1, keepdims=True)
        out_ref[:, g * HD : (g + 1) * HD] = (sum_ref[g] / total).astype(out_ref.dtype)


def attention(lengths, seq_index, q, kv):
    tokens = q.shape[0]
    return pl.pallas_call(
        attention_kernel,
        out_shape=jax.ShapeDtypeStruct(q.shape, q.dtype),
        in_specs=[SM, SM, VM, pl.BlockSpec(memory_space=pl.ANY)],
        out_specs=VM,
        scratch_shapes=[
            pltpu.VMEM(kv.shape, kv.dtype),
            pltpu.VMEM((GROUP, tokens, 1), jnp.float32),
            pltpu.VMEM((GROUP, tokens, HD), jnp.float32),
            pltpu.VMEM((GROUP, tokens, HD), jnp.float32),
            pltpu.SemaphoreType.DMA((kv.shape[0] // KEY_BLOCK,)),
        ],
        compiler_params=pltpu.CompilerParams(vmem_limit_bytes=40 * 1024 * 1024),
        name="attention",
    )(lengths, seq_index, q, kv)


def call(kernel, shapes, specs, name, scratch=()):
    many = isinstance(shapes, tuple)
    return pl.pallas_call(
        kernel,
        out_shape=shapes,
        in_specs=specs,
        out_specs=tuple(VM for _ in shapes) if many else VM,
        scratch_shapes=list(scratch),
        name=name,
    )


def shards(
    q_prefill,
    k_prefill,
    v_prefill,
    pair_lengths,
    q_decode,
    cache_k,
    cache_v,
    cache_lengths,
    stream,
    out_weight,
    norm_gain,
    vocab_table,
    verdict_ids,
):
    f32 = jnp.float32
    lo = lax.axis_size("seq_lo")
    hi = lax.axis_size("seq_hi")
    tp = lax.axis_size(TP)
    columns = q_prefill.shape[1]
    width = stream.shape[1]
    seq_index = lax.axis_index(SEQ).astype(jnp.int32).reshape(1)
    shape = jax.ShapeDtypeStruct

    kv = lax.all_gather(jnp.concatenate([k_prefill, v_prefill], axis=1), SEQ, axis=0, tiled=True)

    picked = call(
        last_rows_kernel, shape((lo, PAIRS, columns), jnp.bfloat16), [SM, SM, VM], "last_rows"
    )(pair_lengths, seq_index, q_prefill)
    rows = jnp.sum(exchanged(picked, "seq_lo").astype(f32), axis=0)
    rows = lax.psum(rows, "seq_hi")

    partials = call(
        partials_kernel,
        shape((lo, GROUP * SLOT, HD), f32),
        [SM, SM, SM] + [VM] * 6,
        "partials",
        [pltpu.VMEM((GROUP * SLOT, HD), f32)],
    )(
        pair_lengths, cache_lengths, seq_index, rows, q_decode, k_prefill, v_prefill, cache_k,
        cache_v,
    )
    partials = exchanged(partials, "seq_lo")
    partials = call(merge_kernel, shape((hi, GROUP * SLOT, HD), f32), [VM], "merge")(partials)
    partials = exchanged(partials, "seq_hi")

    vocab_rows = vocab_table.shape[0]
    ids = jnp.pad(verdict_ids.T, ((0, 0), (0, SLOT - ROWS))).reshape(-1)
    local_ids = ids - lax.axis_index(TP) * vocab_rows
    inside = ((local_ids >= 0) & (local_ids < vocab_rows))[:, None]
    table_rows = vocab_table[jnp.clip(local_ids, 0, vocab_rows - 1)]
    table_rows = jnp.where(inside, table_rows.astype(f32), 0.0)

    pieces = call(
        project_kernel, shape((tp, 3 * SLOT, width), f32), [VM, VM, VM], "project"
    )(partials, out_weight, table_rows)
    pieces = exchanged(pieces, TP)
    gained, sums = call(
        residual_kernel,
        (shape((ROWS, width), f32), shape((lo, ROWS, HD), f32)),
        [VM, VM, VM],
        "residual",
    )(pieces, stream, norm_gain.reshape(1, width))
    sums = jnp.sum(exchanged(sums, "seq_lo"), axis=0)
    sums = lax.psum(sums, "seq_hi")
    verdict_hidden, win = call(
        verdict_kernel,
        (shape((ROWS, width), jnp.bfloat16), shape((ROWS, HD), f32)),
        [VM, VM],
        "verdict",
    )(sums, gained)

    attended = attention(pair_lengths, seq_index, q_prefill, kv)
    return (attended, verdict_hidden, win[:, 0])


def solution(mesh):
    groups, seq = mesh.shape["groups"], mesh.shape["seq"]
    torus = Mesh(
        mesh.devices.reshape(groups, seq // LO, LO, mesh.shape["tp"] // 2, 2),
        ("groups",) + SEQ + TP,
    )
    tokens = ("groups",) + SEQ
    return jax.shard_map(
        shards,
        mesh=torus,
        in_specs=(
            P(tokens, TP),
            P(tokens, TP),
            P(tokens, TP),
            P("groups"),
            P("groups", TP),
            P("groups", SEQ, TP),
            P("groups", SEQ, TP),
            P("groups"),
            P("groups", SEQ),
            P(TP, SEQ),
            P(SEQ),
            P(TP, SEQ),
            P("groups", None),
        ),
        out_specs=(P(tokens, TP), P("groups", SEQ), P("groups")),
        check_vma=False,
    )
```

time: 407 us -> 238 us (0.58)
  waiting for transfers between devices: 132 us -> 27.1 us
  starting transfers between devices: 50.5 us -> 18.3 us
  other arithmetic: 32.1 us -> 3.64 us
  local copies, waits for them, and re-layouts: 24.6 us -> 8.97 us
  Pallas kernels: 0 us -> 15.1 us
  blocking collectives: 141 us -> 149 us
  loops' own time: 6.09 us -> 0 us
  matrix products: 5.65 us -> 0 us
    all_gather x1, waiting for transfers between devices: 75.6 us -> 0.01 us  [shards(): lax.all_gather(jnp.concatenate([k_prefill, v_prefill], axis=1), SEQ, axis...]
    all_gather x1 -> x0, blocking collectives: 73.7 us -> none  [total_of_pieces(): pieces = lax.all_gather(shard, axis).astype(jnp.float32)]
    all_to_all x0 -> x3, blocking collectives: none -> 67.4 us  [exchanged(): return lax.all_to_all(copies, axis, 0, 0, tiled=True)]
    all_to_all x2, starting transfers between devices: 50.5 us -> 18.3 us  [exchanged(): return lax.all_to_all(copies, axis, 0, 0, tiled=True)]
    all_to_all x2, waiting for transfers between devices: 56.7 us -> 27.1 us  [exchanged(): return lax.all_to_all(copies, axis, 0, 0, tiled=True)]
    pallas_call x0 -> x7, Pallas kernels: none -> 15.1 us  [the longest x1 3.74 us: attention(): pl.pallas_call(attention_kernel, out_shape=jax.ShapeDtypeStruct(q.shape,...]
    psum x3 -> x2, blocking collectives: 67 us -> 82 us  [the longest x1 65.4 us: shards(): rows = lax.psum(rows, 'seq_hi')]
    reduce_or x8 -> x0, other arithmetic: 12.4 us -> none  [attend(): jnp.any(visible)]
  transfers between devices with their start and end apart: 3 -> 3, of which waited for: 3 -> 2; matrix products, arithmetic and copies ran while one was open for 5% -> 3% of each run, Pallas kernels for 0% -> 5%
where the time goes in v1:
time: 238 us; the launch traced here: 237 us
  blocking collectives  149 us (63%)
  waiting for transfers between devices  27.1 us (11%)
  starting transfers between devices  18.3 us (8%)
  Pallas kernels  15.1 us (6%)
  between operations  14.2 us (6%)
  local copies, waits for them, and re-layouts  8.97 us (4%)
  other arithmetic  3.64 us (2%)
    all_to_all x3, blocking collectives, exchanged(): return lax.all_to_all(copies, axis, 0, 0, tiled=True)  67.4 us
    psum x1, blocking collectives, shards(): rows = lax.psum(rows, 'seq_hi')  65.4 us
    all_to_all x2, waiting for transfers between devices, exchanged(): return lax.all_to_all(copies, axis, 0, 0, tiled=True)  27.1 us
    all_to_all x2, starting transfers between devices, exchanged(): return lax.all_to_all(copies, axis, 0, 0, tiled=True)  18.3 us
    psum x1, blocking collectives, shards(): sums = lax.psum(sums, 'seq_hi')  16.6 us
  transfers between devices with their start and end apart: 3, of which 2 were waited for; matrix products, arithmetic and copies ran while one was open for 3% of the time, Pallas kernels for 5%

profile of v1, /device:TPU:40, one launch (start us, length us, event | category | flops | bytes accessed | tf_op | source)
XLA Modules:
  0.0 236.7 jit_solution(4386684543074117743)
XLA Ops:
  7.2 0.0 copy-start.2
  7.2 0.0 copy-start.1
  7.2 0.1 all-gather.2.cloned.1.call-start
  7.3 1.5 pad_maximum_fusion
  8.8 0.1 all-gather.2.cloned.1.call-update
  8.9 1.7 last_rows.1
  10.6 29.4 %all_to_all.25 = bf16[8,8,512]{2,1,0:T(8,128)(2,1)S(1)} all-to-all(bf16[8,8,512]{2,1,0:T(8,128)(2,1)} %last_rows.1), channel_id=1, replica_groups=mesh['groups'=2,'seq_hi'=4,'seq_lo'=8,'tp_0'=4,'tp_1'=2] {'seq_lo'}, dimensions={0} | all-to-all | bytes 131072 | tf_op jit(solution)/shard_map/all_to_all | solution.py:36
  40.1 65.4 %psum.14.rows_ref = f32[8,512]{1,0:T(8,128)} all-reduce(f32[8,512]{1,0:T(8,128)S(1)} %convert_reduce_fusion), channel_id=1, replica_groups=mesh['groups'=2,'seq_hi'=4,'seq_lo'=8,'tp_0'=4,'tp_1'=2] {'seq_hi'}, use_global_device_ids=true, to_apply=%region_1.0 | all-reduce | flops 4096 | bytes 32768 | tf_op jit(solution)/shard_map/psum | solution.py:315
  105.5 2.1 partials.1
  107.6 18.8 %all_to_all.26.pieces_ref = f32[8,64,128]{2,1,0:T(8,128)} all-to-all(f32[8,64,128]{2,1,0:T(8,128)} %partials.1), channel_id=1, replica_groups=mesh['groups'=2,'seq_hi'=4,'seq_lo'=8,'tp_0'=4,'tp_1'=2] {'seq_lo'}, dimensions={0} | all-to-all | bytes 524288 | tf_op jit(solution)/shard_map/all_to_all | solution.py:36
  126.4 2.1 merge.1
  128.5 13.8 %all-to-all-start.2 = ((f32[4,64,128]{2,1,0:T(8,128)}), f32[4,64,128]{2,1,0:T(8,128)S(1)}, u32[]{:S(2)}, u32[]{:S(2)}) async-start(f32[4,64,128]{2,1,0:T(8,128)} %merge.1), calls=%async_computation.2 | async-start | bytes 262144 | tf_op jit(solution)/shard_map/all_to_all | solution.py:36
  142.3 0.7 fusion
  143.0 0.1 min.12
  143.1 0.7 compare_and_fusion
  143.7 0.1 and.15
  143.8 3.3 %gather_fusion = bf16[32,256]{1,0:T(8,128)(2,1)S(1)} fusion(bf16[8016,256]{1,0:T(8,128)(2,1)} %param.24, s32[1024]{0:T(1024)S(1)} %pad_clamp_fusion), kind=kCustom, calls=%fused_computation | custom fusion | bytes 32896 | tf_op jit(solution)/shard_map/gather | solution.py:335
  147.1 0.7 convert_select_fusion.table_ref
  147.8 18.7 %all-to-all-done.2.pieces_ref = f32[4,64,128]{2,1,0:T(8,128)S(1)} async-done(((f32[4,64,128]{2,1,0:T(8,128)}), f32[4,64,128]{2,1,0:T(8,128)S(1)}, u32[]{:S(2)}, u32[]{:S(2)}) %all-to-all-start.2) | async-done | bytes 131104 | tf_op jit(solution)/shard_map/all_to_all | solution.py:36
  166.6 0.7 copy-done.4
  167.2 2.2 project.1
  169.4 4.5 %all-to-all-start.3 = ((f32[8,48,256]{2,1,0:T(8,128)}), f32[8,48,256]{2,1,0:T(8,128)S(1)}, u32[]{:S(2)}, u32[]{:S(2)}) async-start(f32[8,48,256]{2,1,0:T(8,128)} %project.1), calls=%async_computation.3 | async-start | bytes 786432 | tf_op jit(solution)/shard_map/all_to_all | solution.py:36
  173.9 0.6 reshape.54.gain_ref
  174.5 8.3 %all-to-all-done.3.pieces_ref = f32[8,48,256]{2,1,0:T(8,128)S(1)} async-done(((f32[8,48,256]{2,1,0:T(8,128)}), f32[8,48,256]{2,1,0:T(8,128)S(1)}, u32[]{:S(2)}, u32[]{:S(2)}) %all-to-all-start.3) | async-done | bytes 393248 | tf_op jit(solution)/shard_map/all_to_all | solution.py:36
  182.8 0.7 copy-done.3
  183.6 1.8 residual.1
  185.3 19.1 %all_to_all.27 = f32[8,12,128]{2,1,0:T(8,128)S(1)} all-to-all(f32[8,12,128]{2,1,0:T(8,128)} %get-tuple-element.7), channel_id=1, replica_groups=mesh['groups'=2,'seq_hi'=4,'seq_lo'=8,'tp_0'=4,'tp_1'=2] {'seq_lo'}, dimensions={0} | all-to-all | bytes 98304 | tf_op jit(solution)/shard_map/all_to_all | solution.py:36
  204.4 16.6 %psum.15.sums_ref = f32[12,128]{1,0:T(8,128)} all-reduce(f32[12,128]{1,0:T(8,128)S(1)} %reduce_sum.19), channel_id=1, replica_groups=mesh['groups'=2,'seq_hi'=4,'seq_lo'=8,'tp_0'=4,'tp_1'=2] {'seq_hi'}, use_global_device_ids=true, to_apply=%region_3.4 | all-reduce | flops 1536 | bytes 12288 | tf_op jit(solution)/shard_map/psum | solution.py:349
  221.0 1.6 verdict.1
  222.6 1.3 slice_reduce_fusion
  223.9 2.2 copy-done
  226.1 3.7 %attention.1 = bf16[256,512]{1,0:T(8,128)(2,1)} custom-call(s32[8]{0:T(128)S(1)} %copy-done.2, s32[1]{0:T(128)} %bitcast.seq_ref, bf16[256,512]{1,0:T(8,128)(2,1)S(1)} %copy-done.1, bf16[8192,256]{1,0:T(8,128)(2,1)S(1)} %copy-done), custom_call_target="tpu_custom_call" | custom-call | tf_op jit(solution)/shard_map/attention/pallas_call | solution.py:256
  (12 shorter events, 0.1 us)
Async XLA Ops:
  7.2 216.7 %copy-start.2 = (s32[8]{0:T(128)S(1)}, s32[8]{0:T(128)}, u32[]{:S(2)}) copy-start(s32[8]{0:T(128)} %lengths_ref.5) | copy-start | bytes 100
  7.2 216.7 %copy-start.1 = (bf16[256,512]{1,0:T(8,128)(2,1)S(1)}, bf16[256,512]{1,0:T(8,128)(2,1)}, u32[]{:S(2)}) copy-start(bf16[256,512]{1,0:T(8,128)(2,1)} %q_ref.3) | copy-start | bytes 786436
  7.2 166.7 %copy-start.5 = (bf16[256]{0:T(256)(128)(2,1)S(1)}, bf16[256]{0:T(256)(128)(2,1)}, u32[]{:S(2)}) copy-start(bf16[256]{0:T(256)(128)(2,1)} %param.23) | copy-start | bytes 1540
  7.2 216.7 %all-gather.2.cloned.1.call-start = ((), (), s32[]{:S(2)}) async-start(), calls=%async_computation.5 | async-start | bytes 4325376 | tf_op jit(solution)/shard_map/all_gather | solution.py:309
  128.5 38.1 %all-to-all-start.2 = ((f32[4,64,128]{2,1,0:T(8,128)}), f32[4,64,128]{2,1,0:T(8,128)S(1)}, u32[]{:S(2)}, u32[]{:S(2)}) async-start(f32[4,64,128]{2,1,0:T(8,128)} %merge.1), calls=%async_computation.2 | async-start | bytes 262144 | tf_op jit(solution)/shard_map/all_to_all | solution.py:36
  166.6 0.7 copy-start.4
  169.4 13.4 %all-to-all-start.3 = ((f32[8,48,256]{2,1,0:T(8,128)}), f32[8,48,256]{2,1,0:T(8,128)S(1)}, u32[]{:S(2)}, u32[]{:S(2)}) async-start(f32[8,48,256]{2,1,0:T(8,128)} %project.1), calls=%async_computation.3 | async-start | bytes 786432 | tf_op jit(solution)/shard_map/all_to_all | solution.py:36
  182.8 0.7 copy-start.3
  223.9 2.2 copy-start
Sparse Core Ops, SparseCore 0:
  10.1 176.5 all-gather.1

commit v2 on v1

--- a/solution.py
+++ b/solution.py
@@ -44,7 +44,9 @@
     return ends
 
 
-def last_rows_kernel(lengths_ref, seq_ref, q_ref, out_ref):
+def last_rows_kernel(lengths_ref, seq_ref, q_ref, k_ref, v_ref, out_ref, kv_ref):
+    kv_ref[:, :HD] = k_ref[...]
+    kv_ref[:, HD:] = v_ref[...]
     tokens = q_ref.shape[0]
     ends = ends_of(lengths_ref)
     row = lax.broadcasted_iota(jnp.int32, (SLOT, tokens), 0)
@@ -98,31 +100,45 @@
     put_partials(out_ref, sums, top, total)
 
 
+def three_parts(x):
+    high = x.astype(jnp.bfloat16).astype(jnp.float32)
+    middle = (x - high).astype(jnp.bfloat16).astype(jnp.float32)
+    return high, middle, x - high - middle
+
+
 def put_partials(out_ref, sums, top, total):
     across = (GROUP * SLOT, HD)
-    top_lanes = jnp.transpose(jnp.broadcast_to(top, across))[:1]
-    total_lanes = jnp.transpose(jnp.broadcast_to(total, across))[:1]
+    row = lax.broadcasted_iota(jnp.int32, across, 0)
+    packed = sums
+    for first, column in ((ROWS, top), (SLOT + ROWS, total)):
+        lanes = jnp.transpose(jnp.broadcast_to(column, across))[:1]
+        lanes = jnp.concatenate([lanes, jnp.zeros_like(lanes)], axis=1)
+        for j, part in enumerate(three_parts(lanes)):
+            packed = jnp.where(row == first + j, part, packed)
+    packed = packed.astype(out_ref.dtype)
     for c in range(out_ref.shape[0]):
-        out_ref[c] = sums
-        out_ref[c, ROWS : ROWS + 1, : GROUP * SLOT] = top_lanes
-        out_ref[c, ROWS + 1 : ROWS + 2, : GROUP * SLOT] = total_lanes
+        out_ref[c] = packed
 
 
 def merged(pieces_ref):
     count = pieces_ref.shape[0]
-    tops, totals = [], []
-    for c in range(count):
-        both = pieces_ref[c, ROWS - 4 : ROWS + 4, :]
-        columns = jnp.transpose(both)[: GROUP * SLOT]
-        tops.append(columns[:, 4:5])
-        totals.append(columns[:, 5:6])
+    pieces = [pieces_ref[c].astype(jnp.float32) for c in range(count)]
+
+    def columns(first):
+        lines = [
+            jnp.sum(piece[first : first + 3], axis=0, keepdims=True) for piece in pieces
+        ] + [jnp.zeros((8 - count % 8, HD), jnp.float32)] * (count % 8 > 0)
+        turned = jnp.transpose(jnp.concatenate(lines, axis=0))[: GROUP * SLOT]
+        return [turned[:, c : c + 1] for c in range(count)]
+
+    tops, totals = columns(ROWS), columns(SLOT + ROWS)
     top = functools.reduce(jnp.maximum, tops)
     total = jnp.zeros_like(top)
     sums = jnp.zeros((GROUP * SLOT, HD), jnp.float32)
     for c in range(count):
         scale = jnp.exp(tops[c] - top)
         total = total + totals[c] * scale
-        sums = sums + pieces_ref[c] * scale
+        sums = sums + pieces[c] * scale
     return sums, top, total
 
 
@@ -140,11 +156,9 @@
             w_ref[g * HD : (g + 1) * HD, :],
             preferred_element_type=jnp.float32,
         )
-    keep = lax.broadcasted_iota(jnp.int32, partial.shape, 0) < ROWS
-    partial = jnp.where(keep, partial, 0.0)
     for c in range(out_ref.shape[0]):
-        out_ref[c, :SLOT] = partial
-        out_ref[c, SLOT:] = table_ref[...]
+        out_ref[c, :ROWS] = partial[:ROWS]
+        out_ref[c, ROWS : 3 * ROWS] = table_ref[...]
 
 
 def residual_kernel(pieces_ref, stream_ref, gain_ref, gained_ref, sums_ref):
@@ -155,8 +169,8 @@
     gained = residual * gain_ref[...].astype(jnp.float32)
     gained_ref[...] = gained
     squares = jnp.sum(residual * residual, axis=1, keepdims=True)
-    first = jnp.sum(gained * total[SLOT : SLOT + ROWS], axis=1, keepdims=True)
-    second = jnp.sum(gained * total[2 * SLOT : 2 * SLOT + ROWS], axis=1, keepdims=True)
+    first = jnp.sum(gained * total[ROWS : 2 * ROWS], axis=1, keepdims=True)
+    second = jnp.sum(gained * total[2 * ROWS : 3 * ROWS], axis=1, keepdims=True)
     lane = lax.broadcasted_iota(jnp.int32, (ROWS, HD), 1)
     packed = jnp.where(lane == 0, squares, jnp.where(lane == 1, first, second))
     for c in range(sums_ref.shape[0]):
@@ -197,8 +211,8 @@
     top_ref[...] = jnp.full_like(top_ref, masked_score)
     total_ref[...] = jnp.zeros_like(total_ref)
     sum_ref[...] = jnp.zeros_like(sum_ref)
-    query_pos = lax.broadcasted_iota(jnp.int32, (tokens, 1), 0) + first
-    query_start = jnp.zeros((tokens, 1), jnp.int32)
+    query_pos = lax.broadcasted_iota(jnp.int32, (1, tokens), 1) + first
+    query_start = jnp.zeros((1, tokens), jnp.int32)
     for p in range(PAIRS):
         query_start = jnp.where(query_pos >= ends[p], ends[p], query_start)
 
@@ -206,27 +220,24 @@
         key_first = b * KEY_BLOCK
         rows = pl.ds(pl.multiple_of(key_first, KEY_BLOCK), KEY_BLOCK)
         keys = kv_buf[rows, :HD]
-        values = kv_buf[rows, HD:]
+        values = jnp.transpose(kv_buf[rows, HD:])
         if masked:
-            key_pos = lax.broadcasted_iota(jnp.int32, (tokens, KEY_BLOCK), 1) + key_first
+            key_pos = lax.broadcasted_iota(jnp.int32, (KEY_BLOCK, tokens), 0) + key_first
             visible = (key_pos >= query_start) & (key_pos <= query_pos)
         for g in range(GROUP):
-            columns = slice(g * HD, (g + 1) * HD)
-            scores = lax.dot_general(
-                q_ref[:, columns], keys, NT, preferred_element_type=jnp.float32
-            )
+            queries = q_ref[:, g * HD : (g + 1) * HD]
+            scores = lax.dot_general(keys, queries, NT, preferred_element_type=jnp.float32)
             if masked:
                 scores = jnp.where(visible, scores, masked_score)
             old_top = top_ref[g]
-            new_top = jnp.maximum(old_top, jnp.max(scores, axis=1, keepdims=True))
+            tops = jnp.max(scores.reshape(KEY_BLOCK // 8, 8, tokens), axis=0)
+            new_top = jnp.maximum(old_top, jnp.max(tops, axis=0, keepdims=True))
             rescale = jnp.exp2((old_top - new_top) * exp2_scale)
             terms = jnp.exp2((scores - new_top) * exp2_scale)
-            lanes = terms[:, :HD]
-            for j in range(1, KEY_BLOCK // HD):
-                lanes = lanes + terms[:, j * HD : (j + 1) * HD]
-            total_ref[g] = total_ref[g] * rescale + lanes
+            sums = jnp.sum(terms.reshape(KEY_BLOCK // 8, 8, tokens), axis=0)
+            total_ref[g] = total_ref[g] * rescale + sums
             sum_ref[g] = sum_ref[g] * rescale + jnp.dot(
-                terms.astype(jnp.bfloat16), values, preferred_element_type=jnp.float32
+                values, terms.astype(jnp.bfloat16), preferred_element_type=jnp.float32
             )
             top_ref[g] = new_top
 
@@ -247,8 +258,9 @@
 
     lax.fori_loop(low, high, step, 0)
     for g in range(GROUP):
-        total = jnp.sum(total_ref[g], axis=1, keepdims=True)
-        out_ref[:, g * HD : (g + 1) * HD] = (sum_ref[g] / total).astype(out_ref.dtype)
+        total = jnp.sum(total_ref[g], axis=0, keepdims=True)
+        rows = jnp.transpose(sum_ref[g] / total)
+        out_ref[:, g * HD : (g + 1) * HD] = rows.astype(out_ref.dtype)
 
 
 def attention(lengths, seq_index, q, kv):
@@ -256,16 +268,16 @@
     return pl.pallas_call(
         attention_kernel,
         out_shape=jax.ShapeDtypeStruct(q.shape, q.dtype),
-        in_specs=[SM, SM, VM, pl.BlockSpec(memory_space=pl.ANY)],
+        in_specs=[SM, SM, VM, pl.BlockSpec(memory_space=pltpu.HBM)],
         out_specs=VM,
         scratch_shapes=[
             pltpu.VMEM(kv.shape, kv.dtype),
-            pltpu.VMEM((GROUP, tokens, 1), jnp.float32),
-            pltpu.VMEM((GROUP, tokens, HD), jnp.float32),
-            pltpu.VMEM((GROUP, tokens, HD), jnp.float32),
+            pltpu.VMEM((GROUP, 1, tokens), jnp.float32),
+            pltpu.VMEM((GROUP, 8, tokens), jnp.float32),
+            pltpu.VMEM((GROUP, HD, tokens), jnp.float32),
             pltpu.SemaphoreType.DMA((kv.shape[0] // KEY_BLOCK,)),
         ],
-        compiler_params=pltpu.CompilerParams(vmem_limit_bytes=40 * 1024 * 1024),
+        compiler_params=pltpu.CompilerParams(vmem_limit_bytes=24 * 1024 * 1024),
         name="attention",
     )(lengths, seq_index, q, kv)
 
@@ -278,6 +290,7 @@
         in_specs=specs,
         out_specs=tuple(VM for _ in shapes) if many else VM,
         scratch_shapes=list(scratch),
+        compiler_params=pltpu.CompilerParams(vmem_limit_bytes=8 * 1024 * 1024),
         name=name,
     )
 
@@ -306,17 +319,22 @@
     seq_index = lax.axis_index(SEQ).astype(jnp.int32).reshape(1)
     shape = jax.ShapeDtypeStruct
 
-    kv = lax.all_gather(jnp.concatenate([k_prefill, v_prefill], axis=1), SEQ, axis=0, tiled=True)
-
-    picked = call(
-        last_rows_kernel, shape((lo, PAIRS, columns), jnp.bfloat16), [SM, SM, VM], "last_rows"
-    )(pair_lengths, seq_index, q_prefill)
+    picked, kv = call(
+        last_rows_kernel,
+        (
+            shape((lo, PAIRS, columns), jnp.bfloat16),
+            shape((q_prefill.shape[0], 2 * HD), jnp.bfloat16),
+        ),
+        [SM, SM, VM, VM, VM],
+        "last_rows",
+    )(pair_lengths, seq_index, q_prefill, k_prefill, v_prefill)
+    kv = lax.all_gather(kv, SEQ, axis=0, tiled=True)
     rows = jnp.sum(exchanged(picked, "seq_lo").astype(f32), axis=0)
     rows = lax.psum(rows, "seq_hi")
 
     partials = call(
         partials_kernel,
-        shape((lo, GROUP * SLOT, HD), f32),
+        shape((lo, GROUP * SLOT, HD), jnp.bfloat16),
         [SM, SM, SM] + [VM] * 6,
         "partials",
         [pltpu.VMEM((GROUP * SLOT, HD), f32)],
@@ -325,18 +343,18 @@
         cache_v,
     )
     partials = exchanged(partials, "seq_lo")
-    partials = call(merge_kernel, shape((hi, GROUP * SLOT, HD), f32), [VM], "merge")(partials)
+    partials = call(merge_kernel, shape((hi, GROUP * SLOT, HD), jnp.bfloat16), [VM], "merge")(partials)
     partials = exchanged(partials, "seq_hi")
 
     vocab_rows = vocab_table.shape[0]
-    ids = jnp.pad(verdict_ids.T, ((0, 0), (0, SLOT - ROWS))).reshape(-1)
+    ids = verdict_ids.T.reshape(-1)
     local_ids = ids - lax.axis_index(TP) * vocab_rows
     inside = ((local_ids >= 0) & (local_ids < vocab_rows))[:, None]
     table_rows = vocab_table[jnp.clip(local_ids, 0, vocab_rows - 1)]
     table_rows = jnp.where(inside, table_rows.astype(f32), 0.0)
 
     pieces = call(
-        project_kernel, shape((tp, 3 * SLOT, width), f32), [VM, VM, VM], "project"
+        project_kernel, shape((tp, 3 * ROWS, width), f32), [VM, VM, VM], "project"
     )(partials, out_weight, table_rows)
     pieces = exchanged(pieces, TP)
     gained, sums = call(

time: 238 us -> 229 us (0.962)
  blocking collectives: 149 us -> 127 us
  waiting for transfers between devices: 27.1 us -> 37.4 us
  local copies, waits for them, and re-layouts: 8.97 us -> 18.8 us
  Pallas kernels: 15.1 us -> 9.71 us
    all_to_all x3 -> x2, blocking collectives: 67.4 us -> 44.5 us  [exchanged(): return lax.all_to_all(copies, axis, 0, 0, tiled=True)]
    unnamed x12 -> x32, local copies, waits for them, and re-layouts: 3.6 us -> 14.1 us
    all_to_all x2 -> x3, waiting for transfers between devices: 27.1 us -> 37.3 us  [exchanged(): return lax.all_to_all(copies, axis, 0, 0, tiled=True)]
    pallas_call x4, Pallas kernels: 8.07 us -> 5.5 us  [the longest x1 1.6 us: shards(): call(partials_kernel, shape((lo, GROUP * SLOT, HD), jnp.bfloat16), [SM, S...]
    all_to_all x2 -> x3, starting transfers between devices: 18.3 us -> 19.6 us  [exchanged(): return lax.all_to_all(copies, axis, 0, 0, tiled=True)]
  transfers between devices with their start and end apart: 3 -> 4, of which waited for: 2 -> 3; matrix products, arithmetic and copies ran while one was open for 3% -> 3% of each run, Pallas kernels for 5% -> 2%
where the time goes in v2:
time: 229 us; the launch traced here: 228 us
  blocking collectives  127 us (55%)
  waiting for transfers between devices  37.4 us (16%)
  starting transfers between devices  19.7 us (9%)
  local copies, waits for them, and re-layouts  18.8 us (8%)
  between operations  14.2 us (6%)
  Pallas kernels  9.71 us (4%)
    psum x1, blocking collectives, shards(): rows = lax.psum(rows, 'seq_hi')  64.8 us
    all_to_all x2, blocking collectives, exchanged(): return lax.all_to_all(copies, axis, 0, 0, tiled=True)  44.5 us
    all_to_all x3, waiting for transfers between devices, exchanged(): return lax.all_to_all(copies, axis, 0, 0, tiled=True)  37.3 us
    all_to_all x3, starting transfers between devices, exchanged(): return lax.all_to_all(copies, axis, 0, 0, tiled=True)  19.6 us
    psum x1, blocking collectives, shards(): sums = lax.psum(sums, 'seq_hi')  17.3 us
    unnamed x32, local copies, waits for them, and re-layouts  14.1 us
  transfers between devices with their start and end apart: 4, of which 3 were waited for; matrix products, arithmetic and copies ran while one was open for 3% of the time, Pallas kernels for 2%

profile of v2, /device:TPU:40, one launch (start us, length us, event | category | flops | bytes accessed | tf_op | source)
XLA Modules:
  0.0 227.8 jit_solution(2188356814303538806)
XLA Ops:
  7.3 0.9 copy-done.1
  8.2 0.8 copy-done.3
  9.0 0.8 copy-done.5
  10.5 1.2 last_rows.1
  11.8 29.3 %all_to_all.25 = bf16[8,8,512]{2,1,0:T(8,128)(2,1)S(1)} all-to-all(bf16[8,8,512]{2,1,0:T(8,128)(2,1)S(1)} %get-tuple-element.10), channel_id=1, replica_groups=mesh['groups'=2,'seq_hi'=4,'seq_lo'=8,'tp_0'=4,'tp_1'=2] {'seq_lo'}, dimensions={0} | all-to-all | bytes 131072 | tf_op jit(solution)/shard_map/all_to_all | solution.py:36
  41.1 64.8 %psum.14.rows_ref = f32[8,512]{1,0:T(8,128)S(1)} all-reduce(f32[8,512]{1,0:T(8,128)S(1)} %convert_reduce_fusion), channel_id=1, replica_groups=mesh['groups'=2,'seq_hi'=4,'seq_lo'=8,'tp_0'=4,'tp_1'=2] {'seq_hi'}, use_global_device_ids=true, to_apply=%region_1.0 | all-reduce | flops 4096 | bytes 32768 | tf_op jit(solution)/shard_map/psum | solution.py:333
  105.9 0.8 copy-done.4
  106.7 0.8 copy-done.6
  107.6 0.8 copy-done.8
  108.4 0.8 copy-done.9
  109.9 0.7 copy-done.14
  111.3 1.6 partials.1
  112.9 3.6 %all-to-all-start.1 = ((bf16[8,64,128]{2,1,0:T(8,128)(2,1)}), bf16[8,64,128]{2,1,0:T(8,128)(2,1)S(1)}, u32[]{:S(2)}, u32[]{:S(2)}) async-start(bf16[8,64,128]{2,1,0:T(8,128)(2,1)} %partials.1), calls=%async_computation.1 | async-start | bytes 262144 | tf_op jit(solution)/shard_map/all_to_all | solution.py:36
  116.5 0.7 clamp_bitcast_fusion
  117.2 0.7 and_bitcast_fusion
  117.9 10.7 %all-to-all-done.1.pieces_ref = bf16[8,64,128]{2,1,0:T(8,128)(2,1)S(1)} async-done(((bf16[8,64,128]{2,1,0:T(8,128)(2,1)}), bf16[8,64,128]{2,1,0:T(8,128)(2,1)S(1)}, u32[]{:S(2)}, u32[]{:S(2)}) %all-to-all-start.1) | async-done | bytes 131104 | tf_op jit(solution)/shard_map/all_to_all | solution.py:36
  128.6 1.3 merge.1
  129.9 11.3 %all-to-all-start.2 = ((bf16[4,64,128]{2,1,0:T(8,128)(2,1)}), bf16[4,64,128]{2,1,0:T(8,128)(2,1)S(1)}, u32[]{:S(2)}, u32[]{:S(2)}) async-start(bf16[4,64,128]{2,1,0:T(8,128)(2,1)} %merge.1), calls=%async_computation.2 | async-start | bytes 131072 | tf_op jit(solution)/shard_map/all_to_all | solution.py:36
  141.3 3.3 %gather_fusion = bf16[24,256]{1,0:T(8,128)(2,1)S(1)} fusion(bf16[8016,256]{1,0:T(8,128)(2,1)} %param.24, s32[1024]{0:T(1024)S(1)} %pad_clamp_fusion), kind=kCustom, calls=%fused_computation | custom fusion | bytes 24672 | tf_op jit(solution)/shard_map/gather | solution.py:353
  144.6 19.1 %all-to-all-done.2.pieces_ref = bf16[4,64,128]{2,1,0:T(8,128)(2,1)S(1)} async-done(((bf16[4,64,128]{2,1,0:T(8,128)(2,1)}), bf16[4,64,128]{2,1,0:T(8,128)(2,1)S(1)}, u32[]{:S(2)}, u32[]{:S(2)}) %all-to-all-start.2) | async-done | bytes 65568 | tf_op jit(solution)/shard_map/all_to_all | solution.py:36
  163.7 0.9 copy-done.7
  164.7 1.3 project.1
  166.0 4.8 %all-to-all-start.3 = ((f32[8,36,256]{2,1,0:T(8,128)}), f32[8,36,256]{2,1,0:T(8,128)S(1)}, u32[]{:S(2)}, u32[]{:S(2)}) async-start(f32[8,36,256]{2,1,0:T(8,128)} %project.1), calls=%async_computation.3 | async-start | bytes 655360 | tf_op jit(solution)/shard_map/all_to_all | solution.py:36
  170.8 0.7 reshape.54.gain_ref
  171.4 7.6 %all-to-all-done.3.pieces_ref = f32[8,36,256]{2,1,0:T(8,128)S(1)} async-done(((f32[8,36,256]{2,1,0:T(8,128)}), f32[8,36,256]{2,1,0:T(8,128)S(1)}, u32[]{:S(2)}, u32[]{:S(2)}) %all-to-all-start.3) | async-done | bytes 294944 | tf_op jit(solution)/shard_map/all_to_all | solution.py:36
  179.0 0.7 copy-done.10
  179.8 15.3 %all_to_all.26 = f32[8,12,128]{2,1,0:T(8,128)S(1)} all-to-all(f32[8,12,128]{2,1,0:T(8,128)S(1)} %get-tuple-element.11), channel_id=1, replica_groups=mesh['groups'=2,'seq_hi'=4,'seq_lo'=8,'tp_0'=4,'tp_1'=2] {'seq_lo'}, dimensions={0} | all-to-all | bytes 98304 | tf_op jit(solution)/shard_map/all_to_all | solution.py:36
  195.0 17.3 %psum.15.sums_ref = f32[12,128]{1,0:T(8,128)S(1)} all-reduce(f32[12,128]{1,0:T(8,128)S(1)} %reduce_sum.19), channel_id=1, replica_groups=mesh['groups'=2,'seq_hi'=4,'seq_lo'=8,'tp_0'=4,'tp_1'=2] {'seq_hi'}, use_global_device_ids=true, to_apply=%region_3.4 | all-reduce | flops 1536 | bytes 12288 | tf_op jit(solution)/shard_map/psum | solution.py:367
  212.3 0.7 verdict.1
  213.6 2.2 copy-done
  215.8 0.9 copy-done.2
  217.4 3.4 %attention.1 = bf16[256,512]{1,0:T(8,128)(2,1)} custom-call(s32[8]{0:T(128)S(1)} %copy-done.13, s32[1]{0:T(128)} %bitcast.seq_ref, bf16[256,512]{1,0:T(8,128)(2,1)S(1)} %copy-done.2, bf16[8192,256]{1,0:T(8,128)(2,1)S(1)} %copy-done), custom_call_target="tpu_custom_call" | custom-call | tf_op jit(solution)/shard_map/attention/pallas_call | solution.py:268
  (32 shorter events, 3.8 us)
Async XLA Ops:
  7.2 206.5 %all-gather.2.cloned.1.call-start = ((), (), s32[]{:S(2)}) async-start(), calls=%async_computation.5 | async-start | bytes 4325376 | tf_op jit(solution)/shard_map/all_gather | solution.py:331
  7.3 1.0 copy-start.1
  8.2 0.8 copy-start.3
  9.0 0.8 copy-start.5
  9.9 0.7 copy-start.11
  105.9 0.8 copy-start.4
  106.7 0.8 copy-start.6
  107.6 0.8 copy-start.8
  108.4 0.8 copy-start.9
  109.3 0.7 copy-start.12
  109.9 0.7 copy-start.14
  110.6 0.7 copy-start.15
  112.9 15.7 %all-to-all-start.1 = ((bf16[8,64,128]{2,1,0:T(8,128)(2,1)}), bf16[8,64,128]{2,1,0:T(8,128)(2,1)S(1)}, u32[]{:S(2)}, u32[]{:S(2)}) async-start(bf16[8,64,128]{2,1,0:T(8,128)(2,1)} %partials.1), calls=%async_computation.1 | async-start | bytes 262144 | tf_op jit(solution)/shard_map/all_to_all | solution.py:36
  129.9 33.8 %all-to-all-start.2 = ((bf16[4,64,128]{2,1,0:T(8,128)(2,1)}), bf16[4,64,128]{2,1,0:T(8,128)(2,1)S(1)}, u32[]{:S(2)}, u32[]{:S(2)}) async-start(bf16[4,64,128]{2,1,0:T(8,128)(2,1)} %merge.1), calls=%async_computation.2 | async-start | bytes 131072 | tf_op jit(solution)/shard_map/all_to_all | solution.py:36
  163.7 1.0 copy-start.7
  166.0 13.0 %all-to-all-start.3 = ((f32[8,36,256]{2,1,0:T(8,128)}), f32[8,36,256]{2,1,0:T(8,128)S(1)}, u32[]{:S(2)}, u32[]{:S(2)}) async-start(f32[8,36,256]{2,1,0:T(8,128)} %project.1), calls=%async_computation.3 | async-start | bytes 655360 | tf_op jit(solution)/shard_map/all_to_all | solution.py:36
  179.0 0.7 copy-start.10
  213.6 2.2 copy-start
  215.8 0.9 copy-start.2
  216.8 0.7 copy-start.13
Sparse Core Ops, SparseCore 0:
  12.0 168.8 all-gather.1

commit v3 on v2

--- a/solution.py
+++ b/solution.py
@@ -30,6 +30,13 @@
 NT = (((1,), (1,)), ((), ()))
 VM = pl.BlockSpec(memory_space=pltpu.VMEM)
 SM = pl.BlockSpec(memory_space=pltpu.SMEM)
+HB = pl.BlockSpec(memory_space=pltpu.HBM)
+PIPE = pl.BlockSpec()
+TABLE_ROWS = 16
+
+
+def held(x):
+    return pltpu.with_memory_space_constraint(x, pltpu.HBM)
 
 
 def exchanged(copies, axis):
@@ -69,7 +76,9 @@
     ends = ends_of(lengths_ref)
     q_scratch[...] = jnp.zeros_like(q_scratch)
     for g in range(GROUP):
-        q_scratch[g * SLOT : g * SLOT + PAIRS, :] = rows_ref[:, g * HD : (g + 1) * HD]
+        q_scratch[g * SLOT : g * SLOT + PAIRS, :] = rows_ref[
+            :, g * HD : (g + 1) * HD
+        ].astype(jnp.float32)
         q_scratch[g * SLOT + PAIRS : g * SLOT + ROWS, :] = qd_ref[
             :, g * HD : (g + 1) * HD
         ].astype(jnp.float32)
@@ -146,7 +155,22 @@
     put_partials(out_ref, *merged(pieces_ref))
 
 
-def project_kernel(pieces_ref, w_ref, table_ref, out_ref):
+def project_kernel(
+    ids_ref, tp_ref, pieces_ref, w_ref, table_ref, out_ref, blocks, rows_scratch, sems
+):
+    vocab_rows = table_ref.shape[0]
+    picks = []
+    for c in range(2):
+        for r in range(ROWS):
+            local = ids_ref[r, c] - tp_ref[0] * vocab_rows
+            inside = (local >= 0) & (local < vocab_rows)
+            local = jnp.clip(local, 0, vocab_rows - 1)
+            picks.append((jnp.where(inside, local % TABLE_ROWS, -1), local // TABLE_ROWS))
+    copies = []
+    for i, (_, block) in enumerate(picks):
+        rows = pl.ds(pl.multiple_of(block * TABLE_ROWS, TABLE_ROWS), TABLE_ROWS)
+        copies.append(pltpu.make_async_copy(table_ref.at[rows], blocks.at[i], sems.at[i]))
+        copies[-1].start()
     sums, _, total = merged(pieces_ref)
     rows = sums / total
     partial = jnp.zeros((SLOT, w_ref.shape[1]), jnp.float32)
@@ -156,9 +180,15 @@
             w_ref[g * HD : (g + 1) * HD, :],
             preferred_element_type=jnp.float32,
         )
+    for copy in copies:
+        copy.wait()
+    index = lax.broadcasted_iota(jnp.int32, (TABLE_ROWS, w_ref.shape[1]), 0)
+    for i, (row, _) in enumerate(picks):
+        block = jnp.where(index == row, blocks[i].astype(jnp.float32), 0.0)
+        rows_scratch[i : i + 1, :] = jnp.sum(block, axis=0, keepdims=True)
     for c in range(out_ref.shape[0]):
         out_ref[c, :ROWS] = partial[:ROWS]
-        out_ref[c, ROWS : 3 * ROWS] = table_ref[...]
+        out_ref[c, ROWS : 3 * ROWS] = rows_scratch[...]
 
 
 def residual_kernel(pieces_ref, stream_ref, gain_ref, gained_ref, sums_ref):
@@ -268,7 +298,7 @@
     return pl.pallas_call(
         attention_kernel,
         out_shape=jax.ShapeDtypeStruct(q.shape, q.dtype),
-        in_specs=[SM, SM, VM, pl.BlockSpec(memory_space=pltpu.HBM)],
+        in_specs=[SM, SM, PIPE, HB],
         out_specs=VM,
         scratch_shapes=[
             pltpu.VMEM(kv.shape, kv.dtype),
@@ -279,7 +309,7 @@
         ],
         compiler_params=pltpu.CompilerParams(vmem_limit_bytes=24 * 1024 * 1024),
         name="attention",
-    )(lengths, seq_index, q, kv)
+    )(lengths, seq_index, held(q), held(kv))
 
 
 def call(kernel, shapes, specs, name, scratch=()):
@@ -316,6 +346,7 @@
     tp = lax.axis_size(TP)
     columns = q_prefill.shape[1]
     width = stream.shape[1]
+    pair_lengths, cache_lengths = held(pair_lengths), held(cache_lengths)
     seq_index = lax.axis_index(SEQ).astype(jnp.int32).reshape(1)
     shape = jax.ShapeDtypeStruct
 
@@ -325,44 +356,46 @@
             shape((lo, PAIRS, columns), jnp.bfloat16),
             shape((q_prefill.shape[0], 2 * HD), jnp.bfloat16),
         ),
-        [SM, SM, VM, VM, VM],
+        [SM, SM, PIPE, PIPE, PIPE],
         "last_rows",
-    )(pair_lengths, seq_index, q_prefill, k_prefill, v_prefill)
+    )(pair_lengths, seq_index, held(q_prefill), held(k_prefill), held(v_prefill))
     kv = lax.all_gather(kv, SEQ, axis=0, tiled=True)
     rows = jnp.sum(exchanged(picked, "seq_lo").astype(f32), axis=0)
-    rows = lax.psum(rows, "seq_hi")
+    rows = lax.psum(rows.astype(jnp.bfloat16), "seq_hi")
 
     partials = call(
         partials_kernel,
         shape((lo, GROUP * SLOT, HD), jnp.bfloat16),
-        [SM, SM, SM] + [VM] * 6,
+        [SM, SM, SM, VM] + [PIPE] * 5,
         "partials",
         [pltpu.VMEM((GROUP * SLOT, HD), f32)],
     )(
-        pair_lengths, cache_lengths, seq_index, rows, q_decode, k_prefill, v_prefill, cache_k,
-        cache_v,
+        pair_lengths, cache_lengths, seq_index, rows, held(q_decode), held(k_prefill),
+        held(v_prefill), held(cache_k), held(cache_v),
     )
     partials = exchanged(partials, "seq_lo")
     partials = call(merge_kernel, shape((hi, GROUP * SLOT, HD), jnp.bfloat16), [VM], "merge")(partials)
     partials = exchanged(partials, "seq_hi")
 
-    vocab_rows = vocab_table.shape[0]
-    ids = verdict_ids.T.reshape(-1)
-    local_ids = ids - lax.axis_index(TP) * vocab_rows
-    inside = ((local_ids >= 0) & (local_ids < vocab_rows))[:, None]
-    table_rows = vocab_table[jnp.clip(local_ids, 0, vocab_rows - 1)]
-    table_rows = jnp.where(inside, table_rows.astype(f32), 0.0)
-
+    tp_index = lax.axis_index(TP).astype(jnp.int32).reshape(1)
     pieces = call(
-        project_kernel, shape((tp, 3 * ROWS, width), f32), [VM, VM, VM], "project"
-    )(partials, out_weight, table_rows)
+        project_kernel,
+        shape((tp, 3 * ROWS, width), f32),
+        [SM, SM, VM, PIPE, HB],
+        "project",
+        [
+            pltpu.VMEM((2 * ROWS, TABLE_ROWS, width), jnp.bfloat16),
+            pltpu.VMEM((2 * ROWS, width), f32),
+            pltpu.SemaphoreType.DMA((2 * ROWS,)),
+        ],
+    )(verdict_ids, tp_index, partials, held(out_weight), held(vocab_table))
     pieces = exchanged(pieces, TP)
     gained, sums = call(
         residual_kernel,
         (shape((ROWS, width), f32), shape((lo, ROWS, HD), f32)),
-        [VM, VM, VM],
+        [VM, PIPE, PIPE],
         "residual",
-    )(pieces, stream, norm_gain.reshape(1, width))
+    )(pieces, held(stream), held(norm_gain.reshape(1, width)))
     sums = jnp.sum(exchanged(sums, "seq_lo"), axis=0)
     sums = lax.psum(sums, "seq_hi")
     verdict_hidden, win = call(

time: 229 us -> 204 us (0.89)
  local copies, waits for them, and re-layouts: 18.8 us -> 1.96 us
  waiting for transfers between devices: 37.4 us -> 29.7 us
  Pallas kernels: 9.71 us -> 14.5 us
  starting transfers between devices: 19.7 us -> 16.2 us
    all_to_all x2 -> x3, blocking collectives: 44.5 us -> 59.4 us  [exchanged(): return lax.all_to_all(copies, axis, 0, 0, tiled=True)]
    psum x1, blocking collectives: 64.8 us -> 50.6 us  [shards(): rows = lax.psum(rows.astype(jnp.bfloat16), 'seq_hi')]
    unnamed x32 -> x3, local copies, waits for them, and re-layouts: 14.1 us -> 0.77 us
    all_to_all x3 -> x2, waiting for transfers between devices: 37.3 us -> 29.6 us  [exchanged(): return lax.all_to_all(copies, axis, 0, 0, tiled=True)]
    all_to_all x3 -> x2, starting transfers between devices: 19.6 us -> 16.1 us  [exchanged(): return lax.all_to_all(copies, axis, 0, 0, tiled=True)]
    gather x1 -> x0, local copies, waits for them, and re-layouts: 3.28 us -> none  [shards(): table_rows = vocab_table[jnp.clip(local_ids, 0, vocab_rows - 1)]]
    pallas_call x1, Pallas kernels: 1.34 us -> 3.87 us  [shards(): call(project_kernel, shape((tp, 3 * ROWS, width), f32), [SM, SM, VM, PIPE...]
  transfers between devices with their start and end apart: 4 -> 3, of which waited for: 3 -> 2; matrix products, arithmetic and copies ran while one was open for 3% -> 1% of each run, Pallas kernels for 2% -> 4%
where the time goes in v3:
time: 204 us; the launch traced here: 203 us
  blocking collectives  126 us (62%)
  waiting for transfers between devices  29.7 us (15%)
  starting transfers between devices  16.2 us (8%)
  Pallas kernels  14.5 us (7%)
  between operations  14.2 us (7%)
    all_to_all x3, blocking collectives, exchanged(): return lax.all_to_all(copies, axis, 0, 0, tiled=True)  59.4 us
    psum x1, blocking collectives, shards(): rows = lax.psum(rows.astype(jnp.bfloat16), 'seq_hi')  50.6 us
    all_to_all x2, waiting for transfers between devices, exchanged(): return lax.all_to_all(copies, axis, 0, 0, tiled=True)  29.6 us
    psum x1, blocking collectives, shards(): sums = lax.psum(sums, 'seq_hi')  16.4 us
    all_to_all x2, starting transfers between devices, exchanged(): return lax.all_to_all(copies, axis, 0, 0, tiled=True)  16.1 us
    pallas_call x1, Pallas kernels, attention(): pl.pallas_call(attention_kernel, out_shape=jax.ShapeDtypeStruct(q.shape,...  4.73 us
  transfers between devices with their start and end apart: 3, of which 2 were waited for; matrix products, arithmetic and copies ran while one was open for 1% of the time, Pallas kernels for 4%

profile of v3, /device:TPU:40, one launch (start us, length us, event | category | flops | bytes accessed | tf_op | source)
XLA Modules:
  0.0 202.9 jit_solution(1301148498505967169)
XLA Ops:
  7.2 0.0 copy-start
  7.2 0.1 all-gather.2.cloned.1.call-start
  7.3 1.7 last_rows.1
  9.0 0.1 all-gather.2.cloned.1.call-update
  9.0 29.3 %all_to_all.25 = bf16[8,8,512]{2,1,0:T(8,128)(2,1)S(1)} all-to-all(bf16[8,8,512]{2,1,0:T(8,128)(2,1)S(1)} %get-tuple-element.10), channel_id=1, replica_groups=mesh['groups'=2,'seq_hi'=4,'seq_lo'=8,'tp_0'=4,'tp_1'=2] {'seq_lo'}, dimensions={0} | all-to-all | bytes 131072 | tf_op jit(solution)/shard_map/all_to_all | solution.py:43
  38.3 50.6 %psum.14.rows_ref = bf16[8,512]{1,0:T(8,128)(2,1)S(1)} all-reduce(bf16[8,512]{1,0:T(8,128)(2,1)S(1)} %reduce_sum.21), channel_id=1, replica_groups=mesh['groups'=2,'seq_hi'=4,'seq_lo'=8,'tp_0'=4,'tp_1'=2] {'seq_hi'}, use_global_device_ids=true, to_apply=%region_1.0 | all-reduce | flops 4096 | bytes 16384 | tf_op jit(solution)/shard_map/psum | solution.py:364
  88.9 1.4 partials.1
  90.3 14.6 %all_to_all.26.pieces_ref = bf16[8,64,128]{2,1,0:T(8,128)(2,1)S(1)} all-to-all(bf16[8,64,128]{2,1,0:T(8,128)(2,1)S(1)} %partials.1), channel_id=1, replica_groups=mesh['groups'=2,'seq_hi'=4,'seq_lo'=8,'tp_0'=4,'tp_1'=2] {'seq_lo'}, dimensions={0} | all-to-all | bytes 262144 | tf_op jit(solution)/shard_map/all_to_all | solution.py:43
  104.9 1.4 merge.1
  106.2 11.6 %all-to-all-start.2 = ((bf16[4,64,128]{2,1,0:T(8,128)(2,1)}), bf16[4,64,128]{2,1,0:T(8,128)(2,1)S(1)}, u32[]{:S(2)}, u32[]{:S(2)}) async-start(bf16[4,64,128]{2,1,0:T(8,128)(2,1)} %merge.1), calls=%async_computation.2 | async-start | bytes 131072 | tf_op jit(solution)/shard_map/all_to_all | solution.py:43
  117.8 0.8 copy.17.ids_ref
  118.6 22.0 %all-to-all-done.2.pieces_ref = bf16[4,64,128]{2,1,0:T(8,128)(2,1)S(1)} async-done(((bf16[4,64,128]{2,1,0:T(8,128)(2,1)}), bf16[4,64,128]{2,1,0:T(8,128)(2,1)S(1)}, u32[]{:S(2)}, u32[]{:S(2)}) %all-to-all-start.2) | async-done | bytes 65568 | tf_op jit(solution)/shard_map/all_to_all | solution.py:43
  140.6 3.9 %project.1 = f32[8,36,256]{2,1,0:T(8,128)} custom-call(s32[12,2]{1,0:T(8,128)S(1)} %copy.17.ids_ref, s32[1]{0:T(128)} %bitcast.1.tp_ref, bf16[4,64,128]{2,1,0:T(8,128)(2,1)S(1)} %all-to-all-done.2.pieces_ref, bf16[512,256]{1,0:T(8,128)(2,1)} %w_ref.1, bf16[8016,256]{1,0:T(8,128)(2,1)} %table_ref.1), custom_call_target="tpu_custom_call" | custom-call | tf_op jit(solution)/shard_map/project/pallas_call | solution.py:381
  144.5 4.5 %all-to-all-start.3 = ((f32[8,36,256]{2,1,0:T(8,128)}), f32[8,36,256]{2,1,0:T(8,128)S(1)}, u32[]{:S(2)}, u32[]{:S(2)}) async-start(f32[8,36,256]{2,1,0:T(8,128)} %project.1), calls=%async_computation.3 | async-start | bytes 655360 | tf_op jit(solution)/shard_map/all_to_all | solution.py:43
  149.0 0.0 copy-done
  149.0 0.6 reshape.17.gain_ref
  149.6 7.6 %all-to-all-done.3.pieces_ref = f32[8,36,256]{2,1,0:T(8,128)S(1)} async-done(((f32[8,36,256]{2,1,0:T(8,128)}), f32[8,36,256]{2,1,0:T(8,128)S(1)}, u32[]{:S(2)}, u32[]{:S(2)}) %all-to-all-start.3) | async-done | bytes 294944 | tf_op jit(solution)/shard_map/all_to_all | solution.py:43
  157.2 0.8 residual.1
  158.0 15.5 %all_to_all.27 = f32[8,12,128]{2,1,0:T(8,128)S(1)} all-to-all(f32[8,12,128]{2,1,0:T(8,128)S(1)} %get-tuple-element.11), channel_id=1, replica_groups=mesh['groups'=2,'seq_hi'=4,'seq_lo'=8,'tp_0'=4,'tp_1'=2] {'seq_lo'}, dimensions={0} | all-to-all | bytes 98304 | tf_op jit(solution)/shard_map/all_to_all | solution.py:43
  173.6 16.4 %psum.15.sums_ref = f32[12,128]{1,0:T(8,128)S(1)} all-reduce(f32[12,128]{1,0:T(8,128)S(1)} %reduce_sum.22), channel_id=1, replica_groups=mesh['groups'=2,'seq_hi'=4,'seq_lo'=8,'tp_0'=4,'tp_1'=2] {'seq_hi'}, use_global_device_ids=true, to_apply=%region_3.0 | all-reduce | flops 1536 | bytes 12288 | tf_op jit(solution)/shard_map/psum | solution.py:400
  189.9 0.7 verdict.1
  190.6 0.6 slice_reduce_fusion
  191.3 0.0 all-gather.2.cloned.1.call-done.kv_ref
  191.3 4.7 %attention.1 = bf16[256,512]{1,0:T(8,128)(2,1)} custom-call(s32[8]{0:T(128)} %lengths_ref.5, s32[1]{0:T(128)} %bitcast.seq_ref, bf16[256,512]{1,0:T(8,128)(2,1)} %q_ref.3, bf16[8192,256]{1,0:T(8,128)(2,1)} %all-gather.2.cloned.1.call-done.kv_ref), custom_call_target="tpu_custom_call" | custom-call | tf_op jit(solution)/shard_map/attention/pallas_call | solution.py:298
  (2 shorter events, 0.0 us)
Async XLA Ops:
  7.2 141.8 %copy-start = (bf16[256]{0:T(256)(128)(2,1)S(1)}, bf16[256]{0:T(256)(128)(2,1)}, u32[]{:S(2)}) copy-start(bf16[256]{0:T(256)(128)(2,1)} %param.23) | copy-start | bytes 1540
  7.2 184.1 %all-gather.2.cloned.1.call-start = ((), (), s32[]{:S(2)}) async-start(), calls=%async_computation.5 | async-start | bytes 4325376 | tf_op jit(solution)/shard_map/all_gather | solution.py:362
  106.2 34.4 %all-to-all-start.2 = ((bf16[4,64,128]{2,1,0:T(8,128)(2,1)}), bf16[4,64,128]{2,1,0:T(8,128)(2,1)S(1)}, u32[]{:S(2)}, u32[]{:S(2)}) async-start(bf16[4,64,128]{2,1,0:T(8,128)(2,1)} %merge.1), calls=%async_computation.2 | async-start | bytes 131072 | tf_op jit(solution)/shard_map/all_to_all | solution.py:43
  144.5 12.7 %all-to-all-start.3 = ((f32[8,36,256]{2,1,0:T(8,128)}), f32[8,36,256]{2,1,0:T(8,128)S(1)}, u32[]{:S(2)}, u32[]{:S(2)}) async-start(f32[8,36,256]{2,1,0:T(8,128)} %project.1), calls=%async_computation.3 | async-start | bytes 655360 | tf_op jit(solution)/shard_map/all_to_all | solution.py:43
Sparse Core Ops, SparseCore 0:
  10.7 171.2 all-gather.1

commit v4 on v3

--- a/solution.py
+++ b/solution.py
@@ -18,7 +18,7 @@
 GROUP = H // KVH
 LO = 8
 SLOT = 16
-KEY_BLOCK = 512
+KEY_BLOCK = 256
 TP = ("tp_0", "tp_1")
 SEQ = ("seq_hi", "seq_lo")
 
@@ -155,10 +155,8 @@
     put_partials(out_ref, *merged(pieces_ref))
 
 
-def project_kernel(
-    ids_ref, tp_ref, pieces_ref, w_ref, table_ref, out_ref, blocks, rows_scratch, sems
-):
-    vocab_rows = table_ref.shape[0]
+def table_kernel(ids_ref, tp_ref, after_ref, table_ref, out_ref, blocks, sems):
+    vocab_rows, width = table_ref.shape
     picks = []
     for c in range(2):
         for r in range(ROWS):
@@ -171,6 +169,15 @@
         rows = pl.ds(pl.multiple_of(block * TABLE_ROWS, TABLE_ROWS), TABLE_ROWS)
         copies.append(pltpu.make_async_copy(table_ref.at[rows], blocks.at[i], sems.at[i]))
         copies[-1].start()
+    for copy in copies:
+        copy.wait()
+    index = lax.broadcasted_iota(jnp.int32, (TABLE_ROWS, width), 0)
+    for i, (row, _) in enumerate(picks):
+        block = jnp.where(index == row, blocks[i].astype(jnp.float32), 0.0)
+        out_ref[i : i + 1, :] = jnp.sum(block, axis=0, keepdims=True)
+
+
+def project_kernel(pieces_ref, w_ref, table_ref, out_ref):
     sums, _, total = merged(pieces_ref)
     rows = sums / total
     partial = jnp.zeros((SLOT, w_ref.shape[1]), jnp.float32)
@@ -180,45 +187,45 @@
             w_ref[g * HD : (g + 1) * HD, :],
             preferred_element_type=jnp.float32,
         )
-    for copy in copies:
-        copy.wait()
-    index = lax.broadcasted_iota(jnp.int32, (TABLE_ROWS, w_ref.shape[1]), 0)
-    for i, (row, _) in enumerate(picks):
-        block = jnp.where(index == row, blocks[i].astype(jnp.float32), 0.0)
-        rows_scratch[i : i + 1, :] = jnp.sum(block, axis=0, keepdims=True)
     for c in range(out_ref.shape[0]):
         out_ref[c, :ROWS] = partial[:ROWS]
-        out_ref[c, ROWS : 3 * ROWS] = rows_scratch[...]
+        out_ref[c, ROWS:] = table_ref[...]
 
 
 def residual_kernel(pieces_ref, stream_ref, gain_ref, gained_ref, sums_ref):
     total = pieces_ref[0]
     for c in range(1, pieces_ref.shape[0]):
         total = total + pieces_ref[c]
+    table = total[ROWS:]
     residual = total[:ROWS] + stream_ref[...].astype(jnp.float32)
     gained = residual * gain_ref[...].astype(jnp.float32)
     gained_ref[...] = gained
     squares = jnp.sum(residual * residual, axis=1, keepdims=True)
-    first = jnp.sum(gained * total[ROWS : 2 * ROWS], axis=1, keepdims=True)
-    second = jnp.sum(gained * total[2 * ROWS : 3 * ROWS], axis=1, keepdims=True)
+    first = jnp.sum(gained * table[:ROWS], axis=1, keepdims=True)
+    second = jnp.sum(gained * table[ROWS:], axis=1, keepdims=True)
     lane = lax.broadcasted_iota(jnp.int32, (ROWS, HD), 1)
     packed = jnp.where(lane == 0, squares, jnp.where(lane == 1, first, second))
+    packed = jnp.concatenate([packed, jnp.zeros((HD - ROWS, HD), jnp.float32)], axis=0)
+    packed = jnp.transpose(packed)[:8]
     for c in range(sums_ref.shape[0]):
         sums_ref[c] = packed
 
 
 def verdict_kernel(sums_ref, gained_ref, hidden_ref, win_ref):
-    inv_rms = 1.0 / jnp.sqrt(sums_ref[:, 0:1] / D + norm_eps)
+    sums = jnp.transpose(sums_ref[...])[:ROWS]
+    inv_rms = 1.0 / jnp.sqrt(sums[:, 0:1] / D + norm_eps)
     hidden_ref[...] = (gained_ref[...] * inv_rms).astype(hidden_ref.dtype)
-    logits = sums_ref[...] * inv_rms
-    win = 1.0 / (1.0 + jnp.exp(logits[:, 2:3] - logits[:, 1:2]))
+    win = 1.0 / (1.0 + jnp.exp((sums[:, 2:3] - sums[:, 1:2]) * inv_rms))
     win_ref[...] = jnp.broadcast_to(win, win_ref.shape)
 
 
 def attention_kernel(
-    lengths_ref, seq_ref, q_ref, kv_ref, out_ref, kv_buf, top_ref, total_ref, sum_ref, sems
+    lengths_ref, seq_ref, q_hbm, kv_ref, out_ref, q_ref, kv_buf, top_ref, total_ref, sum_ref,
+    q_sem, sems,
 ):
     tokens = q_ref.shape[0]
+    q_copy = pltpu.make_async_copy(q_hbm, q_ref, q_sem)
+    q_copy.start()
     first = seq_ref[0] * tokens
     ends = ends_of(lengths_ref)
     start_first = jnp.int32(0)
@@ -286,6 +293,7 @@
 
         return carry
 
+    q_copy.wait()
     lax.fori_loop(low, high, step, 0)
     for g in range(GROUP):
         total = jnp.sum(total_ref[g], axis=0, keepdims=True)
@@ -298,13 +306,15 @@
     return pl.pallas_call(
         attention_kernel,
         out_shape=jax.ShapeDtypeStruct(q.shape, q.dtype),
-        in_specs=[SM, SM, PIPE, HB],
+        in_specs=[SM, SM, HB, HB],
         out_specs=VM,
         scratch_shapes=[
+            pltpu.VMEM(q.shape, q.dtype),
             pltpu.VMEM(kv.shape, kv.dtype),
             pltpu.VMEM((GROUP, 1, tokens), jnp.float32),
             pltpu.VMEM((GROUP, 8, tokens), jnp.float32),
             pltpu.VMEM((GROUP, HD, tokens), jnp.float32),
+            pltpu.SemaphoreType.DMA,
             pltpu.SemaphoreType.DMA((kv.shape[0] // KEY_BLOCK,)),
         ],
         compiler_params=pltpu.CompilerParams(vmem_limit_bytes=24 * 1024 * 1024),
@@ -374,25 +384,29 @@
         held(v_prefill), held(cache_k), held(cache_v),
     )
     partials = exchanged(partials, "seq_lo")
-    partials = call(merge_kernel, shape((hi, GROUP * SLOT, HD), jnp.bfloat16), [VM], "merge")(partials)
-    partials = exchanged(partials, "seq_hi")
+    merged_rows = call(merge_kernel, shape((hi, GROUP * SLOT, HD), jnp.bfloat16), [VM], "merge")(
+        partials
+    )
+    partials = exchanged(merged_rows, "seq_hi")
 
     tp_index = lax.axis_index(TP).astype(jnp.int32).reshape(1)
-    pieces = call(
-        project_kernel,
-        shape((tp, 3 * ROWS, width), f32),
-        [SM, SM, VM, PIPE, HB],
-        "project",
+    table_rows = call(
+        table_kernel,
+        shape((2 * ROWS, width), f32),
+        [SM, SM, HB, HB],
+        "table",
         [
             pltpu.VMEM((2 * ROWS, TABLE_ROWS, width), jnp.bfloat16),
-            pltpu.VMEM((2 * ROWS, width), f32),
             pltpu.SemaphoreType.DMA((2 * ROWS,)),
         ],
-    )(verdict_ids, tp_index, partials, held(out_weight), held(vocab_table))
+    )(verdict_ids, tp_index, merged_rows, held(vocab_table))
+    pieces = call(
+        project_kernel, shape((tp, 3 * ROWS, width), f32), [VM, PIPE, VM], "project"
+    )(partials, held(out_weight), table_rows)
     pieces = exchanged(pieces, TP)
     gained, sums = call(
         residual_kernel,
-        (shape((ROWS, width), f32), shape((lo, ROWS, HD), f32)),
+        (shape((ROWS, width), f32), shape((lo, 8, HD), f32)),
         [VM, PIPE, PIPE],
         "residual",
     )(pieces, held(stream), held(norm_gain.reshape(1, width)))

time: 204 us -> 201 us (0.985)
  waiting for transfers between devices: 29.7 us -> 27.3 us
    all_to_all x2, waiting for transfers between devices: 29.6 us -> 27.3 us  [exchanged(): return lax.all_to_all(copies, axis, 0, 0, tiled=True)]
    pallas_call x2 -> x3, Pallas kernels: 4.67 us -> 5.5 us  [the longest x1 2.37 us: shards(): call(table_kernel, shape((2 * ROWS, width), f32), [SM, SM, HB, HB], 'tabl...]
where the time goes in v4:
time: 201 us; the launch traced here: 200 us
  blocking collectives  126 us (63%)
  waiting for transfers between devices  27.3 us (14%)
  starting transfers between devices  16.5 us (8%)
  Pallas kernels  14.8 us (7%)
  between operations  14.1 us (7%)
    all_to_all x3, blocking collectives, exchanged(): return lax.all_to_all(copies, axis, 0, 0, tiled=True)  59.1 us
    psum x1, blocking collectives, shards(): rows = lax.psum(rows.astype(jnp.bfloat16), 'seq_hi')  50.6 us
    all_to_all x2, waiting for transfers between devices, exchanged(): return lax.all_to_all(copies, axis, 0, 0, tiled=True)  27.3 us
    all_to_all x2, starting transfers between devices, exchanged(): return lax.all_to_all(copies, axis, 0, 0, tiled=True)  16.4 us
    psum x1, blocking collectives, shards(): sums = lax.psum(sums, 'seq_hi')  16.1 us
    pallas_call x1, Pallas kernels, attention(): pl.pallas_call(attention_kernel, out_shape=jax.ShapeDtypeStruct(q.shape,...  4.08 us
  transfers between devices with their start and end apart: 3, of which 2 were waited for; matrix products, arithmetic and copies ran while one was open for 1% of the time, Pallas kernels for 4%

profile of v4, /device:TPU:40, one launch (start us, length us, event | category | flops | bytes accessed | tf_op | source)
XLA Modules:
  0.0 200.5 jit_solution(2357557492347076356)
XLA Ops:
  7.2 0.0 copy-start
  7.2 0.1 all-gather.2.cloned.1.call-start
  7.3 1.7 last_rows.1
  9.0 0.1 all-gather.2.cloned.1.call-update
  9.0 29.3 %all_to_all.25 = bf16[8,8,512]{2,1,0:T(8,128)(2,1)S(1)} all-to-all(bf16[8,8,512]{2,1,0:T(8,128)(2,1)S(1)} %get-tuple-element.10), channel_id=1, replica_groups=mesh['groups'=2,'seq_hi'=4,'seq_lo'=8,'tp_0'=4,'tp_1'=2] {'seq_lo'}, dimensions={0} | all-to-all | bytes 131072 | tf_op jit(solution)/shard_map/all_to_all | solution.py:43
  38.3 50.6 %psum.14.rows_ref = bf16[8,512]{1,0:T(8,128)(2,1)S(1)} all-reduce(bf16[8,512]{1,0:T(8,128)(2,1)S(1)} %reduce_sum.21), channel_id=1, replica_groups=mesh['groups'=2,'seq_hi'=4,'seq_lo'=8,'tp_0'=4,'tp_1'=2] {'seq_hi'}, use_global_device_ids=true, to_apply=%region_1.0 | all-reduce | flops 4096 | bytes 16384 | tf_op jit(solution)/shard_map/psum | solution.py:374
  88.9 1.4 partials.1
  90.3 14.6 %all_to_all.26.pieces_ref = bf16[8,64,128]{2,1,0:T(8,128)(2,1)S(1)} all-to-all(bf16[8,64,128]{2,1,0:T(8,128)(2,1)S(1)} %partials.1), channel_id=1, replica_groups=mesh['groups'=2,'seq_hi'=4,'seq_lo'=8,'tp_0'=4,'tp_1'=2] {'seq_lo'}, dimensions={0} | all-to-all | bytes 262144 | tf_op jit(solution)/shard_map/all_to_all | solution.py:43
  104.9 1.4 merge.1.after_ref
  106.2 11.6 %all-to-all-start.2 = ((bf16[4,64,128]{2,1,0:T(8,128)(2,1)}), bf16[4,64,128]{2,1,0:T(8,128)(2,1)S(1)}, u32[]{:S(2)}, u32[]{:S(2)}) async-start(bf16[4,64,128]{2,1,0:T(8,128)(2,1)} %merge.1.after_ref), calls=%async_computation.2 | async-start | bytes 131072 | tf_op jit(solution)/shard_map/all_to_all | solution.py:43
  117.8 0.8 copy.17.ids_ref
  118.6 2.4 %table.1.table_ref = f32[24,256]{1,0:T(8,128)S(1)} custom-call(s32[12,2]{1,0:T(8,128)S(1)} %copy.17.ids_ref, s32[1]{0:T(128)} %bitcast.1.tp_ref, bf16[4,64,128]{2,1,0:T(8,128)(2,1)} %merge.1.after_ref, bf16[8016,256]{1,0:T(8,128)(2,1)} %table_ref.1), custom_call_target="tpu_custom_call" | custom-call | tf_op jit(solution)/shard_map/table/pallas_call | solution.py:393
  121.0 19.6 %all-to-all-done.2.pieces_ref = bf16[4,64,128]{2,1,0:T(8,128)(2,1)S(1)} async-done(((bf16[4,64,128]{2,1,0:T(8,128)(2,1)}), bf16[4,64,128]{2,1,0:T(8,128)(2,1)S(1)}, u32[]{:S(2)}, u32[]{:S(2)}) %all-to-all-start.2) | async-done | bytes 65568 | tf_op jit(solution)/shard_map/all_to_all | solution.py:43
  140.6 2.3 %project.1 = f32[8,36,256]{2,1,0:T(8,128)} custom-call(bf16[4,64,128]{2,1,0:T(8,128)(2,1)S(1)} %all-to-all-done.2.pieces_ref, bf16[512,256]{1,0:T(8,128)(2,1)} %w_ref.1, f32[24,256]{1,0:T(8,128)S(1)} %table.1.table_ref), custom_call_target="tpu_custom_call" | custom-call | tf_op jit(solution)/shard_map/project/pallas_call | solution.py:403
  142.9 4.8 %all-to-all-start.3 = ((f32[8,36,256]{2,1,0:T(8,128)}), f32[8,36,256]{2,1,0:T(8,128)S(1)}, u32[]{:S(2)}, u32[]{:S(2)}) async-start(f32[8,36,256]{2,1,0:T(8,128)} %project.1), calls=%async_computation.3 | async-start | bytes 655360 | tf_op jit(solution)/shard_map/all_to_all | solution.py:43
  147.7 0.0 copy-done
  147.7 0.6 reshape.17.gain_ref
  148.2 7.6 %all-to-all-done.3.pieces_ref = f32[8,36,256]{2,1,0:T(8,128)S(1)} async-done(((f32[8,36,256]{2,1,0:T(8,128)}), f32[8,36,256]{2,1,0:T(8,128)S(1)}, u32[]{:S(2)}, u32[]{:S(2)}) %all-to-all-start.3) | async-done | bytes 294944 | tf_op jit(solution)/shard_map/all_to_all | solution.py:43
  155.9 0.9 residual.1
  156.7 15.2 %all_to_all.27 = f32[8,8,128]{2,1,0:T(8,128)S(1)} all-to-all(f32[8,8,128]{2,1,0:T(8,128)S(1)} %get-tuple-element.11), channel_id=1, replica_groups=mesh['groups'=2,'seq_hi'=4,'seq_lo'=8,'tp_0'=4,'tp_1'=2] {'seq_lo'}, dimensions={0} | all-to-all | bytes 65536 | tf_op jit(solution)/shard_map/all_to_all | solution.py:43
  172.0 16.1 %psum.15.sums_ref = f32[8,128]{1,0:T(8,128)S(1)} all-reduce(f32[8,128]{1,0:T(8,128)S(1)} %reduce_sum.22), channel_id=1, replica_groups=mesh['groups'=2,'seq_hi'=4,'seq_lo'=8,'tp_0'=4,'tp_1'=2] {'seq_hi'}, use_global_device_ids=true, to_apply=%region_3.0 | all-reduce | flops 1024 | bytes 8192 | tf_op jit(solution)/shard_map/psum | solution.py:414
  188.1 0.8 verdict.1
  188.9 0.6 slice_reduce_fusion
  189.5 0.0 all-gather.2.cloned.1.call-done.kv_ref
  189.5 4.1 %attention.1 = bf16[256,512]{1,0:T(8,128)(2,1)} custom-call(s32[8]{0:T(128)} %lengths_ref.5, s32[1]{0:T(128)} %bitcast.seq_ref, bf16[256,512]{1,0:T(8,128)(2,1)} %q_hbm.1, bf16[8192,256]{1,0:T(8,128)(2,1)} %all-gather.2.cloned.1.call-done.kv_ref), custom_call_target="tpu_custom_call" | custom-call | tf_op jit(solution)/shard_map/attention/pallas_call | solution.py:306
  (2 shorter events, 0.0 us)
Async XLA Ops:
  7.2 140.5 %copy-start = (bf16[256]{0:T(256)(128)(2,1)S(1)}, bf16[256]{0:T(256)(128)(2,1)}, u32[]{:S(2)}) copy-start(bf16[256]{0:T(256)(128)(2,1)} %param.23) | copy-start | bytes 1540
  7.2 182.3 %all-gather.2.cloned.1.call-start = ((), (), s32[]{:S(2)}) async-start(), calls=%async_computation.5 | async-start | bytes 4325376 | tf_op jit(solution)/shard_map/all_gather | solution.py:372
  106.2 34.4 %all-to-all-start.2 = ((bf16[4,64,128]{2,1,0:T(8,128)(2,1)}), bf16[4,64,128]{2,1,0:T(8,128)(2,1)S(1)}, u32[]{:S(2)}, u32[]{:S(2)}) async-start(bf16[4,64,128]{2,1,0:T(8,128)(2,1)} %merge.1.after_ref), calls=%async_computation.2 | async-start | bytes 131072 | tf_op jit(solution)/shard_map/all_to_all | solution.py:43
  142.9 13.0 %all-to-all-start.3 = ((f32[8,36,256]{2,1,0:T(8,128)}), f32[8,36,256]{2,1,0:T(8,128)S(1)}, u32[]{:S(2)}, u32[]{:S(2)}) async-start(f32[8,36,256]{2,1,0:T(8,128)} %project.1), calls=%async_computation.3 | async-start | bytes 655360 | tf_op jit(solution)/shard_map/all_to_all | solution.py:43
Sparse Core Ops, SparseCore 0:
  10.7 170.7 all-gather.1

commit v5 on v4

--- a/solution.py
+++ b/solution.py
@@ -18,6 +18,8 @@
 GROUP = H // KVH
 LO = 8
 SLOT = 16
+PART = 8
+HELD = 6
 KEY_BLOCK = 256
 TP = ("tp_0", "tp_1")
 SEQ = ("seq_hi", "seq_lo")
@@ -67,21 +69,66 @@
         out_ref[c] = picked[:PAIRS].astype(out_ref.dtype)
 
 
+def table_copies(ids_ref, tp_ref, table_ref, blocks, sems):
+    vocab_rows = table_ref.shape[0]
+    copies, places = [], []
+    for c in range(2):
+        for r in range(ROWS):
+            local = ids_ref[r, c] - tp_ref[0] * vocab_rows
+            inside = (local >= 0) & (local < vocab_rows)
+            local = jnp.clip(local, 0, vocab_rows - 1)
+            places.append(jnp.where(inside, local % TABLE_ROWS, -1))
+            first = pl.multiple_of(local // TABLE_ROWS * TABLE_ROWS, TABLE_ROWS)
+            i = len(copies)
+            copies.append(
+                pltpu.make_async_copy(
+                    table_ref.at[pl.ds(first, TABLE_ROWS)], blocks.at[i], sems.at[i]
+                )
+            )
+    return copies, places
+
+
+def spread(columns):
+    row = lax.broadcasted_iota(jnp.int32, (PART, HD), 0)
+    lane = lax.broadcasted_iota(jnp.int32, (PART, HD), 1)
+    line = jnp.zeros((PART, HD), jnp.float32)
+    for j, column in enumerate(columns):
+        line = jnp.where(lane == j * PART + row, column, line)
+    return jnp.sum(line, axis=0, keepdims=True)
+
+
+def gathered(line, first, count):
+    row = lax.broadcasted_iota(jnp.int32, (PART, HD), 0)
+    lane = lax.broadcasted_iota(jnp.int32, (PART, HD), 1)
+    wanted = (lane % PART == row) & (lane >= first * PART) & (lane < (first + count) * PART)
+    return jnp.sum(jnp.where(wanted, line, 0.0), axis=1, keepdims=True)
+
+
+def three_parts(x):
+    high = x.astype(jnp.bfloat16).astype(jnp.float32)
+    middle = (x - high).astype(jnp.bfloat16).astype(jnp.float32)
+    return high, middle, x - high - middle
+
+
 def partials_kernel(
-    lengths_ref, cache_lengths_ref, seq_ref, rows_ref, qd_ref, k_ref, v_ref, ck_ref, cv_ref,
-    out_ref, q_scratch,
+    lengths_ref, cache_lengths_ref, seq_ref, ids_ref, tp_ref, rows_ref, qd_ref, k_ref, v_ref,
+    ck_ref, cv_ref, table_ref, out_ref, picked_ref, q_scratch, blocks, sems,
 ):
+    copies, places = table_copies(ids_ref, tp_ref, table_ref, blocks, sems)
+    for copy in copies:
+        copy.start()
     tokens = k_ref.shape[0]
     cache_count = ck_ref.shape[1]
     ends = ends_of(lengths_ref)
     q_scratch[...] = jnp.zeros_like(q_scratch)
     for g in range(GROUP):
-        q_scratch[g * SLOT : g * SLOT + PAIRS, :] = rows_ref[
-            :, g * HD : (g + 1) * HD
-        ].astype(jnp.float32)
-        q_scratch[g * SLOT + PAIRS : g * SLOT + ROWS, :] = qd_ref[
-            :, g * HD : (g + 1) * HD
-        ].astype(jnp.float32)
+        columns = slice(g * HD, (g + 1) * HD)
+        base, next_part = g * SLOT, g * SLOT + PART
+        both = PAIRS - HELD
+        pair_rows = rows_ref[:, columns].astype(jnp.float32)
+        q_scratch[base : base + HELD, :] = pair_rows[:HELD]
+        q_scratch[next_part : next_part + both, :] = pair_rows[HELD:]
+        q_scratch[next_part + both : next_part + HELD, :] = qd_ref[:, columns].astype(jnp.float32)
     queries = q_scratch[...].astype(jnp.bfloat16)
     keys = jnp.concatenate([k_ref[...], ck_ref[...].reshape(PROMPTS * cache_count, HD)], axis=0)
     values = jnp.concatenate([v_ref[...], cv_ref[...].reshape(PROMPTS * cache_count, HD)], axis=0)
@@ -99,96 +146,70 @@
         cache_pos = lane - first + seq_ref[0] * cache_count
         label = jnp.where(cache_pos < cache_lengths_ref[p], PAIRS + p, -1)
         owner = jnp.where(mine, label, owner)
-    item = lax.broadcasted_iota(jnp.int32, (GROUP * SLOT, count), 0) % SLOT
+    row = lax.broadcasted_iota(jnp.int32, (GROUP * SLOT, count), 0)
+    item = jnp.where(row % PART < HELD, row % PART + row % SLOT // PART * HELD, -2)
     visible = item == owner
     scores = jnp.where(visible, scores, masked_score)
     top = jnp.max(scores, axis=1, keepdims=True)
     terms = jnp.where(visible, jnp.exp(scores - top), 0.0)
     total = jnp.sum(terms, axis=1, keepdims=True)
     sums = jnp.dot(terms.astype(jnp.bfloat16), values, preferred_element_type=jnp.float32)
-    put_partials(out_ref, sums, top, total)
-
-
-def three_parts(x):
-    high = x.astype(jnp.bfloat16).astype(jnp.float32)
-    middle = (x - high).astype(jnp.bfloat16).astype(jnp.float32)
-    return high, middle, x - high - middle
-
-
-def put_partials(out_ref, sums, top, total):
-    across = (GROUP * SLOT, HD)
-    row = lax.broadcasted_iota(jnp.int32, across, 0)
-    packed = sums
-    for first, column in ((ROWS, top), (SLOT + ROWS, total)):
-        lanes = jnp.transpose(jnp.broadcast_to(column, across))[:1]
-        lanes = jnp.concatenate([lanes, jnp.zeros_like(lanes)], axis=1)
-        for j, part in enumerate(three_parts(lanes)):
-            packed = jnp.where(row == first + j, part, packed)
-    packed = packed.astype(out_ref.dtype)
+    place = lax.broadcasted_iota(jnp.int32, (PART, HD), 0)
     for c in range(out_ref.shape[0]):
-        out_ref[c] = packed
-
-
-def merged(pieces_ref):
-    count = pieces_ref.shape[0]
-    pieces = [pieces_ref[c].astype(jnp.float32) for c in range(count)]
-
-    def columns(first):
-        lines = [
-            jnp.sum(piece[first : first + 3], axis=0, keepdims=True) for piece in pieces
-        ] + [jnp.zeros((8 - count % 8, HD), jnp.float32)] * (count % 8 > 0)
-        turned = jnp.transpose(jnp.concatenate(lines, axis=0))[: GROUP * SLOT]
-        return [turned[:, c : c + 1] for c in range(count)]
-
-    tops, totals = columns(ROWS), columns(SLOT + ROWS)
+        rows = slice(c * PART, (c + 1) * PART)
+        out_ref[c] = jnp.where(place == HELD, spread((top[rows], total[rows])), sums[rows])
+    for copy in copies:
+        copy.wait()
+    index = lax.broadcasted_iota(jnp.int32, blocks.shape[1:], 0)
+    for i, wanted in enumerate(places):
+        block = jnp.where(index == wanted, blocks[i].astype(jnp.float32), 0.0)
+        picked_ref[i : i + 1, :] = jnp.sum(block, axis=0, keepdims=True)
+
+
+def merged(pieces, parts):
+    tops = [gathered(piece[HELD : HELD + 1], 0, parts) for piece in pieces]
+    totals = [gathered(piece[HELD : HELD + 1], parts, parts) for piece in pieces]
     top = functools.reduce(jnp.maximum, tops)
     total = jnp.zeros_like(top)
-    sums = jnp.zeros((GROUP * SLOT, HD), jnp.float32)
-    for c in range(count):
-        scale = jnp.exp(tops[c] - top)
-        total = total + totals[c] * scale
-        sums = sums + pieces[c] * scale
+    sums = jnp.zeros((PART, HD), jnp.float32)
+    for piece, piece_top, piece_total in zip(pieces, tops, totals):
+        scale = jnp.exp(piece_top - top)
+        total = total + piece_total * scale
+        sums = sums + piece * scale
     return sums, top, total
 
 
-def merge_kernel(pieces_ref, out_ref):
-    put_partials(out_ref, *merged(pieces_ref))
-
-
-def table_kernel(ids_ref, tp_ref, after_ref, table_ref, out_ref, blocks, sems):
-    vocab_rows, width = table_ref.shape
-    picks = []
-    for c in range(2):
-        for r in range(ROWS):
-            local = ids_ref[r, c] - tp_ref[0] * vocab_rows
-            inside = (local >= 0) & (local < vocab_rows)
-            local = jnp.clip(local, 0, vocab_rows - 1)
-            picks.append((jnp.where(inside, local % TABLE_ROWS, -1), local // TABLE_ROWS))
-    copies = []
-    for i, (_, block) in enumerate(picks):
-        rows = pl.ds(pl.multiple_of(block * TABLE_ROWS, TABLE_ROWS), TABLE_ROWS)
-        copies.append(pltpu.make_async_copy(table_ref.at[rows], blocks.at[i], sems.at[i]))
-        copies[-1].start()
-    for copy in copies:
-        copy.wait()
-    index = lax.broadcasted_iota(jnp.int32, (TABLE_ROWS, width), 0)
-    for i, (row, _) in enumerate(picks):
-        block = jnp.where(index == row, blocks[i].astype(jnp.float32), 0.0)
-        out_ref[i : i + 1, :] = jnp.sum(block, axis=0, keepdims=True)
-
-
-def project_kernel(pieces_ref, w_ref, table_ref, out_ref):
-    sums, _, total = merged(pieces_ref)
-    rows = sums / total
+def merge_kernel(hi_ref, pieces_ref, out_ref):
+    sums, top, total = merged([pieces_ref[c] for c in range(pieces_ref.shape[0])], 1)
+    row = lax.broadcasted_iota(jnp.int32, (PART, HD), 0)
+    line = spread(three_parts(top) + three_parts(total))
+    block = jnp.where(row == HELD, line, jnp.where(row < HELD, sums, 0.0))
+    slots = [jnp.where(hi_ref[0] == k, block, 0.0) for k in range(out_ref.shape[0] // PART)]
+    out_ref[...] = jnp.concatenate(slots, axis=0).astype(out_ref.dtype)
+
+
+def finish_kernel(slots_ref, out_ref):
+    slots = slots_ref[...].astype(jnp.float32)
+    count = slots_ref.shape[0] // PART
+    sums, _, total = merged([slots[k * PART : (k + 1) * PART] for k in range(count)], 3)
+    row = lax.broadcasted_iota(jnp.int32, (PART, HD), 0)
+    rows = jnp.where(row < HELD, sums / total, 0.0).astype(out_ref.dtype)
+    for c in range(out_ref.shape[0]):
+        out_ref[c] = rows
+
+
+def project_kernel(parts_ref, w_ref, table_ref, out_ref):
     partial = jnp.zeros((SLOT, w_ref.shape[1]), jnp.float32)
     for g in range(GROUP):
+        rows = [parts_ref[2 * g + j].astype(jnp.float32) for j in range(2)]
         partial = partial + jnp.dot(
-            rows[g * SLOT : (g + 1) * SLOT].astype(jnp.bfloat16),
+            jnp.concatenate(rows, axis=0).astype(jnp.bfloat16),
             w_ref[g * HD : (g + 1) * HD, :],
             preferred_element_type=jnp.float32,
         )
     for c in range(out_ref.shape[0]):
-        out_ref[c, :ROWS] = partial[:ROWS]
+        out_ref[c, :HELD] = partial[:HELD]
+        out_ref[c, HELD:ROWS] = partial[PART : PART + HELD]
         out_ref[c, ROWS:] = table_ref[...]
 
 
@@ -215,8 +236,10 @@
     sums = jnp.transpose(sums_ref[...])[:ROWS]
     inv_rms = 1.0 / jnp.sqrt(sums[:, 0:1] / D + norm_eps)
     hidden_ref[...] = (gained_ref[...] * inv_rms).astype(hidden_ref.dtype)
-    win = 1.0 / (1.0 + jnp.exp((sums[:, 2:3] - sums[:, 1:2]) * inv_rms))
-    win_ref[...] = jnp.broadcast_to(win, win_ref.shape)
+    lines = sums_ref[...]
+    inv_rms = 1.0 / jnp.sqrt(lines[0:1] / D + norm_eps)
+    win = 1.0 / (1.0 + jnp.exp((lines[2:3] - lines[1:2]) * inv_rms))
+    win_ref[...] = win[0, :ROWS]
 
 
 def attention_kernel(
@@ -373,36 +396,31 @@
     rows = jnp.sum(exchanged(picked, "seq_lo").astype(f32), axis=0)
     rows = lax.psum(rows.astype(jnp.bfloat16), "seq_hi")
 
-    partials = call(
+    tp_index = lax.axis_index(TP).astype(jnp.int32).reshape(1)
+    hi_index = lax.axis_index("seq_hi").astype(jnp.int32).reshape(1)
+    partials, table_rows = call(
         partials_kernel,
-        shape((lo, GROUP * SLOT, HD), jnp.bfloat16),
-        [SM, SM, SM, VM] + [PIPE] * 5,
+        (shape((lo, PART, HD), f32), shape((2 * ROWS, width), f32)),
+        [SM] * 5 + [VM] + [PIPE] * 5 + [HB],
         "partials",
-        [pltpu.VMEM((GROUP * SLOT, HD), f32)],
-    )(
-        pair_lengths, cache_lengths, seq_index, rows, held(q_decode), held(k_prefill),
-        held(v_prefill), held(cache_k), held(cache_v),
-    )
-    partials = exchanged(partials, "seq_lo")
-    merged_rows = call(merge_kernel, shape((hi, GROUP * SLOT, HD), jnp.bfloat16), [VM], "merge")(
-        partials
-    )
-    partials = exchanged(merged_rows, "seq_hi")
-
-    tp_index = lax.axis_index(TP).astype(jnp.int32).reshape(1)
-    table_rows = call(
-        table_kernel,
-        shape((2 * ROWS, width), f32),
-        [SM, SM, HB, HB],
-        "table",
         [
+            pltpu.VMEM((GROUP * SLOT, HD), f32),
             pltpu.VMEM((2 * ROWS, TABLE_ROWS, width), jnp.bfloat16),
             pltpu.SemaphoreType.DMA((2 * ROWS,)),
         ],
-    )(verdict_ids, tp_index, merged_rows, held(vocab_table))
+    )(
+        pair_lengths, cache_lengths, seq_index, verdict_ids, tp_index, rows, held(q_decode),
+        held(k_prefill), held(v_prefill), held(cache_k), held(cache_v), held(vocab_table),
+    )
+    slots = call(merge_kernel, shape((hi * PART, HD), jnp.bfloat16), [SM, VM], "merge")(
+        hi_index, exchanged(partials, "seq_lo")
+    )
+    slots = lax.psum(slots, "seq_hi")
+    parts = call(finish_kernel, shape((lo, PART, HD), jnp.bfloat16), [VM], "finish")(slots)
+    parts = exchanged(parts, "seq_lo")
     pieces = call(
         project_kernel, shape((tp, 3 * ROWS, width), f32), [VM, PIPE, VM], "project"
-    )(partials, held(out_weight), table_rows)
+    )(parts, held(out_weight), table_rows)
     pieces = exchanged(pieces, TP)
     gained, sums = call(
         residual_kernel,
@@ -414,13 +432,13 @@
     sums = lax.psum(sums, "seq_hi")
     verdict_hidden, win = call(
         verdict_kernel,
-        (shape((ROWS, width), jnp.bfloat16), shape((ROWS, HD), f32)),
+        (shape((ROWS, width), jnp.bfloat16), shape((ROWS,), f32)),
         [VM, VM],
         "verdict",
     )(sums, gained)
 
     attended = attention(pair_lengths, seq_index, q_prefill, kv)
-    return (attended, verdict_hidden, win[:, 0])
+    return (attended, verdict_hidden, win)
 
 
 def solution(mesh):

time: 201 us -> 202 us (level)
  waiting for transfers between devices: 27.3 us -> 17.8 us
  starting transfers between devices: 16.5 us -> 23.1 us
  blocking collectives: 126 us -> 132 us
  Pallas kernels: 14.8 us -> 12.4 us
    all_to_all x3, blocking collectives: 59.1 us -> 39.2 us  [exchanged(): return lax.all_to_all(copies, axis, 0, 0, tiled=True)]
    psum x0 -> x1, blocking collectives: none -> 16.3 us  [shards(): slots = lax.psum(slots, 'seq_hi')]
    psum x1, blocking collectives: 16.1 us -> 26.4 us  [shards(): sums = lax.psum(sums, 'seq_hi')]
    all_to_all x2, waiting for transfers between devices: 27.3 us -> 17.8 us  [exchanged(): return lax.all_to_all(copies, axis, 0, 0, tiled=True)]
    all_to_all x2, starting transfers between devices: 16.4 us -> 23 us  [exchanged(): return lax.all_to_all(copies, axis, 0, 0, tiled=True)]
    pallas_call x4, Pallas kernels: 5.87 us -> 3.79 us  [the longest x1 2.82 us: shards(): call(partials_kernel, (shape((lo, PART, HD), f32), shape((2 * ROWS, width...]
  transfers between devices with their start and end apart: 3 -> 3, of which waited for: 2 -> 2; matrix products, arithmetic and copies ran while one was open for 1% -> 1% of each run, Pallas kernels for 4% -> 3%
where the time goes in v5:
time: 202 us; the launch traced here: 201 us
  blocking collectives  132 us (65%)
  starting transfers between devices  23.1 us (11%)
  waiting for transfers between devices  17.8 us (9%)
  between operations  14.2 us (7%)
  Pallas kernels  12.4 us (6%)
    psum x1, blocking collectives, shards(): rows = lax.psum(rows.astype(jnp.bfloat16), 'seq_hi')  50.3 us
    all_to_all x3, blocking collectives, exchanged(): return lax.all_to_all(copies, axis, 0, 0, tiled=True)  39.2 us
    psum x1, blocking collectives, shards(): sums = lax.psum(sums, 'seq_hi')  26.4 us
    all_to_all x2, starting transfers between devices, exchanged(): return lax.all_to_all(copies, axis, 0, 0, tiled=True)  23 us
    all_to_all x2, waiting for transfers between devices, exchanged(): return lax.all_to_all(copies, axis, 0, 0, tiled=True)  17.8 us
    psum x1, blocking collectives, shards(): slots = lax.psum(slots, 'seq_hi')  16.3 us
    pallas_call x1, Pallas kernels, attention(): pl.pallas_call(attention_kernel, out_shape=jax.ShapeDtypeStruct(q.shape,...  4.08 us
  transfers between devices with their start and end apart: 3, of which 2 were waited for; matrix products, arithmetic and copies ran while one was open for 1% of the time, Pallas kernels for 3%

profile of v5, /device:TPU:40, one launch (start us, length us, event | category | flops | bytes accessed | tf_op | source)
XLA Modules:
  0.0 201.0 jit_solution(10768308345005351851)
XLA Ops:
  7.2 0.0 copy-start
  7.2 0.1 all-gather.2.cloned.1.call-start
  7.3 1.8 last_rows.1
  9.1 0.1 all-gather.2.cloned.1.call-update
  9.1 18.6 %all-to-all-start = ((bf16[8,8,512]{2,1,0:T(8,128)(2,1)}), bf16[8,8,512]{2,1,0:T(8,128)(2,1)S(1)}, u32[]{:S(2)}, u32[]{:S(2)}) async-start(bf16[8,8,512]{2,1,0:T(8,128)(2,1)} %get-tuple-element.12), calls=%async_computation | async-start | bytes 131072 | tf_op jit(solution)/shard_map/all_to_all | solution.py:45
  27.7 0.8 copy.16.ids_ref
  28.4 10.1 %all-to-all-done = bf16[8,8,512]{2,1,0:T(8,128)(2,1)S(1)} async-done(((bf16[8,8,512]{2,1,0:T(8,128)(2,1)}), bf16[8,8,512]{2,1,0:T(8,128)(2,1)S(1)}, u32[]{:S(2)}, u32[]{:S(2)}) %all-to-all-start) | async-done | bytes 65568 | tf_op jit(solution)/shard_map/all_to_all | solution.py:45
  38.6 50.3 %psum.21.rows_ref = bf16[8,512]{1,0:T(8,128)(2,1)S(1)} all-reduce(bf16[8,512]{1,0:T(8,128)(2,1)S(1)} %reduce_sum.21), channel_id=1, replica_groups=mesh['groups'=2,'seq_hi'=4,'seq_lo'=8,'tp_0'=4,'tp_1'=2] {'seq_hi'}, use_global_device_ids=true, to_apply=%region_1.0 | all-reduce | flops 4096 | bytes 16384 | tf_op jit(solution)/shard_map/psum | solution.py:397
  88.9 2.8 %partials.1 = (f32[8,8,128]{2,1,0:T(8,128)S(1)}, f32[24,256]{1,0:T(8,128)S(1)}) custom-call(s32[8]{0:T(128)} %lengths_ref.5, s32[4]{0:T(128)} %cache_lengths_ref.1, s32[1]{0:T(128)} %bitcast.seq_ref, s32[12,2]{1,0:T(8,128)S(1)} %copy.16.ids_ref, s32[1]{0:T(128)} %bitcast.2.tp_ref, bf16[8,512]{1,0:T(8,128)(2,1)S(1)} %psum.21.rows_ref, bf16[4,512]{1,0:T(4,128)(2,1)} %qd_ref.1, ...), custom_call_target="tpu_custom_call" | custom-call | tf_op jit(solution)/shard_map/partials/pallas_call | solution.py:401
  91.7 13.1 %all_to_all.25.pieces_ref = f32[8,8,128]{2,1,0:T(8,128)S(1)} all-to-all(f32[8,8,128]{2,1,0:T(8,128)S(1)} %get-tuple-element.13), channel_id=1, replica_groups=mesh['groups'=2,'seq_hi'=4,'seq_lo'=8,'tp_0'=4,'tp_1'=2] {'seq_lo'}, dimensions={0} | all-to-all | bytes 65536 | tf_op jit(solution)/shard_map/all_to_all | solution.py:45
  104.8 0.1 merge.1
  105.0 16.3 %psum.22.slots_ref = bf16[32,128]{1,0:T(8,128)(2,1)S(1)} all-reduce(bf16[32,128]{1,0:T(8,128)(2,1)S(1)} %merge.1), channel_id=1, replica_groups=mesh['groups'=2,'seq_hi'=4,'seq_lo'=8,'tp_0'=4,'tp_1'=2] {'seq_hi'}, use_global_device_ids=true, to_apply=%region_2.0 | all-reduce | flops 4096 | bytes 16384 | tf_op jit(solution)/shard_map/psum | solution.py:418
  121.3 0.1 finish.1
  121.4 13.0 %all_to_all.26.parts_ref = bf16[8,8,128]{2,1,0:T(8,128)(2,1)S(1)} all-to-all(bf16[8,8,128]{2,1,0:T(8,128)(2,1)S(1)} %finish.1), channel_id=1, replica_groups=mesh['groups'=2,'seq_hi'=4,'seq_lo'=8,'tp_0'=4,'tp_1'=2] {'seq_lo'}, dimensions={0} | all-to-all | bytes 32768 | tf_op jit(solution)/shard_map/all_to_all | solution.py:45
  134.4 1.8 project.1
  136.2 4.4 %all-to-all-start.3 = ((f32[8,36,256]{2,1,0:T(8,128)}), f32[8,36,256]{2,1,0:T(8,128)S(1)}, u32[]{:S(2)}, u32[]{:S(2)}) async-start(f32[8,36,256]{2,1,0:T(8,128)} %project.1), calls=%async_computation.3 | async-start | bytes 655360 | tf_op jit(solution)/shard_map/all_to_all | solution.py:45
  140.6 0.0 copy-done
  140.6 0.6 reshape.21.gain_ref
  141.2 7.6 %all-to-all-done.3.pieces_ref = f32[8,36,256]{2,1,0:T(8,128)S(1)} async-done(((f32[8,36,256]{2,1,0:T(8,128)}), f32[8,36,256]{2,1,0:T(8,128)S(1)}, u32[]{:S(2)}, u32[]{:S(2)}) %all-to-all-start.3) | async-done | bytes 294944 | tf_op jit(solution)/shard_map/all_to_all | solution.py:45
  148.9 0.9 residual.1
  149.7 13.1 %all_to_all.27 = f32[8,8,128]{2,1,0:T(8,128)S(1)} all-to-all(f32[8,8,128]{2,1,0:T(8,128)S(1)} %get-tuple-element.15), channel_id=1, replica_groups=mesh['groups'=2,'seq_hi'=4,'seq_lo'=8,'tp_0'=4,'tp_1'=2] {'seq_lo'}, dimensions={0} | all-to-all | bytes 65536 | tf_op jit(solution)/shard_map/all_to_all | solution.py:45
  162.8 26.4 %psum.23.sums_ref = f32[8,128]{1,0:T(8,128)S(1)} all-reduce(f32[8,128]{1,0:T(8,128)S(1)} %reduce_sum.22), channel_id=1, replica_groups=mesh['groups'=2,'seq_hi'=4,'seq_lo'=8,'tp_0'=4,'tp_1'=2] {'seq_hi'}, use_global_device_ids=true, to_apply=%region_4.0 | all-reduce | flops 1024 | bytes 8192 | tf_op jit(solution)/shard_map/psum | solution.py:432
  189.3 0.8 verdict.1
  190.0 0.0 all-gather.2.cloned.1.call-done.kv_ref
  190.0 4.1 %attention.1 = bf16[256,512]{1,0:T(8,128)(2,1)} custom-call(s32[8]{0:T(128)} %lengths_ref.5, s32[1]{0:T(128)} %bitcast.seq_ref, bf16[256,512]{1,0:T(8,128)(2,1)} %q_hbm.1, bf16[8192,256]{1,0:T(8,128)(2,1)} %all-gather.2.cloned.1.call-done.kv_ref), custom_call_target="tpu_custom_call" | custom-call | tf_op jit(solution)/shard_map/attention/pallas_call | solution.py:329
  (2 shorter events, 0.0 us)
Async XLA Ops:
  7.2 133.5 %copy-start = (bf16[256]{0:T(256)(128)(2,1)S(1)}, bf16[256]{0:T(256)(128)(2,1)}, u32[]{:S(2)}) copy-start(bf16[256]{0:T(256)(128)(2,1)} %param.23) | copy-start | bytes 1540
  7.2 182.9 %all-gather.2.cloned.1.call-start = ((), (), s32[]{:S(2)}) async-start(), calls=%async_computation.5 | async-start | bytes 4325376 | tf_op jit(solution)/shard_map/all_gather | solution.py:395
  9.1 29.5 %all-to-all-start = ((bf16[8,8,512]{2,1,0:T(8,128)(2,1)}), bf16[8,8,512]{2,1,0:T(8,128)(2,1)S(1)}, u32[]{:S(2)}, u32[]{:S(2)}) async-start(bf16[8,8,512]{2,1,0:T(8,128)(2,1)} %get-tuple-element.12), calls=%async_computation | async-start | bytes 131072 | tf_op jit(solution)/shard_map/all_to_all | solution.py:45
  136.2 12.6 %all-to-all-start.3 = ((f32[8,36,256]{2,1,0:T(8,128)}), f32[8,36,256]{2,1,0:T(8,128)S(1)}, u32[]{:S(2)}, u32[]{:S(2)}) async-start(f32[8,36,256]{2,1,0:T(8,128)} %project.1), calls=%async_computation.3 | async-start | bytes 655360 | tf_op jit(solution)/shard_map/all_to_all | solution.py:45
Sparse Core Ops, SparseCore 0:
  10.7 166.4 all-gather.1

commit v6 on v5

--- a/solution.py
+++ b/solution.py
@@ -74,7 +74,7 @@
     copies, places = [], []
     for c in range(2):
         for r in range(ROWS):
-            local = ids_ref[r, c] - tp_ref[0] * vocab_rows
+            local = ids_ref[c, r] - tp_ref[0] * vocab_rows
             inside = (local >= 0) & (local < vocab_rows)
             local = jnp.clip(local, 0, vocab_rows - 1)
             places.append(jnp.where(inside, local % TABLE_ROWS, -1))
@@ -207,16 +207,17 @@
             w_ref[g * HD : (g + 1) * HD, :],
             preferred_element_type=jnp.float32,
         )
+    both = jnp.concatenate(
+        [partial[:HELD], partial[PART : PART + HELD], table_ref[...]], axis=0
+    ).astype(out_ref.dtype)
     for c in range(out_ref.shape[0]):
-        out_ref[c, :HELD] = partial[:HELD]
-        out_ref[c, HELD:ROWS] = partial[PART : PART + HELD]
-        out_ref[c, ROWS:] = table_ref[...]
+        out_ref[c] = both
 
 
 def residual_kernel(pieces_ref, stream_ref, gain_ref, gained_ref, sums_ref):
-    total = pieces_ref[0]
+    total = pieces_ref[0].astype(jnp.float32)
     for c in range(1, pieces_ref.shape[0]):
-        total = total + pieces_ref[c]
+        total = total + pieces_ref[c].astype(jnp.float32)
     table = total[ROWS:]
     residual = total[:ROWS] + stream_ref[...].astype(jnp.float32)
     gained = residual * gain_ref[...].astype(jnp.float32)
@@ -227,23 +228,23 @@
     lane = lax.broadcasted_iota(jnp.int32, (ROWS, HD), 1)
     packed = jnp.where(lane == 0, squares, jnp.where(lane == 1, first, second))
     packed = jnp.concatenate([packed, jnp.zeros((HD - ROWS, HD), jnp.float32)], axis=0)
-    packed = jnp.transpose(packed)[:8]
-    for c in range(sums_ref.shape[0]):
-        sums_ref[c] = packed
-
-
-def verdict_kernel(sums_ref, gained_ref, hidden_ref, win_ref):
-    sums = jnp.transpose(sums_ref[...])[:ROWS]
+    sums_ref[...] = jnp.transpose(packed)[:8]
+
+
+def verdict_kernel(sums_ref, gained_ref, after_ref, hidden_ref, win_ref):
+    lines = sums_ref[0]
+    for c in range(1, sums_ref.shape[0]):
+        lines = lines + sums_ref[c]
+    sums = jnp.transpose(lines)[:ROWS]
     inv_rms = 1.0 / jnp.sqrt(sums[:, 0:1] / D + norm_eps)
     hidden_ref[...] = (gained_ref[...] * inv_rms).astype(hidden_ref.dtype)
-    lines = sums_ref[...]
     inv_rms = 1.0 / jnp.sqrt(lines[0:1] / D + norm_eps)
     win = 1.0 / (1.0 + jnp.exp((lines[2:3] - lines[1:2]) * inv_rms))
     win_ref[...] = win[0, :ROWS]
 
 
 def attention_kernel(
-    lengths_ref, seq_ref, q_hbm, kv_ref, out_ref, q_ref, kv_buf, top_ref, total_ref, sum_ref,
+    lengths_ref, seq_ref, q_hbm, kv_ref, after_ref, out_ref, q_ref, kv_buf, top_ref, total_ref, sum_ref,
     q_sem, sems,
 ):
     tokens = q_ref.shape[0]
@@ -324,12 +325,12 @@
         out_ref[:, g * HD : (g + 1) * HD] = rows.astype(out_ref.dtype)
 
 
-def attention(lengths, seq_index, q, kv):
+def attention(lengths, seq_index, q, kv, after):
     tokens = q.shape[0]
     return pl.pallas_call(
         attention_kernel,
         out_shape=jax.ShapeDtypeStruct(q.shape, q.dtype),
-        in_specs=[SM, SM, HB, HB],
+        in_specs=[SM, SM, HB, HB, VM],
         out_specs=VM,
         scratch_shapes=[
             pltpu.VMEM(q.shape, q.dtype),
@@ -342,7 +343,7 @@
         ],
         compiler_params=pltpu.CompilerParams(vmem_limit_bytes=24 * 1024 * 1024),
         name="attention",
-    )(lengths, seq_index, held(q), held(kv))
+    )(lengths, seq_index, held(q), held(kv), after)
 
 
 def call(kernel, shapes, specs, name, scratch=()):
@@ -409,7 +410,7 @@
             pltpu.SemaphoreType.DMA((2 * ROWS,)),
         ],
     )(
-        pair_lengths, cache_lengths, seq_index, verdict_ids, tp_index, rows, held(q_decode),
+        pair_lengths, cache_lengths, seq_index, held(verdict_ids.T), tp_index, rows, held(q_decode),
         held(k_prefill), held(v_prefill), held(cache_k), held(cache_v), held(vocab_table),
     )
     slots = call(merge_kernel, shape((hi * PART, HD), jnp.bfloat16), [SM, VM], "merge")(
@@ -419,25 +420,25 @@
     parts = call(finish_kernel, shape((lo, PART, HD), jnp.bfloat16), [VM], "finish")(slots)
     parts = exchanged(parts, "seq_lo")
     pieces = call(
-        project_kernel, shape((tp, 3 * ROWS, width), f32), [VM, PIPE, VM], "project"
+        project_kernel, shape((tp, 3 * ROWS, width), jnp.bfloat16), [VM, PIPE, VM], "project"
     )(parts, held(out_weight), table_rows)
     pieces = exchanged(pieces, TP)
     gained, sums = call(
         residual_kernel,
-        (shape((ROWS, width), f32), shape((lo, 8, HD), f32)),
+        (shape((ROWS, width), f32), shape((8, HD), f32)),
         [VM, PIPE, PIPE],
         "residual",
     )(pieces, held(stream), held(norm_gain.reshape(1, width)))
-    sums = jnp.sum(exchanged(sums, "seq_lo"), axis=0)
     sums = lax.psum(sums, "seq_hi")
+    attended = attention(pair_lengths, seq_index, q_prefill, kv, sums)
+    sums = exchanged(jnp.broadcast_to(sums[None], (lo, *sums.shape)), "seq_lo")
     verdict_hidden, win = call(
         verdict_kernel,
         (shape((ROWS, width), jnp.bfloat16), shape((ROWS,), f32)),
-        [VM, VM],
+        [VM, VM, HB],
         "verdict",
-    )(sums, gained)
-
-    attended = attention(pair_lengths, seq_index, q_prefill, kv)
+    )(sums, gained, held(attended))
+
     return (attended, verdict_hidden, win)
 
 

time: 202 us -> 198 us (0.980)
  blocking collectives: 132 us -> 119 us
  waiting for transfers between devices: 17.8 us -> 23.2 us
  starting transfers between devices: 23.1 us -> 27.2 us
    all_to_all x3 -> x2, blocking collectives: 39.2 us -> 26.3 us  [exchanged(): return lax.all_to_all(copies, axis, 0, 0, tiled=True)]
    all_to_all x2 -> x3, waiting for transfers between devices: 17.8 us -> 23.1 us  [exchanged(): return lax.all_to_all(copies, axis, 0, 0, tiled=True)]
    all_to_all x2 -> x3, starting transfers between devices: 23 us -> 27.1 us  [exchanged(): return lax.all_to_all(copies, axis, 0, 0, tiled=True)]
  transfers between devices with their start and end apart: 3 -> 4, of which waited for: 2 -> 3; matrix products, arithmetic and copies ran while one was open for 1% -> 1% of each run, Pallas kernels for 3% -> 5%
where the time goes in v6:
time: 198 us; the launch traced here: 197 us
  blocking collectives  119 us (60%)
  starting transfers between devices  27.2 us (14%)
  waiting for transfers between devices  23.2 us (12%)
  between operations  14.1 us (7%)
  Pallas kernels  12.2 us (6%)
    psum x1, blocking collectives, shards(): rows = lax.psum(rows.astype(jnp.bfloat16), 'seq_hi')  50.2 us
    all_to_all x3, starting transfers between devices, exchanged(): return lax.all_to_all(copies, axis, 0, 0, tiled=True)  27.1 us
    psum x1, blocking collectives, shards(): sums = lax.psum(sums, 'seq_hi')  26.3 us
    all_to_all x2, blocking collectives, exchanged(): return lax.all_to_all(copies, axis, 0, 0, tiled=True)  26.3 us
    all_to_all x3, waiting for transfers between devices, exchanged(): return lax.all_to_all(copies, axis, 0, 0, tiled=True)  23.1 us
    psum x1, blocking collectives, shards(): slots = lax.psum(slots, 'seq_hi')  16.3 us
    pallas_call x1, Pallas kernels, attention(): pl.pallas_call(attention_kernel, out_shape=jax.ShapeDtypeStruct(q.shape,...  4.08 us
  transfers between devices with their start and end apart: 4, of which 3 were waited for; matrix products, arithmetic and copies ran while one was open for 1% of the time, Pallas kernels for 5%

profile of v6, /device:TPU:40, one launch (start us, length us, event | category | flops | bytes accessed | tf_op | source)
XLA Modules:
  0.0 197.1 jit_solution(15893148467126015938)
XLA Ops:
  7.2 0.0 copy-start
  7.2 0.1 all-gather.2.cloned.1.call-start
  7.3 1.8 last_rows.1
  9.1 0.1 all-gather.2.cloned.1.call-update
  9.1 18.6 %all-to-all-start = ((bf16[8,8,512]{2,1,0:T(8,128)(2,1)}), bf16[8,8,512]{2,1,0:T(8,128)(2,1)S(1)}, u32[]{:S(2)}, u32[]{:S(2)}) async-start(bf16[8,8,512]{2,1,0:T(8,128)(2,1)} %get-tuple-element.12), calls=%async_computation | async-start | bytes 131072 | tf_op jit(solution)/shard_map/all_to_all | solution.py:45
  27.7 10.9 %all-to-all-done = bf16[8,8,512]{2,1,0:T(8,128)(2,1)S(1)} async-done(((bf16[8,8,512]{2,1,0:T(8,128)(2,1)}), bf16[8,8,512]{2,1,0:T(8,128)(2,1)S(1)}, u32[]{:S(2)}, u32[]{:S(2)}) %all-to-all-start) | async-done | bytes 65568 | tf_op jit(solution)/shard_map/all_to_all | solution.py:45
  38.6 50.2 %psum.21.rows_ref = bf16[8,512]{1,0:T(8,128)(2,1)S(1)} all-reduce(bf16[8,512]{1,0:T(8,128)(2,1)S(1)} %reduce_sum.12), channel_id=1, replica_groups=mesh['groups'=2,'seq_hi'=4,'seq_lo'=8,'tp_0'=4,'tp_1'=2] {'seq_hi'}, use_global_device_ids=true, to_apply=%region_1.0 | all-reduce | flops 4096 | bytes 16384 | tf_op jit(solution)/shard_map/psum | solution.py:398
  88.8 2.7 %partials.1 = (f32[8,8,128]{2,1,0:T(8,128)S(1)}, f32[24,256]{1,0:T(8,128)S(1)}) custom-call(s32[8]{0:T(128)} %lengths_ref.5, s32[4]{0:T(128)} %cache_lengths_ref.1, s32[1]{0:T(128)} %bitcast.seq_ref, s32[2,12]{1,0:T(2,128)} %bitcast.4, s32[1]{0:T(128)} %bitcast.3.tp_ref, bf16[8,512]{1,0:T(8,128)(2,1)S(1)} %psum.21.rows_ref, bf16[4,512]{1,0:T(4,128)(2,1)} %qd_ref.1, ...), custom_call_target="tpu_custom_call" | custom-call | tf_op jit(solution)/shard_map/partials/pallas_call | solution.py:402
  91.6 13.1 %all_to_all.25.pieces_ref = f32[8,8,128]{2,1,0:T(8,128)S(1)} all-to-all(f32[8,8,128]{2,1,0:T(8,128)S(1)} %get-tuple-element.13), channel_id=1, replica_groups=mesh['groups'=2,'seq_hi'=4,'seq_lo'=8,'tp_0'=4,'tp_1'=2] {'seq_lo'}, dimensions={0} | all-to-all | bytes 65536 | tf_op jit(solution)/shard_map/all_to_all | solution.py:45
  104.7 0.1 merge.1
  104.8 16.3 %psum.22.slots_ref = bf16[32,128]{1,0:T(8,128)(2,1)S(1)} all-reduce(bf16[32,128]{1,0:T(8,128)(2,1)S(1)} %merge.1), channel_id=1, replica_groups=mesh['groups'=2,'seq_hi'=4,'seq_lo'=8,'tp_0'=4,'tp_1'=2] {'seq_hi'}, use_global_device_ids=true, to_apply=%region_2.0 | all-reduce | flops 4096 | bytes 16384 | tf_op jit(solution)/shard_map/psum | solution.py:419
  121.1 0.1 finish.1
  121.2 13.2 %all_to_all.26.parts_ref = bf16[8,8,128]{2,1,0:T(8,128)(2,1)S(1)} all-to-all(bf16[8,8,128]{2,1,0:T(8,128)(2,1)S(1)} %finish.1), channel_id=1, replica_groups=mesh['groups'=2,'seq_hi'=4,'seq_lo'=8,'tp_0'=4,'tp_1'=2] {'seq_lo'}, dimensions={0} | all-to-all | bytes 32768 | tf_op jit(solution)/shard_map/all_to_all | solution.py:45
  134.4 1.8 project.1
  136.1 5.0 %all-to-all-start.3 = ((bf16[8,36,256]{2,1,0:T(8,128)(2,1)}), bf16[8,36,256]{2,1,0:T(8,128)(2,1)S(1)}, u32[]{:S(2)}, u32[]{:S(2)}) async-start(bf16[8,36,256]{2,1,0:T(8,128)(2,1)} %project.1), calls=%async_computation.3 | async-start | bytes 327680 | tf_op jit(solution)/shard_map/all_to_all | solution.py:45
  141.2 0.0 copy-done
  141.2 0.6 reshape.22.gain_ref
  141.8 5.9 %all-to-all-done.3.pieces_ref = bf16[8,36,256]{2,1,0:T(8,128)(2,1)S(1)} async-done(((bf16[8,36,256]{2,1,0:T(8,128)(2,1)}), bf16[8,36,256]{2,1,0:T(8,128)(2,1)S(1)}, u32[]{:S(2)}, u32[]{:S(2)}) %all-to-all-start.3) | async-done | bytes 147488 | tf_op jit(solution)/shard_map/all_to_all | solution.py:45
  147.6 0.9 residual.1
  148.5 26.3 %psum.23.after_ref = f32[8,128]{1,0:T(8,128)S(1)} all-reduce(f32[8,128]{1,0:T(8,128)S(1)} %get-tuple-element.15), channel_id=1, replica_groups=mesh['groups'=2,'seq_hi'=4,'seq_lo'=8,'tp_0'=4,'tp_1'=2] {'seq_hi'}, use_global_device_ids=true, to_apply=%region_3.0 | all-reduce | flops 1024 | bytes 8192 | tf_op jit(solution)/shard_map/psum | solution.py:432
  174.8 0.6 broadcast_in_dim.2
  175.4 3.5 %all-to-all-start.4 = ((f32[8,8,128]{2,1,0:T(8,128)}), f32[8,8,128]{2,1,0:T(8,128)S(1)}, u32[]{:S(2)}, u32[]{:S(2)}) async-start(f32[8,8,128]{2,1,0:T(8,128)} %broadcast_in_dim.2), calls=%async_computation.4 | async-start | bytes 65536 | tf_op jit(solution)/shard_map/all_to_all | solution.py:45
  179.0 0.0 all-gather.2.cloned.1.call-done.kv_ref
  179.0 4.1 %attention.1.after_ref = bf16[256,512]{1,0:T(8,128)(2,1)} custom-call(s32[8]{0:T(128)} %lengths_ref.5, s32[1]{0:T(128)} %bitcast.seq_ref, bf16[256,512]{1,0:T(8,128)(2,1)} %q_hbm.1, bf16[8192,256]{1,0:T(8,128)(2,1)} %all-gather.2.cloned.1.call-done.kv_ref, f32[8,128]{1,0:T(8,128)S(1)} %psum.23.after_ref), custom_call_target="tpu_custom_call" | custom-call | tf_op jit(solution)/shard_map/attention/pallas_call | solution.py:330
  183.1 6.3 %all-to-all-done.4.sums_ref = f32[8,8,128]{2,1,0:T(8,128)S(1)} async-done(((f32[8,8,128]{2,1,0:T(8,128)}), f32[8,8,128]{2,1,0:T(8,128)S(1)}, u32[]{:S(2)}, u32[]{:S(2)}) %all-to-all-start.4) | async-done | bytes 32800 | tf_op jit(solution)/shard_map/all_to_all | solution.py:45
  189.4 0.8 verdict.1
  (1 shorter events, 0.0 us)
Async XLA Ops:
  7.2 134.0 %copy-start = (bf16[256]{0:T(256)(128)(2,1)S(1)}, bf16[256]{0:T(256)(128)(2,1)}, u32[]{:S(2)}) copy-start(bf16[256]{0:T(256)(128)(2,1)} %param.23) | copy-start | bytes 1540
  7.2 171.8 %all-gather.2.cloned.1.call-start = ((), (), s32[]{:S(2)}) async-start(), calls=%async_computation.5 | async-start | bytes 4325376 | tf_op jit(solution)/shard_map/all_gather | solution.py:396
  9.1 29.5 %all-to-all-start = ((bf16[8,8,512]{2,1,0:T(8,128)(2,1)}), bf16[8,8,512]{2,1,0:T(8,128)(2,1)S(1)}, u32[]{:S(2)}, u32[]{:S(2)}) async-start(bf16[8,8,512]{2,1,0:T(8,128)(2,1)} %get-tuple-element.12), calls=%async_computation | async-start | bytes 131072 | tf_op jit(solution)/shard_map/all_to_all | solution.py:45
  136.1 11.5 %all-to-all-start.3 = ((bf16[8,36,256]{2,1,0:T(8,128)(2,1)}), bf16[8,36,256]{2,1,0:T(8,128)(2,1)S(1)}, u32[]{:S(2)}, u32[]{:S(2)}) async-start(bf16[8,36,256]{2,1,0:T(8,128)(2,1)} %project.1), calls=%async_computation.3 | async-start | bytes 327680 | tf_op jit(solution)/shard_map/all_to_all | solution.py:45
  175.4 14.0 %all-to-all-start.4 = ((f32[8,8,128]{2,1,0:T(8,128)}), f32[8,8,128]{2,1,0:T(8,128)S(1)}, u32[]{:S(2)}, u32[]{:S(2)}) async-start(f32[8,8,128]{2,1,0:T(8,128)} %broadcast_in_dim.2), calls=%async_computation.4 | async-start | bytes 65536 | tf_op jit(solution)/shard_map/all_to_all | solution.py:45
Sparse Core Ops, SparseCore 0:
  10.1 165.8 all-gather.1

commit v7 on v6

--- a/solution.py
+++ b/solution.py
@@ -111,12 +111,9 @@
 
 
 def partials_kernel(
-    lengths_ref, cache_lengths_ref, seq_ref, ids_ref, tp_ref, rows_ref, qd_ref, k_ref, v_ref,
-    ck_ref, cv_ref, table_ref, out_ref, picked_ref, q_scratch, blocks, sems,
+    lengths_ref, cache_lengths_ref, seq_ref, rows_ref, qd_ref, k_ref, v_ref, ck_ref, cv_ref,
+    out_ref, q_scratch,
 ):
-    copies, places = table_copies(ids_ref, tp_ref, table_ref, blocks, sems)
-    for copy in copies:
-        copy.start()
     tokens = k_ref.shape[0]
     cache_count = ck_ref.shape[1]
     ends = ends_of(lengths_ref)
@@ -158,12 +155,6 @@
     for c in range(out_ref.shape[0]):
         rows = slice(c * PART, (c + 1) * PART)
         out_ref[c] = jnp.where(place == HELD, spread((top[rows], total[rows])), sums[rows])
-    for copy in copies:
-        copy.wait()
-    index = lax.broadcasted_iota(jnp.int32, blocks.shape[1:], 0)
-    for i, wanted in enumerate(places):
-        block = jnp.where(index == wanted, blocks[i].astype(jnp.float32), 0.0)
-        picked_ref[i : i + 1, :] = jnp.sum(block, axis=0, keepdims=True)
 
 
 def merged(pieces, parts):
@@ -196,6 +187,23 @@
     rows = jnp.where(row < HELD, sums / total, 0.0).astype(out_ref.dtype)
     for c in range(out_ref.shape[0]):
         out_ref[c] = rows
+
+
+def prepare_kernel(
+    ids_ref, tp_ref, after_ref, w_hbm, table_ref, picked_ref, w_ref, blocks, w_sem, sems
+):
+    copies, places = table_copies(ids_ref, tp_ref, table_ref, blocks, sems)
+    w_copy = pltpu.make_async_copy(w_hbm, w_ref, w_sem)
+    for copy in copies:
+        copy.start()
+    w_copy.start()
+    for copy in copies:
+        copy.wait()
+    index = lax.broadcasted_iota(jnp.int32, blocks.shape[1:], 0)
+    for i, wanted in enumerate(places):
+        block = jnp.where(index == wanted, blocks[i].astype(jnp.float32), 0.0)
+        picked_ref[i : i + 1, :] = jnp.sum(block, axis=0, keepdims=True)
+    w_copy.wait()
 
 
 def project_kernel(parts_ref, w_ref, table_ref, out_ref):
@@ -399,29 +407,36 @@
 
     tp_index = lax.axis_index(TP).astype(jnp.int32).reshape(1)
     hi_index = lax.axis_index("seq_hi").astype(jnp.int32).reshape(1)
-    partials, table_rows = call(
+    partials = call(
         partials_kernel,
-        (shape((lo, PART, HD), f32), shape((2 * ROWS, width), f32)),
-        [SM] * 5 + [VM] + [PIPE] * 5 + [HB],
+        shape((lo, PART, HD), f32),
+        [SM] * 3 + [VM] + [PIPE] * 5,
         "partials",
-        [
-            pltpu.VMEM((GROUP * SLOT, HD), f32),
-            pltpu.VMEM((2 * ROWS, TABLE_ROWS, width), jnp.bfloat16),
-            pltpu.SemaphoreType.DMA((2 * ROWS,)),
-        ],
+        [pltpu.VMEM((GROUP * SLOT, HD), f32)],
     )(
-        pair_lengths, cache_lengths, seq_index, held(verdict_ids.T), tp_index, rows, held(q_decode),
-        held(k_prefill), held(v_prefill), held(cache_k), held(cache_v), held(vocab_table),
+        pair_lengths, cache_lengths, seq_index, rows, held(q_decode), held(k_prefill),
+        held(v_prefill), held(cache_k), held(cache_v),
     )
     slots = call(merge_kernel, shape((hi * PART, HD), jnp.bfloat16), [SM, VM], "merge")(
         hi_index, exchanged(partials, "seq_lo")
     )
     slots = lax.psum(slots, "seq_hi")
     parts = call(finish_kernel, shape((lo, PART, HD), jnp.bfloat16), [VM], "finish")(slots)
+    table_rows, weight = call(
+        prepare_kernel,
+        (shape((2 * ROWS, width), f32), shape(out_weight.shape, out_weight.dtype)),
+        [SM, SM, VM, HB, HB],
+        "prepare",
+        [
+            pltpu.VMEM((2 * ROWS, TABLE_ROWS, width), jnp.bfloat16),
+            pltpu.SemaphoreType.DMA,
+            pltpu.SemaphoreType.DMA((2 * ROWS,)),
+        ],
+    )(held(verdict_ids.T), tp_index, parts, held(out_weight), held(vocab_table))
     parts = exchanged(parts, "seq_lo")
     pieces = call(
-        project_kernel, shape((tp, 3 * ROWS, width), jnp.bfloat16), [VM, PIPE, VM], "project"
-    )(parts, held(out_weight), table_rows)
+        project_kernel, shape((tp, 3 * ROWS, width), jnp.bfloat16), [VM, VM, VM], "project"
+    )(parts, weight, table_rows)
     pieces = exchanged(pieces, TP)
     gained, sums = call(
         residual_kernel,

time: 198 us -> 196 us (0.990)
  blocking collectives: 119 us -> 135 us
  starting transfers between devices: 27.2 us -> 11.7 us
  waiting for transfers between devices: 23.2 us -> 20.2 us
    all_to_all x2, blocking collectives: 26.3 us -> 42.5 us  [exchanged(): return lax.all_to_all(copies, axis, 0, 0, tiled=True)]
    all_to_all x3, starting transfers between devices: 27.1 us -> 11.6 us  [exchanged(): return lax.all_to_all(copies, axis, 0, 0, tiled=True)]
    all_to_all x3, waiting for transfers between devices: 23.1 us -> 20.1 us  [exchanged(): return lax.all_to_all(copies, axis, 0, 0, tiled=True)]
    pallas_call x2 -> x3, Pallas kernels: 4.52 us -> 4.74 us  [the longest x1 2.56 us: shards(): call(prepare_kernel, (shape((2 * ROWS, width), f32), shape(out_weight.sha...]
where the time goes in v7:
time: 196 us
  blocking collectives  135 us (69%)
  waiting for transfers between devices  20.2 us (10%)
  between operations  14.1 us (7%)
  Pallas kernels  13 us (7%)
  starting transfers between devices  11.7 us (6%)
    psum x1, blocking collectives, shards(): rows = lax.psum(rows.astype(jnp.bfloat16), 'seq_hi')  50.1 us
    all_to_all x2, blocking collectives, exchanged(): return lax.all_to_all(copies, axis, 0, 0, tiled=True)  42.5 us
    psum x1, blocking collectives, shards(): sums = lax.psum(sums, 'seq_hi')  26.6 us
    all_to_all x3, waiting for transfers between devices, exchanged(): return lax.all_to_all(copies, axis, 0, 0, tiled=True)  20.1 us
    psum x1, blocking collectives, shards(): slots = lax.psum(slots, 'seq_hi')  16.3 us
    all_to_all x3, starting transfers between devices, exchanged(): return lax.all_to_all(copies, axis, 0, 0, tiled=True)  11.6 us
    pallas_call x1, Pallas kernels, attention(): pl.pallas_call(attention_kernel, out_shape=jax.ShapeDtypeStruct(q.shape,...  4.08 us
  transfers between devices with their start and end apart: 4, of which 3 were waited for; matrix products, arithmetic and copies ran while one was open for 1% of the time, Pallas kernels for 5%

profile of v7, /device:TPU:40, one launch (start us, length us, event | category | flops | bytes accessed | tf_op | source)
XLA Modules:
  0.0 195.6 jit_solution(11689769838858589262)
XLA Ops:
  7.2 0.0 copy-start
  7.2 0.1 all-gather.2.cloned.1.call-start
  7.3 1.7 last_rows.1
  8.9 0.1 all-gather.2.cloned.1.call-update
  9.0 29.3 %all_to_all.25 = bf16[8,8,512]{2,1,0:T(8,128)(2,1)S(1)} all-to-all(bf16[8,8,512]{2,1,0:T(8,128)(2,1)S(1)} %get-tuple-element.12), channel_id=1, replica_groups=mesh['groups'=2,'seq_hi'=4,'seq_lo'=8,'tp_0'=4,'tp_1'=2] {'seq_lo'}, dimensions={0} | all-to-all | bytes 131072 | tf_op jit(solution)/shard_map/all_to_all | solution.py:45
  38.3 50.1 %psum.21.rows_ref = bf16[8,512]{1,0:T(8,128)(2,1)S(1)} all-reduce(bf16[8,512]{1,0:T(8,128)(2,1)S(1)} %reduce_sum.12), channel_id=1, replica_groups=mesh['groups'=2,'seq_hi'=4,'seq_lo'=8,'tp_0'=4,'tp_1'=2] {'seq_hi'}, use_global_device_ids=true, to_apply=%region_1.0 | all-reduce | flops 4096 | bytes 16384 | tf_op jit(solution)/shard_map/psum | solution.py:406
  88.4 1.4 partials.1
  89.7 13.2 %all_to_all.26.pieces_ref = f32[8,8,128]{2,1,0:T(8,128)S(1)} all-to-all(f32[8,8,128]{2,1,0:T(8,128)S(1)} %partials.1), channel_id=1, replica_groups=mesh['groups'=2,'seq_hi'=4,'seq_lo'=8,'tp_0'=4,'tp_1'=2] {'seq_lo'}, dimensions={0} | all-to-all | bytes 65536 | tf_op jit(solution)/shard_map/all_to_all | solution.py:45
  103.0 0.1 merge.1
  103.1 16.3 %psum.22.slots_ref = bf16[32,128]{1,0:T(8,128)(2,1)S(1)} all-reduce(bf16[32,128]{1,0:T(8,128)(2,1)S(1)} %merge.1), channel_id=1, replica_groups=mesh['groups'=2,'seq_hi'=4,'seq_lo'=8,'tp_0'=4,'tp_1'=2] {'seq_hi'}, use_global_device_ids=true, to_apply=%region_2.0 | all-reduce | flops 4096 | bytes 16384 | tf_op jit(solution)/shard_map/psum | solution.py:423
  119.4 0.7 finish.1.after_ref
  120.1 3.5 %all-to-all-start.2 = ((bf16[8,8,128]{2,1,0:T(8,128)(2,1)}), bf16[8,8,128]{2,1,0:T(8,128)(2,1)S(1)}, u32[]{:S(2)}, u32[]{:S(2)}) async-start(bf16[8,8,128]{2,1,0:T(8,128)(2,1)} %finish.1.after_ref), calls=%async_computation.2 | async-start | bytes 32768 | tf_op jit(solution)/shard_map/all_to_all | solution.py:45
  123.7 2.6 %prepare.1 = (f32[24,256]{1,0:T(8,128)S(1)}, bf16[512,256]{1,0:T(8,128)(2,1)S(1)}) custom-call(s32[2,12]{1,0:T(2,128)} %bitcast.4, s32[1]{0:T(128)} %bitcast.3.tp_ref, bf16[8,8,128]{2,1,0:T(8,128)(2,1)} %finish.1.after_ref, bf16[512,256]{1,0:T(8,128)(2,1)} %w_hbm.1, bf16[8016,256]{1,0:T(8,128)(2,1)} %table_ref.1), custom_call_target="tpu_custom_call" | custom-call | tf_op jit(solution)/shard_map/prepare/pallas_call | solution.py:425
  126.2 7.9 %all-to-all-done.2.parts_ref = bf16[8,8,128]{2,1,0:T(8,128)(2,1)S(1)} async-done(((bf16[8,8,128]{2,1,0:T(8,128)(2,1)}), bf16[8,8,128]{2,1,0:T(8,128)(2,1)S(1)}, u32[]{:S(2)}, u32[]{:S(2)}) %all-to-all-start.2) | async-done | bytes 16416 | tf_op jit(solution)/shard_map/all_to_all | solution.py:45
  134.1 0.8 project.1
  134.9 4.5 %all-to-all-start.3 = ((bf16[8,36,256]{2,1,0:T(8,128)(2,1)}), bf16[8,36,256]{2,1,0:T(8,128)(2,1)S(1)}, u32[]{:S(2)}, u32[]{:S(2)}) async-start(bf16[8,36,256]{2,1,0:T(8,128)(2,1)} %project.1), calls=%async_computation.3 | async-start | bytes 327680 | tf_op jit(solution)/shard_map/all_to_all | solution.py:45
  139.5 0.0 copy-done
  139.5 0.6 reshape.22.gain_ref
  140.1 5.9 %all-to-all-done.3.pieces_ref = bf16[8,36,256]{2,1,0:T(8,128)(2,1)S(1)} async-done(((bf16[8,36,256]{2,1,0:T(8,128)(2,1)}), bf16[8,36,256]{2,1,0:T(8,128)(2,1)S(1)}, u32[]{:S(2)}, u32[]{:S(2)}) %all-to-all-start.3) | async-done | bytes 147488 | tf_op jit(solution)/shard_map/all_to_all | solution.py:45
  145.9 0.9 residual.1
  146.8 26.6 %psum.23.after_ref = f32[8,128]{1,0:T(8,128)S(1)} all-reduce(f32[8,128]{1,0:T(8,128)S(1)} %get-tuple-element.15), channel_id=1, replica_groups=mesh['groups'=2,'seq_hi'=4,'seq_lo'=8,'tp_0'=4,'tp_1'=2] {'seq_hi'}, use_global_device_ids=true, to_apply=%region_3.0 | all-reduce | flops 1024 | bytes 8192 | tf_op jit(solution)/shard_map/psum | solution.py:447
  173.4 0.6 broadcast_in_dim.2
  174.0 3.5 %all-to-all-start.4 = ((f32[8,8,128]{2,1,0:T(8,128)}), f32[8,8,128]{2,1,0:T(8,128)S(1)}, u32[]{:S(2)}, u32[]{:S(2)}) async-start(f32[8,8,128]{2,1,0:T(8,128)} %broadcast_in_dim.2), calls=%async_computation.4 | async-start | bytes 65536 | tf_op jit(solution)/shard_map/all_to_all | solution.py:45
  177.6 0.0 all-gather.2.cloned.1.call-done.kv_ref
  177.6 4.1 %attention.1.after_ref = bf16[256,512]{1,0:T(8,128)(2,1)} custom-call(s32[8]{0:T(128)} %lengths_ref.5, s32[1]{0:T(128)} %bitcast.seq_ref, bf16[256,512]{1,0:T(8,128)(2,1)} %q_hbm.1, bf16[8192,256]{1,0:T(8,128)(2,1)} %all-gather.2.cloned.1.call-done.kv_ref, f32[8,128]{1,0:T(8,128)S(1)} %psum.23.after_ref), custom_call_target="tpu_custom_call" | custom-call | tf_op jit(solution)/shard_map/attention/pallas_call | solution.py:338
  181.7 6.3 %all-to-all-done.4.sums_ref = f32[8,8,128]{2,1,0:T(8,128)S(1)} async-done(((f32[8,8,128]{2,1,0:T(8,128)}), f32[8,8,128]{2,1,0:T(8,128)S(1)}, u32[]{:S(2)}, u32[]{:S(2)}) %all-to-all-start.4) | async-done | bytes 32800 | tf_op jit(solution)/shard_map/all_to_all | solution.py:45
  188.0 0.8 verdict.1
  (1 shorter events, 0.0 us)
Async XLA Ops:
  7.2 132.3 %copy-start = (bf16[256]{0:T(256)(128)(2,1)S(1)}, bf16[256]{0:T(256)(128)(2,1)}, u32[]{:S(2)}) copy-start(bf16[256]{0:T(256)(128)(2,1)} %param.23) | copy-start | bytes 1540
  7.2 170.4 %all-gather.2.cloned.1.call-start = ((), (), s32[]{:S(2)}) async-start(), calls=%async_computation.5 | async-start | bytes 4325376 | tf_op jit(solution)/shard_map/all_gather | solution.py:404
  120.1 14.0 %all-to-all-start.2 = ((bf16[8,8,128]{2,1,0:T(8,128)(2,1)}), bf16[8,8,128]{2,1,0:T(8,128)(2,1)S(1)}, u32[]{:S(2)}, u32[]{:S(2)}) async-start(bf16[8,8,128]{2,1,0:T(8,128)(2,1)} %finish.1.after_ref), calls=%async_computation.2 | async-start | bytes 32768 | tf_op jit(solution)/shard_map/all_to_all | solution.py:45
  134.9 11.0 %all-to-all-start.3 = ((bf16[8,36,256]{2,1,0:T(8,128)(2,1)}), bf16[8,36,256]{2,1,0:T(8,128)(2,1)S(1)}, u32[]{:S(2)}, u32[]{:S(2)}) async-start(bf16[8,36,256]{2,1,0:T(8,128)(2,1)} %project.1), calls=%async_computation.3 | async-start | bytes 327680 | tf_op jit(solution)/shard_map/all_to_all | solution.py:45
  174.0 14.0 %all-to-all-start.4 = ((f32[8,8,128]{2,1,0:T(8,128)}), f32[8,8,128]{2,1,0:T(8,128)S(1)}, u32[]{:S(2)}, u32[]{:S(2)}) async-start(f32[8,8,128]{2,1,0:T(8,128)} %broadcast_in_dim.2), calls=%async_computation.4 | async-start | bytes 65536 | tf_op jit(solution)/shard_map/all_to_all | solution.py:45
Sparse Core Ops, SparseCore 0:
  10.1 166.5 all-gather.1

commit v8 on v7

--- a/solution.py
+++ b/solution.py
@@ -112,7 +112,7 @@
 
 def partials_kernel(
     lengths_ref, cache_lengths_ref, seq_ref, rows_ref, qd_ref, k_ref, v_ref, ck_ref, cv_ref,
-    out_ref, q_scratch,
+    after_ref, out_ref, q_scratch,
 ):
     tokens = k_ref.shape[0]
     cache_count = ck_ref.shape[1]
@@ -189,20 +189,21 @@
         out_ref[c] = rows
 
 
-def prepare_kernel(
-    ids_ref, tp_ref, after_ref, w_hbm, table_ref, picked_ref, w_ref, blocks, w_sem, sems
-):
+def table_kernel(ids_ref, tp_ref, after_ref, table_ref, picked_ref, blocks, sems):
     copies, places = table_copies(ids_ref, tp_ref, table_ref, blocks, sems)
-    w_copy = pltpu.make_async_copy(w_hbm, w_ref, w_sem)
     for copy in copies:
         copy.start()
-    w_copy.start()
     for copy in copies:
         copy.wait()
     index = lax.broadcasted_iota(jnp.int32, blocks.shape[1:], 0)
     for i, wanted in enumerate(places):
         block = jnp.where(index == wanted, blocks[i].astype(jnp.float32), 0.0)
         picked_ref[i : i + 1, :] = jnp.sum(block, axis=0, keepdims=True)
+
+
+def weight_kernel(after_ref, w_hbm, w_ref, w_sem):
+    w_copy = pltpu.make_async_copy(w_hbm, w_ref, w_sem)
+    w_copy.start()
     w_copy.wait()
 
 
@@ -402,40 +403,47 @@
         "last_rows",
     )(pair_lengths, seq_index, held(q_prefill), held(k_prefill), held(v_prefill))
     kv = lax.all_gather(kv, SEQ, axis=0, tiled=True)
+    tp_index = lax.axis_index(TP).astype(jnp.int32).reshape(1)
+    table_rows = call(
+        table_kernel,
+        shape((2 * ROWS, width), f32),
+        [SM, SM, HB, HB],
+        "table",
+        [
+            pltpu.VMEM((2 * ROWS, TABLE_ROWS, width), jnp.bfloat16),
+            pltpu.SemaphoreType.DMA((2 * ROWS,)),
+        ],
+    )(held(verdict_ids.T), tp_index, picked, held(vocab_table))
+    table_rows = held(table_rows)
     rows = jnp.sum(exchanged(picked, "seq_lo").astype(f32), axis=0)
     rows = lax.psum(rows.astype(jnp.bfloat16), "seq_hi")
 
-    tp_index = lax.axis_index(TP).astype(jnp.int32).reshape(1)
     hi_index = lax.axis_index("seq_hi").astype(jnp.int32).reshape(1)
     partials = call(
         partials_kernel,
         shape((lo, PART, HD), f32),
-        [SM] * 3 + [VM] + [PIPE] * 5,
+        [SM] * 3 + [VM] + [PIPE] * 5 + [HB],
         "partials",
         [pltpu.VMEM((GROUP * SLOT, HD), f32)],
     )(
         pair_lengths, cache_lengths, seq_index, rows, held(q_decode), held(k_prefill),
-        held(v_prefill), held(cache_k), held(cache_v),
+        held(v_prefill), held(cache_k), held(cache_v), table_rows,
     )
     slots = call(merge_kernel, shape((hi * PART, HD), jnp.bfloat16), [SM, VM], "merge")(
         hi_index, exchanged(partials, "seq_lo")
     )
     slots = lax.psum(slots, "seq_hi")
     parts = call(finish_kernel, shape((lo, PART, HD), jnp.bfloat16), [VM], "finish")(slots)
-    table_rows, weight = call(
-        prepare_kernel,
-        (shape((2 * ROWS, width), f32), shape(out_weight.shape, out_weight.dtype)),
-        [SM, SM, VM, HB, HB],
-        "prepare",
-        [
-            pltpu.VMEM((2 * ROWS, TABLE_ROWS, width), jnp.bfloat16),
-            pltpu.SemaphoreType.DMA,
-            pltpu.SemaphoreType.DMA((2 * ROWS,)),
-        ],
-    )(held(verdict_ids.T), tp_index, parts, held(out_weight), held(vocab_table))
+    weight = call(
+        weight_kernel,
+        shape(out_weight.shape, out_weight.dtype),
+        [VM, HB],
+        "weight",
+        [pltpu.SemaphoreType.DMA],
+    )(parts, held(out_weight))
     parts = exchanged(parts, "seq_lo")
     pieces = call(
-        project_kernel, shape((tp, 3 * ROWS, width), jnp.bfloat16), [VM, VM, VM], "project"
+        project_kernel, shape((tp, 3 * ROWS, width), jnp.bfloat16), [VM, VM, PIPE], "project"
     )(parts, weight, table_rows)
     pieces = exchanged(pieces, TP)
     gained, sums = call(

time: 196 us -> 198 us (1.010)
  blocking collectives: 135 us -> 106 us
  starting transfers between devices: 11.7 us -> 30.6 us
  waiting for transfers between devices: 20.2 us -> 28.9 us
  Pallas kernels: 13 us -> 15.4 us
    all_to_all x2 -> x1, blocking collectives: 42.5 us -> 13.3 us  [exchanged(): return lax.all_to_all(copies, axis, 0, 0, tiled=True)]
    all_to_all x3 -> x4, starting transfers between devices: 11.6 us -> 30.6 us  [exchanged(): return lax.all_to_all(copies, axis, 0, 0, tiled=True)]
    all_to_all x3 -> x4, waiting for transfers between devices: 20.1 us -> 28.8 us  [exchanged(): return lax.all_to_all(copies, axis, 0, 0, tiled=True)]
    pallas_call x1 -> x2, Pallas kernels: 2.56 us -> 4.17 us  [the longest x1 2.46 us: shards(): call(table_kernel, shape((2 * ROWS, width), f32), [SM, SM, HB, HB], 'tabl...]
  transfers between devices with their start and end apart: 4 -> 5, of which waited for: 3 -> 4; matrix products, arithmetic and copies ran while one was open for 1% -> 1% of each run, Pallas kernels for 5% -> 7%
where the time goes in v8:
time: 198 us; the launch traced here: 197 us
  blocking collectives  106 us (54%)
  starting transfers between devices  30.6 us (15%)
  waiting for transfers between devices  28.9 us (15%)
  Pallas kernels  15.4 us (8%)
  between operations  14.2 us (7%)
    psum x1, blocking collectives, shards(): rows = lax.psum(rows.astype(jnp.bfloat16), 'seq_hi')  50.2 us
    all_to_all x4, starting transfers between devices, exchanged(): return lax.all_to_all(copies, axis, 0, 0, tiled=True)  30.6 us
    all_to_all x4, waiting for transfers between devices, exchanged(): return lax.all_to_all(copies, axis, 0, 0, tiled=True)  28.8 us
    psum x1, blocking collectives, shards(): sums = lax.psum(sums, 'seq_hi')  26.7 us
    psum x1, blocking collectives, shards(): slots = lax.psum(slots, 'seq_hi')  16.3 us
    all_to_all x1, blocking collectives, exchanged(): return lax.all_to_all(copies, axis, 0, 0, tiled=True)  13.3 us
    pallas_call x1, Pallas kernels, attention(): pl.pallas_call(attention_kernel, out_shape=jax.ShapeDtypeStruct(q.shape,...  4.08 us
  transfers between devices with their start and end apart: 5, of which 4 were waited for; matrix products, arithmetic and copies ran while one was open for 1% of the time, Pallas kernels for 7%

profile of v8, /device:TPU:40, one launch (start us, length us, event | category | flops | bytes accessed | tf_op | source)
XLA Modules:
  0.0 197.3 jit_solution(13727850186176024258)
XLA Ops:
  7.2 0.0 copy-start.1
  7.2 0.1 all-gather.2.cloned.1.call-start
  7.3 1.8 last_rows.1
  9.1 0.1 all-gather.2.cloned.1.call-update
  9.1 18.6 %all-to-all-start = ((bf16[8,8,512]{2,1,0:T(8,128)(2,1)}), bf16[8,8,512]{2,1,0:T(8,128)(2,1)S(1)}, u32[]{:S(2)}, u32[]{:S(2)}) async-start(bf16[8,8,512]{2,1,0:T(8,128)(2,1)} %get-tuple-element.10.after_ref), calls=%async_computation | async-start | bytes 131072 | tf_op jit(solution)/shard_map/all_to_all | solution.py:45
  27.7 2.5 %table.1.after_ref.table_ref = f32[24,256]{1,0:T(8,128)S(1)} custom-call(s32[2,12]{1,0:T(2,128)} %bitcast.4, s32[1]{0:T(128)} %bitcast.3.tp_ref, bf16[8,8,512]{2,1,0:T(8,128)(2,1)} %get-tuple-element.10.after_ref, bf16[8016,256]{1,0:T(8,128)(2,1)} %table_ref.1), custom_call_target="tpu_custom_call" | custom-call | tf_op jit(solution)/shard_map/table/pallas_call | solution.py:407
  30.1 0.0 copy-start
  30.2 0.6 copy-done
  30.7 7.8 %all-to-all-done = bf16[8,8,512]{2,1,0:T(8,128)(2,1)S(1)} async-done(((bf16[8,8,512]{2,1,0:T(8,128)(2,1)}), bf16[8,8,512]{2,1,0:T(8,128)(2,1)S(1)}, u32[]{:S(2)}, u32[]{:S(2)}) %all-to-all-start) | async-done | bytes 65568 | tf_op jit(solution)/shard_map/all_to_all | solution.py:45
  38.6 50.2 %psum.21.rows_ref = bf16[8,512]{1,0:T(8,128)(2,1)S(1)} all-reduce(bf16[8,512]{1,0:T(8,128)(2,1)S(1)} %reduce_sum.12), channel_id=1, replica_groups=mesh['groups'=2,'seq_hi'=4,'seq_lo'=8,'tp_0'=4,'tp_1'=2] {'seq_hi'}, use_global_device_ids=true, to_apply=%region_1.0 | all-reduce | flops 4096 | bytes 16384 | tf_op jit(solution)/shard_map/psum | solution.py:419
  88.8 1.4 partials.1
  90.2 13.3 %all_to_all.25.pieces_ref = f32[8,8,128]{2,1,0:T(8,128)S(1)} all-to-all(f32[8,8,128]{2,1,0:T(8,128)S(1)} %partials.1), channel_id=1, replica_groups=mesh['groups'=2,'seq_hi'=4,'seq_lo'=8,'tp_0'=4,'tp_1'=2] {'seq_lo'}, dimensions={0} | all-to-all | bytes 65536 | tf_op jit(solution)/shard_map/all_to_all | solution.py:45
  103.5 0.1 merge.1
  103.6 16.3 %psum.22.slots_ref = bf16[32,128]{1,0:T(8,128)(2,1)S(1)} all-reduce(bf16[32,128]{1,0:T(8,128)(2,1)S(1)} %merge.1), channel_id=1, replica_groups=mesh['groups'=2,'seq_hi'=4,'seq_lo'=8,'tp_0'=4,'tp_1'=2] {'seq_hi'}, use_global_device_ids=true, to_apply=%region_2.0 | all-reduce | flops 4096 | bytes 16384 | tf_op jit(solution)/shard_map/psum | solution.py:435
  119.9 0.7 finish.1.after_ref
  120.6 3.5 %all-to-all-start.2 = ((bf16[8,8,128]{2,1,0:T(8,128)(2,1)}), bf16[8,8,128]{2,1,0:T(8,128)(2,1)S(1)}, u32[]{:S(2)}, u32[]{:S(2)}) async-start(bf16[8,8,128]{2,1,0:T(8,128)(2,1)} %finish.1.after_ref), calls=%async_computation.2 | async-start | bytes 32768 | tf_op jit(solution)/shard_map/all_to_all | solution.py:45
  124.1 1.7 weight.1.w_ref
  125.9 8.8 %all-to-all-done.2.parts_ref = bf16[8,8,128]{2,1,0:T(8,128)(2,1)S(1)} async-done(((bf16[8,8,128]{2,1,0:T(8,128)(2,1)}), bf16[8,8,128]{2,1,0:T(8,128)(2,1)S(1)}, u32[]{:S(2)}, u32[]{:S(2)}) %all-to-all-start.2) | async-done | bytes 16416 | tf_op jit(solution)/shard_map/all_to_all | solution.py:45
  134.6 1.6 project.1
  136.2 4.9 %all-to-all-start.3 = ((bf16[8,36,256]{2,1,0:T(8,128)(2,1)}), bf16[8,36,256]{2,1,0:T(8,128)(2,1)S(1)}, u32[]{:S(2)}, u32[]{:S(2)}) async-start(bf16[8,36,256]{2,1,0:T(8,128)(2,1)} %project.1), calls=%async_computation.3 | async-start | bytes 327680 | tf_op jit(solution)/shard_map/all_to_all | solution.py:45
  141.1 0.0 copy-done.1
  141.1 0.6 reshape.22.gain_ref
  141.7 5.9 %all-to-all-done.3.pieces_ref = bf16[8,36,256]{2,1,0:T(8,128)(2,1)S(1)} async-done(((bf16[8,36,256]{2,1,0:T(8,128)(2,1)}), bf16[8,36,256]{2,1,0:T(8,128)(2,1)S(1)}, u32[]{:S(2)}, u32[]{:S(2)}) %all-to-all-start.3) | async-done | bytes 147488 | tf_op jit(solution)/shard_map/all_to_all | solution.py:45
  147.6 0.9 residual.1
  148.4 26.7 %psum.23.after_ref = f32[8,128]{1,0:T(8,128)S(1)} all-reduce(f32[8,128]{1,0:T(8,128)S(1)} %get-tuple-element.11), channel_id=1, replica_groups=mesh['groups'=2,'seq_hi'=4,'seq_lo'=8,'tp_0'=4,'tp_1'=2] {'seq_hi'}, use_global_device_ids=true, to_apply=%region_3.0 | all-reduce | flops 1024 | bytes 8192 | tf_op jit(solution)/shard_map/psum | solution.py:455
  175.1 0.6 broadcast_in_dim.2
  175.7 3.5 %all-to-all-start.4 = ((f32[8,8,128]{2,1,0:T(8,128)}), f32[8,8,128]{2,1,0:T(8,128)S(1)}, u32[]{:S(2)}, u32[]{:S(2)}) async-start(f32[8,8,128]{2,1,0:T(8,128)} %broadcast_in_dim.2), calls=%async_computation.4 | async-start | bytes 65536 | tf_op jit(solution)/shard_map/all_to_all | solution.py:45
  179.3 0.0 all-gather.2.cloned.1.call-done.kv_ref
  179.3 4.1 %attention.1.after_ref = bf16[256,512]{1,0:T(8,128)(2,1)} custom-call(s32[8]{0:T(128)} %lengths_ref.5, s32[1]{0:T(128)} %bitcast.seq_ref, bf16[256,512]{1,0:T(8,128)(2,1)} %q_hbm.1, bf16[8192,256]{1,0:T(8,128)(2,1)} %all-gather.2.cloned.1.call-done.kv_ref, f32[8,128]{1,0:T(8,128)S(1)} %psum.23.after_ref), custom_call_target="tpu_custom_call" | custom-call | tf_op jit(solution)/shard_map/attention/pallas_call | solution.py:339
  183.4 6.3 %all-to-all-done.4.sums_ref = f32[8,8,128]{2,1,0:T(8,128)S(1)} async-done(((f32[8,8,128]{2,1,0:T(8,128)}), f32[8,8,128]{2,1,0:T(8,128)S(1)}, u32[]{:S(2)}, u32[]{:S(2)}) %all-to-all-start.4) | async-done | bytes 32800 | tf_op jit(solution)/shard_map/all_to_all | solution.py:45
  189.7 0.8 verdict.1
  (1 shorter events, 0.0 us)
Async XLA Ops:
  7.2 133.9 %copy-start.1 = (bf16[256]{0:T(256)(128)(2,1)S(1)}, bf16[256]{0:T(256)(128)(2,1)}, u32[]{:S(2)}) copy-start(bf16[256]{0:T(256)(128)(2,1)} %param.23) | copy-start | bytes 1540
  7.2 172.1 %all-gather.2.cloned.1.call-start = ((), (), s32[]{:S(2)}) async-start(), calls=%async_computation.5 | async-start | bytes 4325376 | tf_op jit(solution)/shard_map/all_gather | solution.py:405
  9.1 29.5 %all-to-all-start = ((bf16[8,8,512]{2,1,0:T(8,128)(2,1)}), bf16[8,8,512]{2,1,0:T(8,128)(2,1)S(1)}, u32[]{:S(2)}, u32[]{:S(2)}) async-start(bf16[8,8,512]{2,1,0:T(8,128)(2,1)} %get-tuple-element.10.after_ref), calls=%async_computation | async-start | bytes 131072 | tf_op jit(solution)/shard_map/all_to_all | solution.py:45
  30.1 0.6 copy-start
  120.6 14.0 %all-to-all-start.2 = ((bf16[8,8,128]{2,1,0:T(8,128)(2,1)}), bf16[8,8,128]{2,1,0:T(8,128)(2,1)S(1)}, u32[]{:S(2)}, u32[]{:S(2)}) async-start(bf16[8,8,128]{2,1,0:T(8,128)(2,1)} %finish.1.after_ref), calls=%async_computation.2 | async-start | bytes 32768 | tf_op jit(solution)/shard_map/all_to_all | solution.py:45
  136.2 11.4 %all-to-all-start.3 = ((bf16[8,36,256]{2,1,0:T(8,128)(2,1)}), bf16[8,36,256]{2,1,0:T(8,128)(2,1)S(1)}, u32[]{:S(2)}, u32[]{:S(2)}) async-start(bf16[8,36,256]{2,1,0:T(8,128)(2,1)} %project.1), calls=%async_computation.3 | async-start | bytes 327680 | tf_op jit(solution)/shard_map/all_to_all | solution.py:45
  175.7 14.0 %all-to-all-start.4 = ((f32[8,8,128]{2,1,0:T(8,128)}), f32[8,8,128]{2,1,0:T(8,128)S(1)}, u32[]{:S(2)}, u32[]{:S(2)}) async-start(f32[8,8,128]{2,1,0:T(8,128)} %broadcast_in_dim.2), calls=%async_computation.4 | async-start | bytes 65536 | tf_op jit(solution)/shard_map/all_to_all | solution.py:45
Sparse Core Ops, SparseCore 0:
  10.1 166.5 all-gather.1

commit v9 on v7

--- a/solution.py
+++ b/solution.py
@@ -20,7 +20,7 @@
 SLOT = 16
 PART = 8
 HELD = 6
-KEY_BLOCK = 256
+KEY_BLOCK = 512
 TP = ("tp_0", "tp_1")
 SEQ = ("seq_hi", "seq_lo")
 

time: 196 us -> 196 us (level)
  transfers between devices with their start and end apart: 4 -> 4, of which waited for: 3 -> 3; matrix products, arithmetic and copies ran while one was open for 1% -> 1% of each run, Pallas kernels for 5% -> 6%
where the time goes in v9:
time: 196 us
  blocking collectives  135 us (69%)
  waiting for transfers between devices  19.7 us (10%)
  between operations  14.1 us (7%)
  Pallas kernels  13.4 us (7%)
  starting transfers between devices  11.7 us (6%)
    psum x1, blocking collectives, shards(): rows = lax.psum(rows.astype(jnp.bfloat16), 'seq_hi')  50.1 us
    all_to_all x2, blocking collectives, exchanged(): return lax.all_to_all(copies, axis, 0, 0, tiled=True)  42.5 us
    psum x1, blocking collectives, shards(): sums = lax.psum(sums, 'seq_hi')  26.5 us
    all_to_all x3, waiting for transfers between devices, exchanged(): return lax.all_to_all(copies, axis, 0, 0, tiled=True)  19.6 us
    psum x1, blocking collectives, shards(): slots = lax.psum(slots, 'seq_hi')  16.3 us
    all_to_all x3, starting transfers between devices, exchanged(): return lax.all_to_all(copies, axis, 0, 0, tiled=True)  11.6 us
    pallas_call x1, Pallas kernels, attention(): pl.pallas_call(attention_kernel, out_shape=jax.ShapeDtypeStruct(q.shape,...  4.5 us
  transfers between devices with their start and end apart: 4, of which 3 were waited for; matrix products, arithmetic and copies ran while one was open for 1% of the time, Pallas kernels for 6%

profile of v9, /device:TPU:40, one launch (start us, length us, event | category | flops | bytes accessed | tf_op | source)
XLA Modules:
  0.0 195.5 jit_solution(625198006916393051)
XLA Ops:
  7.2 0.0 copy-start
  7.2 0.1 all-gather.2.cloned.1.call-start
  7.3 1.7 last_rows.1
  8.9 0.1 all-gather.2.cloned.1.call-update
  9.0 29.3 %all_to_all.25 = bf16[8,8,512]{2,1,0:T(8,128)(2,1)S(1)} all-to-all(bf16[8,8,512]{2,1,0:T(8,128)(2,1)S(1)} %get-tuple-element.12), channel_id=1, replica_groups=mesh['groups'=2,'seq_hi'=4,'seq_lo'=8,'tp_0'=4,'tp_1'=2] {'seq_lo'}, dimensions={0} | all-to-all | bytes 131072 | tf_op jit(solution)/shard_map/all_to_all | solution.py:45
  38.3 50.1 %psum.21.rows_ref = bf16[8,512]{1,0:T(8,128)(2,1)S(1)} all-reduce(bf16[8,512]{1,0:T(8,128)(2,1)S(1)} %reduce_sum.12), channel_id=1, replica_groups=mesh['groups'=2,'seq_hi'=4,'seq_lo'=8,'tp_0'=4,'tp_1'=2] {'seq_hi'}, use_global_device_ids=true, to_apply=%region_1.0 | all-reduce | flops 4096 | bytes 16384 | tf_op jit(solution)/shard_map/psum | solution.py:406
  88.4 1.4 partials.1
  89.7 13.2 %all_to_all.26.pieces_ref = f32[8,8,128]{2,1,0:T(8,128)S(1)} all-to-all(f32[8,8,128]{2,1,0:T(8,128)S(1)} %partials.1), channel_id=1, replica_groups=mesh['groups'=2,'seq_hi'=4,'seq_lo'=8,'tp_0'=4,'tp_1'=2] {'seq_lo'}, dimensions={0} | all-to-all | bytes 65536 | tf_op jit(solution)/shard_map/all_to_all | solution.py:45
  103.0 0.1 merge.1
  103.1 16.3 %psum.22.slots_ref = bf16[32,128]{1,0:T(8,128)(2,1)S(1)} all-reduce(bf16[32,128]{1,0:T(8,128)(2,1)S(1)} %merge.1), channel_id=1, replica_groups=mesh['groups'=2,'seq_hi'=4,'seq_lo'=8,'tp_0'=4,'tp_1'=2] {'seq_hi'}, use_global_device_ids=true, to_apply=%region_2.0 | all-reduce | flops 4096 | bytes 16384 | tf_op jit(solution)/shard_map/psum | solution.py:423
  119.4 0.7 finish.1.after_ref
  120.1 3.5 %all-to-all-start.2 = ((bf16[8,8,128]{2,1,0:T(8,128)(2,1)}), bf16[8,8,128]{2,1,0:T(8,128)(2,1)S(1)}, u32[]{:S(2)}, u32[]{:S(2)}) async-start(bf16[8,8,128]{2,1,0:T(8,128)(2,1)} %finish.1.after_ref), calls=%async_computation.2 | async-start | bytes 32768 | tf_op jit(solution)/shard_map/all_to_all | solution.py:45
  123.7 2.6 %prepare.1 = (f32[24,256]{1,0:T(8,128)S(1)}, bf16[512,256]{1,0:T(8,128)(2,1)S(1)}) custom-call(s32[2,12]{1,0:T(2,128)} %bitcast.4, s32[1]{0:T(128)} %bitcast.3.tp_ref, bf16[8,8,128]{2,1,0:T(8,128)(2,1)} %finish.1.after_ref, bf16[512,256]{1,0:T(8,128)(2,1)} %w_hbm.1, bf16[8016,256]{1,0:T(8,128)(2,1)} %table_ref.1), custom_call_target="tpu_custom_call" | custom-call | tf_op jit(solution)/shard_map/prepare/pallas_call | solution.py:425
  126.3 7.8 %all-to-all-done.2.parts_ref = bf16[8,8,128]{2,1,0:T(8,128)(2,1)S(1)} async-done(((bf16[8,8,128]{2,1,0:T(8,128)(2,1)}), bf16[8,8,128]{2,1,0:T(8,128)(2,1)S(1)}, u32[]{:S(2)}, u32[]{:S(2)}) %all-to-all-start.2) | async-done | bytes 16416 | tf_op jit(solution)/shard_map/all_to_all | solution.py:45
  134.1 0.8 project.1
  134.9 4.5 %all-to-all-start.3 = ((bf16[8,36,256]{2,1,0:T(8,128)(2,1)}), bf16[8,36,256]{2,1,0:T(8,128)(2,1)S(1)}, u32[]{:S(2)}, u32[]{:S(2)}) async-start(bf16[8,36,256]{2,1,0:T(8,128)(2,1)} %project.1), calls=%async_computation.3 | async-start | bytes 327680 | tf_op jit(solution)/shard_map/all_to_all | solution.py:45
  139.5 0.0 copy-done
  139.5 0.6 reshape.22.gain_ref
  140.1 5.9 %all-to-all-done.3.pieces_ref = bf16[8,36,256]{2,1,0:T(8,128)(2,1)S(1)} async-done(((bf16[8,36,256]{2,1,0:T(8,128)(2,1)}), bf16[8,36,256]{2,1,0:T(8,128)(2,1)S(1)}, u32[]{:S(2)}, u32[]{:S(2)}) %all-to-all-start.3) | async-done | bytes 147488 | tf_op jit(solution)/shard_map/all_to_all | solution.py:45
  145.9 0.9 residual.1
  146.8 26.5 %psum.23.after_ref = f32[8,128]{1,0:T(8,128)S(1)} all-reduce(f32[8,128]{1,0:T(8,128)S(1)} %get-tuple-element.15), channel_id=1, replica_groups=mesh['groups'=2,'seq_hi'=4,'seq_lo'=8,'tp_0'=4,'tp_1'=2] {'seq_hi'}, use_global_device_ids=true, to_apply=%region_3.0 | all-reduce | flops 1024 | bytes 8192 | tf_op jit(solution)/shard_map/psum | solution.py:447
  173.3 0.6 broadcast_in_dim.2
  173.9 3.5 %all-to-all-start.4 = ((f32[8,8,128]{2,1,0:T(8,128)}), f32[8,8,128]{2,1,0:T(8,128)S(1)}, u32[]{:S(2)}, u32[]{:S(2)}) async-start(f32[8,8,128]{2,1,0:T(8,128)} %broadcast_in_dim.2), calls=%async_computation.4 | async-start | bytes 65536 | tf_op jit(solution)/shard_map/all_to_all | solution.py:45
  177.4 0.0 all-gather.2.cloned.1.call-done.kv_ref
  177.5 4.5 %attention.1.after_ref = bf16[256,512]{1,0:T(8,128)(2,1)} custom-call(s32[8]{0:T(128)} %lengths_ref.5, s32[1]{0:T(128)} %bitcast.seq_ref, bf16[256,512]{1,0:T(8,128)(2,1)} %q_hbm.1, bf16[8192,256]{1,0:T(8,128)(2,1)} %all-gather.2.cloned.1.call-done.kv_ref, f32[8,128]{1,0:T(8,128)S(1)} %psum.23.after_ref), custom_call_target="tpu_custom_call" | custom-call | tf_op jit(solution)/shard_map/attention/pallas_call | solution.py:338
  182.0 5.9 %all-to-all-done.4.sums_ref = f32[8,8,128]{2,1,0:T(8,128)S(1)} async-done(((f32[8,8,128]{2,1,0:T(8,128)}), f32[8,8,128]{2,1,0:T(8,128)S(1)}, u32[]{:S(2)}, u32[]{:S(2)}) %all-to-all-start.4) | async-done | bytes 32800 | tf_op jit(solution)/shard_map/all_to_all | solution.py:45
  187.9 0.8 verdict.1
  (1 shorter events, 0.0 us)
Async XLA Ops:
  7.2 132.3 %copy-start = (bf16[256]{0:T(256)(128)(2,1)S(1)}, bf16[256]{0:T(256)(128)(2,1)}, u32[]{:S(2)}) copy-start(bf16[256]{0:T(256)(128)(2,1)} %param.23) | copy-start | bytes 1540
  7.2 170.3 %all-gather.2.cloned.1.call-start = ((), (), s32[]{:S(2)}) async-start(), calls=%async_computation.5 | async-start | bytes 4325376 | tf_op jit(solution)/shard_map/all_gather | solution.py:404
  120.1 14.0 %all-to-all-start.2 = ((bf16[8,8,128]{2,1,0:T(8,128)(2,1)}), bf16[8,8,128]{2,1,0:T(8,128)(2,1)S(1)}, u32[]{:S(2)}, u32[]{:S(2)}) async-start(bf16[8,8,128]{2,1,0:T(8,128)(2,1)} %finish.1.after_ref), calls=%async_computation.2 | async-start | bytes 32768 | tf_op jit(solution)/shard_map/all_to_all | solution.py:45
  134.9 11.0 %all-to-all-start.3 = ((bf16[8,36,256]{2,1,0:T(8,128)(2,1)}), bf16[8,36,256]{2,1,0:T(8,128)(2,1)S(1)}, u32[]{:S(2)}, u32[]{:S(2)}) async-start(bf16[8,36,256]{2,1,0:T(8,128)(2,1)} %project.1), calls=%async_computation.3 | async-start | bytes 327680 | tf_op jit(solution)/shard_map/all_to_all | solution.py:45
  173.9 14.0 %all-to-all-start.4 = ((f32[8,8,128]{2,1,0:T(8,128)}), f32[8,8,128]{2,1,0:T(8,128)S(1)}, u32[]{:S(2)}, u32[]{:S(2)}) async-start(f32[8,8,128]{2,1,0:T(8,128)} %broadcast_in_dim.2), calls=%async_computation.4 | async-start | bytes 65536 | tf_op jit(solution)/shard_map/all_to_all | solution.py:45
Sparse Core Ops, SparseCore 0:
  10.1 166.5 all-gather.1
